TPU v7x, 256 devices: a whole 4x4x8 slice. The times are simulated.
256 devices in a mesh: lat: 8 (over z), lon: 16 (over x, y), obs: 2 (over core).
Axes of the slice: x: 4, y: 4, z: 8, core: 2. Of those that a mesh axis runs over, the one named last changes fastest.
Arguments:
- innovation: float32 [32768, 128], P(('lat', 'lon', 'obs')), may hold values from -6 to 6
- obs_error: float32 [32768, 128], P(('lat', 'lon', 'obs')), may hold values from 0.5 to 2
- obs_offset: float32 [2, 32768, 128], P(None, ('lat', 'lon', 'obs')), may hold values from 0 to 1
- obs_cell: int32 [32768, 128], P(('lat', 'lon', 'obs')), may hold values from 0 to 65535
- obs_owner: int32 [256, 128], P(('lat', 'lon', 'obs')), may hold values from 0 to 127, as said below
- block_count: int32 [256], P(('lat', 'lon', 'obs')), may hold values from 64 to 128
- land_mask: int32 [512, 16384], P(('lat', 'obs'), 'lon'), may hold values from 0 to 1, as said below
- inertia: float32 [512, 16384], P(('lat', 'obs'), 'lon'), may hold values from 0.002 to 0.05
- sea_depth: float32 [512, 16384], P(('lat', 'obs'), 'lon'), may hold values from 0.5 to 5
Outputs:
- adjoint_field: float32 [512, 16384], P(('lat', 'obs'), 'lon')
- residual: float32 [512, 16384], P(('lat', 'obs'), 'lon')
Inputs may be any that keep to these rules, and one draw needn't show every extreme that they name: `obs_owner`: among the live blocks of one device at most 3 name the same tile; in every draw some tile is named by exactly 3 live blocks of every device. `land_mask`: the first and the last grid row are land.
All inputs are finite; a program needn't handle non-finite values.
Results may differ from a plain program's by a relative error of at most 0.0003.
Values sent between devices are 32-bit elements; how exact they have to be, the bound alone decides.
No kernel may reach another device: no remote copies, remote signals or barrier semaphores. Data moves between devices by JAX's collectives and lax.ppermute only.
A program may use at most 64 MiB of HBM per device.

v0:
```python
import jax
import jax.numpy as jnp
from jax import lax
from jax.sharding import Mesh
from jax.sharding import PartitionSpec as P

ITERS = 5
LON = ("lon_0", "lon_1")
LAT_LON_OBS = ("lat", "lon_0", "lon_1", "obs")
LAT_LON = ("lat", "lon_0", "lon_1")


def extended(block, sides, width):
    for axis, dim in sides:
        count = lax.axis_size(axis)
        forward = [(i, i + 1) for i in range(count - 1)]
        forward.append((count - 1, 0))
        backward = [(target, source) for source, target in forward]
        low = lax.ppermute(
            lax.slice_in_dim(block, block.shape[dim] - width, None, axis=dim), axis, forward
        )
        high = lax.ppermute(lax.slice_in_dim(block, 0, width, axis=dim), axis, backward)
        block = jnp.concatenate([low, block, high], axis=dim)
    return block


def by_axis(value, axes):
    for axis in axes:
        value = lax.psum(value, axis)
    return value


def cut_along(value, dim, peers):
    shape = value.shape
    tiles = value.reshape(*shape[:dim], peers, shape[dim] // peers, *shape[dim + 1 :])
    return jnp.moveaxis(tiles, dim, 0)


def in_order(tiles, dim):
    tiles = jnp.moveaxis(tiles, 0, dim)
    shape = tiles.shape
    return tiles.reshape(*shape[:dim], shape[dim] * shape[dim + 1], *shape[dim + 2 :])


def exchange_both(value, axis, axes, splits, concats):
    sizes = [lax.axis_size(a) for a in axes]
    tiles = cut_along(value, splits[0], sizes[0])
    tiles = jnp.moveaxis(cut_along(tiles, splits[1] + 1, sizes[1]), 0, 1)
    inside = tiles.shape[2:]
    tiles = tiles.reshape(-1, *inside)
    tiles = lax.all_to_all(tiles, axis, split_axis=0, concat_axis=0, tiled=True)
    tiles = in_order(tiles.reshape(*sizes, *inside), concats[0] + 1)
    return in_order(tiles, concats[1])


def shifted(value, axis, steps):
    count = lax.axis_size(axis)
    pairs = [(source, (source + steps) % count) for source in range(count)]
    return lax.ppermute(value, axis, pairs)


def shifted_2(block, axis, distance):
    devices = range(lax.axis_size(axis))
    route = [(i - distance, i) for i in devices if i - distance in devices]
    return lax.ppermute(block, axis, route)


def sent_and_summed(value, axis, dim):
    tiles = cut_along(value, dim, lax.axis_size(axis))
    arrived = lax.all_to_all(tiles, axis, split_axis=0, concat_axis=0, tiled=True)
    return arrived.sum(axis=0)


def border(field):
    return extended(field, ((("lat", "obs"), 0), (LON, 1)), 1)


def two_products(residual, applied):
    return (
        by_axis(jnp.sum(residual * residual), LAT_LON_OBS),
        by_axis(jnp.sum(residual * applied), LAT_LON_OBS),
    )


def body(
    innovation,
    obs_error,
    obs_offset,
    obs_cell,
    obs_owner,
    block_count,
    land_mask,
    inertia,
    sea_depth,
):
    block_total = obs_owner.shape[1]
    block_width = innovation.shape[1]
    n_lat = lax.axis_size("lat")
    n_lon = lax.axis_size(LON)
    tile_count = n_lat * n_lon
    capacity = max(3, 2 * ((block_total + tile_count - 1) // tile_count))
    slot_total = tile_count * capacity
    tile_rows = land_mask.shape[0] * lax.axis_size("obs")
    tile_cols = land_mask.shape[1]
    owners = obs_owner[0]
    block_ids = jnp.arange(block_total)
    is_live = block_ids < block_count[0]
    earlier = block_ids[None, :] < block_ids[:, None]
    same_owner = (owners[None, :] == owners[:, None]) & earlier & is_live[None, :]
    slot_rank = jnp.sum(same_owner.astype(jnp.int32), axis=1)
    target = jnp.where(is_live, owners * capacity + slot_rank, slot_total)
    scaled = innovation / (obs_error * obs_error)
    floats = jnp.stack([scaled, obs_offset[0], obs_offset[1]], axis=1)

    def put_slots(values):
        holder = jnp.zeros((slot_total + 1,) + values.shape[1:], values.dtype)
        return holder.at[target].set(values)[:slot_total]

    sent_floats = put_slots(floats)
    sent_cells = put_slots(obs_cell)
    received, cell_ids = (
        exchange_both(
            sent_floats.reshape(n_lat, n_lon, capacity, 3, block_width),
            LAT_LON,
            ("lat", LON),
            (0, 1),
            (0, 1),
        ),
        exchange_both(
            sent_cells.reshape(n_lat, n_lon, capacity, block_width),
            LAT_LON,
            ("lat", LON),
            (0, 1),
            (0, 1),
        ),
    )
    received = received.reshape(-1, 3, block_width)
    cell_ids = cell_ids.reshape(-1, block_width)
    group = 1
    for size_try in range(1, slot_total + 1):
        if slot_total % size_try == 0 and size_try * block_width <= 4096:
            group = size_try
    turns = slot_total // group
    group_obs = group * block_width
    scaled_in = received[:, 0].reshape(turns, group_obs)
    north_frac = received[:, 1].reshape(turns, group_obs)
    east_frac = received[:, 2].reshape(turns, group_obs)
    cells_in = cell_ids.reshape(turns, group_obs)
    wide = tile_cols + 1
    row_axis = jnp.arange(tile_rows + 1, dtype=jnp.int32)[:, None]
    col_axis = jnp.arange(wide, dtype=jnp.int32)[None, :]

    def spread(total, pieces):
        amount, north, east, cells = pieces
        cell_row = (cells // tile_cols)[None, :]
        cell_col = (cells % tile_cols)[:, None]
        row_weights = (
            jnp.where(row_axis == cell_row, 1.0 - north[None, :], 0.0)
            + jnp.where(row_axis == cell_row + 1, north[None, :], 0.0)
        ) * amount[None, :]
        col_weights = jnp.where(col_axis == cell_col, 1.0 - east[:, None], 0.0) + jnp.where(
            col_axis == cell_col + 1, east[:, None], 0.0
        )
        return (
            total
            + jnp.dot(
                row_weights,
                col_weights,
                precision=lax.Precision.HIGHEST,
                preferred_element_type=jnp.float32,
            ),
            None,
        )

    partial_value, unused = lax.scan(
        spread,
        jnp.zeros((tile_rows + 1, wide), jnp.float32),
        (scaled_in, north_frac, east_frac, cells_in),
    )
    arrived_col = shifted(partial_value[:, tile_cols], LON, 1)
    partial_value = partial_value[:, :tile_cols].at[:, 0].add(arrived_col)
    arrived_row = shifted_2(partial_value[tile_rows], "lat", 1)
    tile_part = partial_value[:tile_rows].at[0].add(arrived_row)
    ocean = land_mask.astype(jnp.float32)
    forcing = sent_and_summed(tile_part, "obs", 0) * ocean
    conduct = ocean * sea_depth
    padded = border(conduct)
    cond_north = jnp.sqrt(conduct * padded[:-2, 1:-1])
    cond_south = jnp.sqrt(conduct * padded[2:, 1:-1])
    cond_west = jnp.sqrt(conduct * padded[1:-1, :-2])
    cond_east = jnp.sqrt(conduct * padded[1:-1, 2:])
    diagonal = inertia + cond_north + cond_south + cond_west + cond_east

    def operate(field):
        outer = border(field)
        return (
            diagonal * field
            - cond_north * outer[:-2, 1:-1]
            - cond_south * outer[2:, 1:-1]
            - cond_west * outer[1:-1, :-2]
            - cond_east * outer[1:-1, 2:]
        )

    adjoint_field = jnp.zeros_like(forcing)
    residual = forcing
    applied = operate(residual)
    norm_now, product = two_products(residual, applied)
    step_size = norm_now / product
    direction = residual
    applied_dir = applied
    for iteration in range(ITERS):
        adjoint_field = adjoint_field + step_size * direction
        residual = residual - step_size * applied_dir
        if iteration + 1 < ITERS:
            applied = operate(residual)
            norm_next, product = two_products(residual, applied)
            beta_ratio = norm_next / norm_now
            step_size = norm_next / (product - beta_ratio * norm_next / step_size)
            direction = residual + beta_ratio * direction
            applied_dir = applied + beta_ratio * applied_dir
            norm_now = norm_next
    return (adjoint_field, residual)


def solution(mesh):
    split = Mesh(
        mesh.devices.reshape(mesh.shape["lat"], 4, 4, mesh.shape["obs"]),
        ("lat", "lon_0", "lon_1", "obs"),
    )
    return jax.shard_map(
        body,
        mesh=split,
        in_specs=(
            P(LAT_LON_OBS, None),
            P(LAT_LON_OBS, None),
            P(None, LAT_LON_OBS, None),
            P(LAT_LON_OBS, None),
            P(LAT_LON_OBS, None),
            P(LAT_LON_OBS),
            P(("lat", "obs"), LON),
            P(("lat", "obs"), LON),
            P(("lat", "obs"), LON),
        ),
        out_specs=(P(("lat", "obs"), LON), P(("lat", "obs"), LON)),
        check_vma=False,
    )
```

profile of v0, /device:TPU:1, one launch (start us, length us, event | category | flops | bytes accessed | tf_op | source)
XLA Modules:
  0.0 612.3 jit_solution(17351134791260999394)
XLA Ops:
  2.9 1.2 scatter_custom_fusion
  4.8 16.3 %all-to-all-start = ((s32[128,1,1,3,128]{4,2,3,1,0:T(1,128)}), s32[128,1,1,3,128]{4,2,3,1,0:T(1,128)S(1)}, u32[]{:S(2)}, u32[]{:S(2)}) async-start(s32[128,1,1,3,128]{4,2,3,1,0:T(1,128)} %bitcast.5), calls=%async_computation | async-start | bytes 393216 | tf_op jit(solution)/shard_map/all_to_all | solution.py:51
  21.5 4.4 scatter_fusion
  26.1 1.4 copy.29
  27.5 5.7 all-to-all-done
  33.1 7.6 %all-to-all-start.1 = ((f32[128,1,1,3,3,128]{5,2,4,3,1,0:T(1,128)}), f32[128,1,1,3,3,128]{5,2,4,3,1,0:T(1,128)S(1)}, u32[]{:S(2)}, u32[]{:S(2)}) async-start(f32[128,1,1,3,3,128]{5,2,4,3,1,0:T(1,128)} %copy.29), calls=%async_computation.1 | async-start | bytes 1179648 | tf_op jit(solution)/shard_map/all_to_all | solution.py:51
  40.9 19.1 %all-to-all-done.1 = f32[128,1,1,3,3,128]{5,2,4,3,1,0:T(1,128)S(1)} async-done(((f32[128,1,1,3,3,128]{5,2,4,3,1,0:T(1,128)}), f32[128,1,1,3,3,128]{5,2,4,3,1,0:T(1,128)S(1)}, u32[]{:S(2)}, u32[]{:S(2)}) %all-to-all-start.1) | async-done | bytes 589856 | tf_op jit(solution)/shard_map/all_to_all | solution.py:51
  60.7 239.6 %while.16 = (s32[]{:T(128)}, f32[65,1025]{1,0:T(8,128)S(1)}, s32[12,4096]{1,0:T(8,128)S(1)}, f32[12,4096]{1,0:T(8,128)S(1)}, f32[12,4096]{1,0:T(8,128)S(1)}, /*index=5*/f32[12,4096]{1,0:T(8,128)S(1)}, s32[]{:T(128)}, s32[]{:T(128)}) while((s32[]{:T(128)}, f32[65,1025]{1,0:T(8,128)S(1)}, s32[12,4096]{1,0:T(8,128)S(1)}, ...), condition=%wide.region_4.5_spmd.clone.clone, body=%wide.region_3.4_spmd.clone.clone.sunk | while | flops 3297597440 | bytes 942707 | solution.py:175
  72.5 18.7 %fusion.98 = f32[65,1025]{1,0:T(8,128)S(1)} fusion(f32[4096]{0:T(1024)S(1)} %bitcast.80, s32[4096]{0:T(1024)S(1)} %get-tuple-element.342, f32[4096]{0:T(1024)S(1)} %broadcast_subtract_fusion.5, s32[4096]{0:T(1024)S(1)} %get-tuple-element.343, f32[4096]{0:T(1024)S(1)} %bitcast.87, f32[4096]{0:T(1024)S(1)} %bitcast.86, s32[4096]{0:T(1024)S(1)} %bitcast.88, ...), kind=kOutput, calls=%fused_computation.15.clone.1 | convolution fusion | flops 3297474560 | bytes 680457 | tf_op jit(solution)/shard_map/while/body/eval_jaxpr/dot_general | solution.py:166
  91.5 18.7 %fusion.98 = f32[65,1025]{1,0:T(8,128)S(1)} fusion(f32[4096]{0:T(1024)S(1)} %bitcast.80, s32[4096]{0:T(1024)S(1)} %get-tuple-element.342, f32[4096]{0:T(1024)S(1)} %broadcast_subtract_fusion.5, s32[4096]{0:T(1024)S(1)} %get-tuple-element.343, f32[4096]{0:T(1024)S(1)} %bitcast.87, f32[4096]{0:T(1024)S(1)} %bitcast.86, s32[4096]{0:T(1024)S(1)} %bitcast.88, ...), kind=kOutput, calls=%fused_computation.15.clone.1 | convolution fusion | flops 3297474560 | bytes 680457 | tf_op jit(solution)/shard_map/while/body/eval_jaxpr/dot_general | solution.py:166
  110.5 18.7 %fusion.98 = f32[65,1025]{1,0:T(8,128)S(1)} fusion(f32[4096]{0:T(1024)S(1)} %bitcast.80, s32[4096]{0:T(1024)S(1)} %get-tuple-element.342, f32[4096]{0:T(1024)S(1)} %broadcast_subtract_fusion.5, s32[4096]{0:T(1024)S(1)} %get-tuple-element.343, f32[4096]{0:T(1024)S(1)} %bitcast.87, f32[4096]{0:T(1024)S(1)} %bitcast.86, s32[4096]{0:T(1024)S(1)} %bitcast.88, ...), kind=kOutput, calls=%fused_computation.15.clone.1 | convolution fusion | flops 3297474560 | bytes 680457 | tf_op jit(solution)/shard_map/while/body/eval_jaxpr/dot_general | solution.py:166
  129.5 18.7 %fusion.98 = f32[65,1025]{1,0:T(8,128)S(1)} fusion(f32[4096]{0:T(1024)S(1)} %bitcast.80, s32[4096]{0:T(1024)S(1)} %get-tuple-element.342, f32[4096]{0:T(1024)S(1)} %broadcast_subtract_fusion.5, s32[4096]{0:T(1024)S(1)} %get-tuple-element.343, f32[4096]{0:T(1024)S(1)} %bitcast.87, f32[4096]{0:T(1024)S(1)} %bitcast.86, s32[4096]{0:T(1024)S(1)} %bitcast.88, ...), kind=kOutput, calls=%fused_computation.15.clone.1 | convolution fusion | flops 3297474560 | bytes 680457 | tf_op jit(solution)/shard_map/while/body/eval_jaxpr/dot_general | solution.py:166
  148.5 18.7 %fusion.98 = f32[65,1025]{1,0:T(8,128)S(1)} fusion(f32[4096]{0:T(1024)S(1)} %bitcast.80, s32[4096]{0:T(1024)S(1)} %get-tuple-element.342, f32[4096]{0:T(1024)S(1)} %broadcast_subtract_fusion.5, s32[4096]{0:T(1024)S(1)} %get-tuple-element.343, f32[4096]{0:T(1024)S(1)} %bitcast.87, f32[4096]{0:T(1024)S(1)} %bitcast.86, s32[4096]{0:T(1024)S(1)} %bitcast.88, ...), kind=kOutput, calls=%fused_computation.15.clone.1 | convolution fusion | flops 3297474560 | bytes 680457 | tf_op jit(solution)/shard_map/while/body/eval_jaxpr/dot_general | solution.py:166
  167.5 18.7 %fusion.98 = f32[65,1025]{1,0:T(8,128)S(1)} fusion(f32[4096]{0:T(1024)S(1)} %bitcast.80, s32[4096]{0:T(1024)S(1)} %get-tuple-element.342, f32[4096]{0:T(1024)S(1)} %broadcast_subtract_fusion.5, s32[4096]{0:T(1024)S(1)} %get-tuple-element.343, f32[4096]{0:T(1024)S(1)} %bitcast.87, f32[4096]{0:T(1024)S(1)} %bitcast.86, s32[4096]{0:T(1024)S(1)} %bitcast.88, ...), kind=kOutput, calls=%fused_computation.15.clone.1 | convolution fusion | flops 3297474560 | bytes 680457 | tf_op jit(solution)/shard_map/while/body/eval_jaxpr/dot_general | solution.py:166
  186.5 18.7 %fusion.98 = f32[65,1025]{1,0:T(8,128)S(1)} fusion(f32[4096]{0:T(1024)S(1)} %bitcast.80, s32[4096]{0:T(1024)S(1)} %get-tuple-element.342, f32[4096]{0:T(1024)S(1)} %broadcast_subtract_fusion.5, s32[4096]{0:T(1024)S(1)} %get-tuple-element.343, f32[4096]{0:T(1024)S(1)} %bitcast.87, f32[4096]{0:T(1024)S(1)} %bitcast.86, s32[4096]{0:T(1024)S(1)} %bitcast.88, ...), kind=kOutput, calls=%fused_computation.15.clone.1 | convolution fusion | flops 3297474560 | bytes 680457 | tf_op jit(solution)/shard_map/while/body/eval_jaxpr/dot_general | solution.py:166
  205.5 18.7 %fusion.98 = f32[65,1025]{1,0:T(8,128)S(1)} fusion(f32[4096]{0:T(1024)S(1)} %bitcast.80, s32[4096]{0:T(1024)S(1)} %get-tuple-element.342, f32[4096]{0:T(1024)S(1)} %broadcast_subtract_fusion.5, s32[4096]{0:T(1024)S(1)} %get-tuple-element.343, f32[4096]{0:T(1024)S(1)} %bitcast.87, f32[4096]{0:T(1024)S(1)} %bitcast.86, s32[4096]{0:T(1024)S(1)} %bitcast.88, ...), kind=kOutput, calls=%fused_computation.15.clone.1 | convolution fusion | flops 3297474560 | bytes 680457 | tf_op jit(solution)/shard_map/while/body/eval_jaxpr/dot_general | solution.py:166
  224.4 18.7 %fusion.98 = f32[65,1025]{1,0:T(8,128)S(1)} fusion(f32[4096]{0:T(1024)S(1)} %bitcast.80, s32[4096]{0:T(1024)S(1)} %get-tuple-element.342, f32[4096]{0:T(1024)S(1)} %broadcast_subtract_fusion.5, s32[4096]{0:T(1024)S(1)} %get-tuple-element.343, f32[4096]{0:T(1024)S(1)} %bitcast.87, f32[4096]{0:T(1024)S(1)} %bitcast.86, s32[4096]{0:T(1024)S(1)} %bitcast.88, ...), kind=kOutput, calls=%fused_computation.15.clone.1 | convolution fusion | flops 3297474560 | bytes 680457 | tf_op jit(solution)/shard_map/while/body/eval_jaxpr/dot_general | solution.py:166
  243.4 18.7 %fusion.98 = f32[65,1025]{1,0:T(8,128)S(1)} fusion(f32[4096]{0:T(1024)S(1)} %bitcast.80, s32[4096]{0:T(1024)S(1)} %get-tuple-element.342, f32[4096]{0:T(1024)S(1)} %broadcast_subtract_fusion.5, s32[4096]{0:T(1024)S(1)} %get-tuple-element.343, f32[4096]{0:T(1024)S(1)} %bitcast.87, f32[4096]{0:T(1024)S(1)} %bitcast.86, s32[4096]{0:T(1024)S(1)} %bitcast.88, ...), kind=kOutput, calls=%fused_computation.15.clone.1 | convolution fusion | flops 3297474560 | bytes 680457 | tf_op jit(solution)/shard_map/while/body/eval_jaxpr/dot_general | solution.py:166
  262.4 18.7 %fusion.98 = f32[65,1025]{1,0:T(8,128)S(1)} fusion(f32[4096]{0:T(1024)S(1)} %bitcast.80, s32[4096]{0:T(1024)S(1)} %get-tuple-element.342, f32[4096]{0:T(1024)S(1)} %broadcast_subtract_fusion.5, s32[4096]{0:T(1024)S(1)} %get-tuple-element.343, f32[4096]{0:T(1024)S(1)} %bitcast.87, f32[4096]{0:T(1024)S(1)} %bitcast.86, s32[4096]{0:T(1024)S(1)} %bitcast.88, ...), kind=kOutput, calls=%fused_computation.15.clone.1 | convolution fusion | flops 3297474560 | bytes 680457 | tf_op jit(solution)/shard_map/while/body/eval_jaxpr/dot_general | solution.py:166
  281.4 18.7 %fusion.98 = f32[65,1025]{1,0:T(8,128)S(1)} fusion(f32[4096]{0:T(1024)S(1)} %bitcast.80, s32[4096]{0:T(1024)S(1)} %get-tuple-element.342, f32[4096]{0:T(1024)S(1)} %broadcast_subtract_fusion.5, s32[4096]{0:T(1024)S(1)} %get-tuple-element.343, f32[4096]{0:T(1024)S(1)} %bitcast.87, f32[4096]{0:T(1024)S(1)} %bitcast.86, s32[4096]{0:T(1024)S(1)} %bitcast.88, ...), kind=kOutput, calls=%fused_computation.15.clone.1 | convolution fusion | flops 3297474560 | bytes 680457 | tf_op jit(solution)/shard_map/while/body/eval_jaxpr/dot_general | solution.py:166
  301.7 4.5 collective-permute-done
  307.2 2.7 collective-permute-start.1
  310.7 9.0 %all_to_all.15 = f32[2,32,1024]{2,1,0:T(8,128)S(1)} all-to-all(f32[2,32,1024]{2,1,0:T(8,128)S(1)} %bitcast.83), channel_id=1, replica_groups=mesh['lat'=8,'lon_0'=4,'lon_1'=4,'obs'=2] {'obs'}, dimensions={0} | all-to-all | bytes 524288 | tf_op jit(solution)/shard_map/all_to_all | solution.py:70
  319.9 2.3 collective-permute-start.2
  322.1 1.7 collective-permute-start.6
  323.9 1.3 collective-permute-done.3
  325.3 4.8 collective-permute-start.5
  330.2 4.8 collective-permute-start.9
  337.0 13.2 %all-reduce.4 = (f32[]{:T(128)}, f32[]{:T(128)}) all-reduce(f32[]{:T(128)} %get-tuple-element.194, f32[]{:T(128)} %get-tuple-element.193), channel_id=1, replica_groups=mesh['lat'=8,'lon_0'=4,'lon_1'=4,'obs'=2] {'lat'}, use_global_device_ids=true, to_apply=%region_8.9 | all-reduce | flops 2 | bytes 16 | tf_op jit(solution)/shard_map/psum | solution.py:29
  350.2 6.6 %all-reduce.14 = (f32[]{:T(128)}, f32[]{:T(128)}) all-reduce(f32[]{:T(128)} %get-tuple-element.215, f32[]{:T(128)} %get-tuple-element.216), channel_id=1, replica_groups=mesh['lat'=8,'lon_0'=4,'lon_1'=4,'obs'=2] {'lon_0'}, use_global_device_ids=true, to_apply=%region_9.10 | all-reduce | flops 2 | bytes 16 | tf_op jit(solution)/shard_map/psum | solution.py:29
  356.8 11.7 %all-reduce.9 = (f32[]{:T(128)}, f32[]{:T(128)}) all-reduce(f32[]{:T(128)} %get-tuple-element.235, f32[]{:T(128)} %get-tuple-element.236), channel_id=1, replica_groups=mesh['lat'=8,'lon_0'=4,'lon_1'=4,'obs'=2] {'lon_1'}, use_global_device_ids=true, to_apply=%region_10.11 | all-reduce | flops 2 | bytes 16 | tf_op jit(solution)/shard_map/psum | solution.py:29
  368.5 11.4 %all-reduce.19 = (f32[]{:T(128)}, f32[]{:T(128)}) all-reduce(f32[]{:T(128)} %get-tuple-element.225, f32[]{:T(128)} %get-tuple-element.226), channel_id=1, replica_groups=mesh['lat'=8,'lon_0'=4,'lon_1'=4,'obs'=2] {'obs'}, use_global_device_ids=true, to_apply=%region_11.12 | all-reduce | flops 2 | bytes 16 | tf_op jit(solution)/shard_map/psum | solution.py:29
  381.2 2.0 collective-permute-start.10
  384.0 2.3 collective-permute-done.11
  386.4 4.8 collective-permute-start.13
  391.1 1.6 collective-permute-done.12
  393.7 13.4 %all-reduce.3 = (f32[]{:T(128)}, f32[]{:T(128)}) all-reduce(f32[]{:T(128)} %get-tuple-element.192, f32[]{:T(128)} %get-tuple-element.191), channel_id=1, replica_groups=mesh['lat'=8,'lon_0'=4,'lon_1'=4,'obs'=2] {'lat'}, use_global_device_ids=true, to_apply=%region_18.19 | all-reduce | flops 2 | bytes 16 | tf_op jit(solution)/shard_map/psum | solution.py:29
  407.1 6.7 %all-reduce.13 = (f32[]{:T(128)}, f32[]{:T(128)}) all-reduce(f32[]{:T(128)} %get-tuple-element.213, f32[]{:T(128)} %get-tuple-element.214), channel_id=1, replica_groups=mesh['lat'=8,'lon_0'=4,'lon_1'=4,'obs'=2] {'lon_0'}, use_global_device_ids=true, to_apply=%region_19.20 | all-reduce | flops 2 | bytes 16 | tf_op jit(solution)/shard_map/psum | solution.py:29
  413.7 11.9 %all-reduce.8 = (f32[]{:T(128)}, f32[]{:T(128)}) all-reduce(f32[]{:T(128)} %get-tuple-element.233, f32[]{:T(128)} %get-tuple-element.234), channel_id=1, replica_groups=mesh['lat'=8,'lon_0'=4,'lon_1'=4,'obs'=2] {'lon_1'}, use_global_device_ids=true, to_apply=%region_20.21 | all-reduce | flops 2 | bytes 16 | tf_op jit(solution)/shard_map/psum | solution.py:29
  425.6 9.6 %all-reduce.18 = (f32[]{:T(128)}, f32[]{:T(128)}) all-reduce(f32[]{:T(128)} %get-tuple-element.223, f32[]{:T(128)} %get-tuple-element.224), channel_id=1, replica_groups=mesh['lat'=8,'lon_0'=4,'lon_1'=4,'obs'=2] {'obs'}, use_global_device_ids=true, to_apply=%region_21.22 | all-reduce | flops 2 | bytes 16 | tf_op jit(solution)/shard_map/psum | solution.py:29
  439.9 1.2 collective-permute-start.14
  441.8 2.3 collective-permute-done.15
  444.2 4.8 collective-permute-start.17
  449.0 1.2 collective-permute-done.16
  451.1 14.4 %all-reduce.2 = (f32[]{:T(128)}, f32[]{:T(128)}) all-reduce(f32[]{:T(128)} %get-tuple-element.190, f32[]{:T(128)} %get-tuple-element.189), channel_id=1, replica_groups=mesh['lat'=8,'lon_0'=4,'lon_1'=4,'obs'=2] {'lat'}, use_global_device_ids=true, to_apply=%region_28.29 | all-reduce | flops 2 | bytes 16 | tf_op jit(solution)/shard_map/psum | solution.py:29
  465.4 6.6 %all-reduce.12 = (f32[]{:T(128)}, f32[]{:T(128)}) all-reduce(f32[]{:T(128)} %get-tuple-element.211, f32[]{:T(128)} %get-tuple-element.212), channel_id=1, replica_groups=mesh['lat'=8,'lon_0'=4,'lon_1'=4,'obs'=2] {'lon_0'}, use_global_device_ids=true, to_apply=%region_29.30 | all-reduce | flops 2 | bytes 16 | tf_op jit(solution)/shard_map/psum | solution.py:29
  472.0 11.9 %all-reduce.7 = (f32[]{:T(128)}, f32[]{:T(128)}) all-reduce(f32[]{:T(128)} %get-tuple-element.231, f32[]{:T(128)} %get-tuple-element.232), channel_id=1, replica_groups=mesh['lat'=8,'lon_0'=4,'lon_1'=4,'obs'=2] {'lon_1'}, use_global_device_ids=true, to_apply=%region_30.31 | all-reduce | flops 2 | bytes 16 | tf_op jit(solution)/shard_map/psum | solution.py:29
  484.0 8.8 %all-reduce.17 = (f32[]{:T(128)}, f32[]{:T(128)}) all-reduce(f32[]{:T(128)} %get-tuple-element.221, f32[]{:T(128)} %get-tuple-element.222), channel_id=1, replica_groups=mesh['lat'=8,'lon_0'=4,'lon_1'=4,'obs'=2] {'obs'}, use_global_device_ids=true, to_apply=%region_31.32 | all-reduce | flops 2 | bytes 16 | tf_op jit(solution)/shard_map/psum | solution.py:29
  496.7 2.0 collective-permute-start.18
  499.5 2.3 collective-permute-done.19
  501.9 4.8 collective-permute-start.21
  506.6 1.6 collective-permute-done.20
  509.1 13.4 %all-reduce.1 = (f32[]{:T(128)}, f32[]{:T(128)}) all-reduce(f32[]{:T(128)} %get-tuple-element.188, f32[]{:T(128)} %get-tuple-element.187), channel_id=1, replica_groups=mesh['lat'=8,'lon_0'=4,'lon_1'=4,'obs'=2] {'lat'}, use_global_device_ids=true, to_apply=%region_38.39 | all-reduce | flops 2 | bytes 16 | tf_op jit(solution)/shard_map/psum | solution.py:29
  522.5 6.6 %all-reduce.11 = (f32[]{:T(128)}, f32[]{:T(128)}) all-reduce(f32[]{:T(128)} %get-tuple-element.209, f32[]{:T(128)} %get-tuple-element.210), channel_id=1, replica_groups=mesh['lat'=8,'lon_0'=4,'lon_1'=4,'obs'=2] {'lon_0'}, use_global_device_ids=true, to_apply=%region_39.40 | all-reduce | flops 2 | bytes 16 | tf_op jit(solution)/shard_map/psum | solution.py:29
  529.1 11.9 %all-reduce.6 = (f32[]{:T(128)}, f32[]{:T(128)}) all-reduce(f32[]{:T(128)} %get-tuple-element.229, f32[]{:T(128)} %get-tuple-element.230), channel_id=1, replica_groups=mesh['lat'=8,'lon_0'=4,'lon_1'=4,'obs'=2] {'lon_1'}, use_global_device_ids=true, to_apply=%region_40.41 | all-reduce | flops 2 | bytes 16 | tf_op jit(solution)/shard_map/psum | solution.py:29
  541.0 9.5 %all-reduce.16 = (f32[]{:T(128)}, f32[]{:T(128)}) all-reduce(f32[]{:T(128)} %get-tuple-element.219, f32[]{:T(128)} %get-tuple-element.220), channel_id=1, replica_groups=mesh['lat'=8,'lon_0'=4,'lon_1'=4,'obs'=2] {'obs'}, use_global_device_ids=true, to_apply=%region_41.42 | all-reduce | flops 2 | bytes 16 | tf_op jit(solution)/shard_map/psum | solution.py:29
  554.3 1.2 collective-permute-start.22
  556.3 2.3 collective-permute-done.23
  558.6 4.8 collective-permute-start.25
  563.4 1.2 collective-permute-done.24
  565.5 14.4 %all-reduce = (f32[]{:T(128)}, f32[]{:T(128)}) all-reduce(f32[]{:T(128)} %get-tuple-element.186, f32[]{:T(128)} %get-tuple-element.185), channel_id=1, replica_groups=mesh['lat'=8,'lon_0'=4,'lon_1'=4,'obs'=2] {'lat'}, use_global_device_ids=true, to_apply=%region_48.49 | all-reduce | flops 2 | bytes 16 | tf_op jit(solution)/shard_map/psum | solution.py:29
  579.9 6.6 %all-reduce.10 = (f32[]{:T(128)}, f32[]{:T(128)}) all-reduce(f32[]{:T(128)} %get-tuple-element.207, f32[]{:T(128)} %get-tuple-element.208), channel_id=1, replica_groups=mesh['lat'=8,'lon_0'=4,'lon_1'=4,'obs'=2] {'lon_0'}, use_global_device_ids=true, to_apply=%region_49.50 | all-reduce | flops 2 | bytes 16 | tf_op jit(solution)/shard_map/psum | solution.py:29
  586.5 11.9 %all-reduce.5 = (f32[]{:T(128)}, f32[]{:T(128)}) all-reduce(f32[]{:T(128)} %get-tuple-element.227, f32[]{:T(128)} %get-tuple-element.228), channel_id=1, replica_groups=mesh['lat'=8,'lon_0'=4,'lon_1'=4,'obs'=2] {'lon_1'}, use_global_device_ids=true, to_apply=%region_50.51 | all-reduce | flops 2 | bytes 16 | tf_op jit(solution)/shard_map/psum | solution.py:29
  598.4 8.8 %all-reduce.15 = (f32[]{:T(128)}, f32[]{:T(128)}) all-reduce(f32[]{:T(128)} %get-tuple-element.217, f32[]{:T(128)} %get-tuple-element.218), channel_id=1, replica_groups=mesh['lat'=8,'lon_0'=4,'lon_1'=4,'obs'=2] {'obs'}, use_global_device_ids=true, to_apply=%region_51.52 | all-reduce | flops 2 | bytes 16 | tf_op jit(solution)/shard_map/psum | solution.py:29
  (155 shorter events, 19.2 us)
Async XLA Ops:
  0.6 20.5 %copy-start.3 = (f32[2,128,128]{2,1,0:T(8,128)S(1)}, f32[2,128,128]{2,1,0:T(8,128)}, u32[]{:S(2)}) copy-start(f32[2,128,128]{2,1,0:T(8,128)} %param.17) | copy-start | bytes 393220
  0.6 20.6 %copy-start.4 = (f32[128,128]{1,0:T(8,128)S(1)}, f32[128,128]{1,0:T(8,128)}, u32[]{:S(2)}) copy-start(f32[128,128]{1,0:T(8,128)} %param.15) | copy-start | bytes 196612
  0.7 20.6 %copy-start.5 = (f32[128,128]{1,0:T(8,128)S(1)}, f32[128,128]{1,0:T(8,128)}, u32[]{:S(2)}) copy-start(f32[128,128]{1,0:T(8,128)} %param.16) | copy-start | bytes 196612
  4.8 28.3 %all-to-all-start = ((s32[128,1,1,3,128]{4,2,3,1,0:T(1,128)}), s32[128,1,1,3,128]{4,2,3,1,0:T(1,128)S(1)}, u32[]{:S(2)}, u32[]{:S(2)}) async-start(s32[128,1,1,3,128]{4,2,3,1,0:T(1,128)} %bitcast.5), calls=%async_computation | async-start | bytes 393216 | tf_op jit(solution)/shard_map/all_to_all | solution.py:51
  33.1 26.9 %all-to-all-start.1 = ((f32[128,1,1,3,3,128]{5,2,4,3,1,0:T(1,128)}), f32[128,1,1,3,3,128]{5,2,4,3,1,0:T(1,128)S(1)}, u32[]{:S(2)}, u32[]{:S(2)}) async-start(f32[128,1,1,3,3,128]{5,2,4,3,1,0:T(1,128)} %copy.29), calls=%async_computation.1 | async-start | bytes 1179648 | tf_op jit(solution)/shard_map/all_to_all | solution.py:51
  300.4 5.8 collective-permute-start
  306.9 12.9 %copy-start.1 = (f32[32,1024]{1,0:T(8,128)S(1)}, f32[32,1024]{1,0:T(8,128)}, u32[]{:S(2)}) copy-start(f32[32,1024]{1,0:T(8,128)} %param.23) | copy-start | bytes 393220
  306.9 12.9 %copy-start.2 = (s32[32,1024]{1,0:T(8,128)S(1)}, s32[32,1024]{1,0:T(8,128)}, u32[]{:S(2)}) copy-start(s32[32,1024]{1,0:T(8,128)} %param.21) | copy-start | bytes 393220
  307.2 3.4 collective-permute-start.1
  319.8 16.3 %copy-start = (f32[32,1024]{1,0:T(8,128)S(1)}, f32[32,1024]{1,0:T(8,128)}, u32[]{:S(2)}) copy-start(f32[32,1024]{1,0:T(8,128)} %param.22) | copy-start | bytes 393220
  319.9 4.0 collective-permute-start.2
  322.1 3.0 collective-permute-start.3
  322.1 7.9 %collective-permute-start.6 = (f32[1,1024]{1,0:T(1,128)S(1)}, f32[1,1024]{1,0:T(1,128)S(1)}, u32[]{:S(2)}, u32[]{:S(2)}) collective-permute-start(f32[1,1024]{1,0:T(1,128)S(1)} %get-tuple-element.291), channel_id=1, source_target_pairs={{0,1},{1,32},{32,33},{33,64},{64,65},{65,96},{96,97},{97,128},{128... | collective-permute-start | bytes 12296 | tf_op jit(solution)/shard_map/ppermute | solution.py:19
  323.9 6.2 %collective-permute-start.7 = (f32[1,1024]{1,0:T(1,128)S(1)}, f32[1,1024]{1,0:T(1,128)S(1)}, u32[]{:S(2)}, u32[]{:S(2)}) collective-permute-start(f32[1,1024]{1,0:T(1,128)S(1)} %get-tuple-element.292), channel_id=1, source_target_pairs={{1,0},{32,1},{33,32},{64,33},{65,64},{96,65},{97,96},{128,97},{129... | collective-permute-start | bytes 12296 | tf_op jit(solution)/shard_map/ppermute | solution.py:22
  325.2 9.7 %collective-permute-start.4 = (f32[34,1]{1,0:T(8,128)S(1)}, f32[34,1]{1,0:T(8,128)S(1)}, u32[]{:S(2)}, u32[]{:S(2)}) collective-permute-start(f32[34,1]{1,0:T(8,128)S(1)} %get-tuple-element.273), channel_id=1, source_target_pairs={{0,2},{2,4},{4,6},{6,8},{8,10},{10,12},{12,14},{14,16},{16,18},{18... | collective-permute-start | bytes 416 | tf_op jit(solution)/shard_map/ppermute | solution.py:19
  325.3 9.7 %collective-permute-start.5 = (f32[34,1]{1,0:T(8,128)S(1)}, f32[34,1]{1,0:T(8,128)S(1)}, u32[]{:S(2)}, u32[]{:S(2)}) collective-permute-start(f32[34,1]{1,0:T(8,128)S(1)} %get-tuple-element.274), channel_id=1, source_target_pairs={{2,0},{4,2},{6,4},{8,6},{10,8},{12,10},{14,12},{16,14},{18,16},{20... | collective-permute-start | bytes 416 | tf_op jit(solution)/shard_map/ppermute | solution.py:22
  330.1 6.0 collective-permute-start.8
  330.2 5.9 collective-permute-start.9
  381.2 2.7 collective-permute-start.10
  383.2 3.0 collective-permute-start.11
  386.3 6.4 %collective-permute-start.12 = (f32[34,1]{1,0:T(8,128)S(1)}, f32[34,1]{1,0:T(8,128)S(1)}, u32[]{:S(2)}, u32[]{:S(2)}) collective-permute-start(f32[34,1]{1,0:T(8,128)S(1)} %get-tuple-element.271), channel_id=1, source_target_pairs={{0,2},{2,4},{4,6},{6,8},{8,10},{10,12},{12,14},{14,16},{16,18},{18... | collective-permute-start | bytes 416 | tf_op jit(solution)/shard_map/ppermute | solution.py:19
  386.4 6.4 %collective-permute-start.13 = (f32[34,1]{1,0:T(8,128)S(1)}, f32[34,1]{1,0:T(8,128)S(1)}, u32[]{:S(2)}, u32[]{:S(2)}) collective-permute-start(f32[34,1]{1,0:T(8,128)S(1)} %get-tuple-element.272), channel_id=1, source_target_pairs={{2,0},{4,2},{6,4},{8,6},{10,8},{12,10},{14,12},{16,14},{18,16},{20... | collective-permute-start | bytes 416 | tf_op jit(solution)/shard_map/ppermute | solution.py:22
  439.9 1.9 collective-permute-start.14
  441.0 3.0 collective-permute-start.15
  444.2 6.0 collective-permute-start.16
  444.2 5.9 collective-permute-start.17
  496.7 2.7 collective-permute-start.18
  498.7 3.0 collective-permute-start.19
  501.8 6.4 %collective-permute-start.20 = (f32[34,1]{1,0:T(8,128)S(1)}, f32[34,1]{1,0:T(8,128)S(1)}, u32[]{:S(2)}, u32[]{:S(2)}) collective-permute-start(f32[34,1]{1,0:T(8,128)S(1)} %get-tuple-element.267), channel_id=1, source_target_pairs={{0,2},{2,4},{4,6},{6,8},{8,10},{10,12},{12,14},{14,16},{16,18},{18... | collective-permute-start | bytes 416 | tf_op jit(solution)/shard_map/ppermute | solution.py:19
  501.9 6.3 %collective-permute-start.21 = (f32[34,1]{1,0:T(8,128)S(1)}, f32[34,1]{1,0:T(8,128)S(1)}, u32[]{:S(2)}, u32[]{:S(2)}) collective-permute-start(f32[34,1]{1,0:T(8,128)S(1)} %get-tuple-element.268), channel_id=1, source_target_pairs={{2,0},{4,2},{6,4},{8,6},{10,8},{12,10},{14,12},{16,14},{18,16},{20... | collective-permute-start | bytes 416 | tf_op jit(solution)/shard_map/ppermute | solution.py:22
  554.3 1.9 collective-permute-start.22
  555.5 3.0 collective-permute-start.23
  558.6 6.0 collective-permute-start.24
  558.6 5.9 collective-permute-start.25
where the time goes:
time: 617 us; the launch traced here: 612 us
  matrix products  225 us (36%)
  blocking collectives  218 us (35%)
  starting transfers between devices  66.1 us (11%)
  waiting for transfers between devices  50.1 us (8%)
  between operations  19.6 us (3%)
  loops' own time  12.5 us (2%)
  other arithmetic  10.9 us (2%)
  local copies, waits for them, and re-layouts  9.92 us (2%)
    dot_general x12, matrix products, spread(): jnp.dot(row_weights, col_weights, precision=lax.Precision.HIGHEST, prefer...  225 us
    psum x20, blocking collectives, by_axis(): value = lax.psum(value, axis)  209 us
    ppermute x12, starting transfers between devices, extended(): lax.ppermute(lax.slice_in_dim(block, 0, width, axis=dim), axis, backward)  28.7 us
    all_to_all x2, waiting for transfers between devices, exchange_both(): tiles = lax.all_to_all(tiles, axis, split_axis=0, concat_axis=0, tiled=True)  24.8 us
    all_to_all x2, starting transfers between devices, exchange_both(): tiles = lax.all_to_all(tiles, axis, split_axis=0, concat_axis=0, tiled=True)  23.9 us
    another operation x1, loops' own time, body(): lax.scan(spread, jnp.zeros((tile_rows + 1, wide), jnp.float32), (scaled_i...  12.5 us
  transfers between devices with their start and end apart: 28, of which 18 were waited for; matrix products, arithmetic and copies ran while one was open for 1% of the time, Pallas kernels for 0%

commit v1 on v0

v1 whole, which is shorter than its diff:
```python
import jax
import jax.numpy as jnp
from jax import lax
from jax.experimental import pallas as pl
from jax.experimental.pallas import tpu as pltpu
from jax.sharding import Mesh
from jax.sharding import PartitionSpec as P

ITERS = 5
MOMENTS = 2 * ITERS
CAP = 3
WORDS = 4
LON = ("lon_0", "lon_1")
LAT_OBS = ("lat", "obs")
LAT_LON_OBS = ("lat", "lon_0", "lon_1", "obs")
LAT_LON = ("lat", "lon_0", "lon_1")
F32 = jnp.float32
BF16 = jnp.bfloat16
GROUPS = 2
CHUNK = 8


def vmem():
    return pl.BlockSpec(memory_space=pltpu.VMEM)


def smem():
    return pl.BlockSpec(memory_space=pltpu.SMEM)


def pack_kernel(owner, count, innovation, error, offset, cell, out, rows, seen):
    blocks = innovation.shape[0]
    tiles = out.shape[0] // (CAP * WORDS)
    err = error[...]
    rows[pl.ds(0, blocks, stride=WORDS), :] = innovation[...] / (err * err)
    rows[pl.ds(1, blocks, stride=WORDS), :] = offset[0]
    rows[pl.ds(2, blocks, stride=WORDS), :] = offset[1]
    rows[pl.ds(3, blocks, stride=WORDS), :] = cell[...].astype(F32)
    out[...] = jnp.zeros(out.shape, F32)

    def clear(tile, carry):
        seen[tile] = 0
        return carry

    lax.fori_loop(0, tiles, clear, 0)

    def place(block, carry):
        tile = owner[0, block]
        rank = seen[tile]
        seen[tile] = rank + 1
        slot = tile * CAP + rank
        out[pl.ds(slot * WORDS, WORDS), :] = rows[pl.ds(block * WORDS, WORDS), :]
        return carry

    lax.fori_loop(0, count[0], place, 0)


def pack(owner, count, innovation, error, offset, cell, tiles):
    blocks = innovation.shape[0]
    return pl.pallas_call(
        pack_kernel,
        out_shape=jax.ShapeDtypeStruct((tiles * CAP * WORDS, 128), F32),
        in_specs=[smem(), smem(), vmem(), vmem(), vmem(), vmem()],
        out_specs=vmem(),
        scratch_shapes=[pltpu.VMEM((blocks * WORDS, 128), F32), pltpu.SMEM((tiles,), jnp.int32)],
        name="pack",
    )(owner, count, innovation, error, offset, cell)


def deposit(arrived, tile_rows, tile_cols):
    slots = arrived.shape[0] // WORDS
    row_pad = (tile_rows + 1 + 7) // 8 * 8
    m_one = (GROUPS * row_pad + 15) // 16 * 16
    width = tile_cols // GROUPS
    m_all = 4 * m_one
    steps = slots // CHUNK
    half_m = m_one // 2
    half_n = width // 2

    def kernel(src, out, left_a, left_b, right_a, right_b, acc):
        m_index = (lax.broadcasted_iota(jnp.int32, (m_one, 128), 0) - half_m).astype(F32).astype(BF16)
        n_index = (lax.broadcasted_iota(jnp.int32, (width, 128), 0) - half_n).astype(F32).astype(BF16)
        n_one = jnp.ones((width, 128), BF16)
        n_zero = jnp.zeros((width, 128), BF16)
        m_zero = jnp.zeros((m_one, 128), BF16)

        def spread(x, j, n):
            row = jnp.broadcast_to(x[j : j + 1, :], (16, 128)).astype(BF16)
            return jnp.broadcast_to(row[None], (n // 16, 16, 128)).reshape(n, 128)

        def build(chunk, left, right):
            base = chunk * (CHUNK * WORDS)
            amount = src[pl.ds(base, CHUNK, stride=WORDS), :]
            north = src[pl.ds(base + 1, CHUNK, stride=WORDS), :]
            east = src[pl.ds(base + 2, CHUNK, stride=WORDS), :]
            cell = src[pl.ds(base + 3, CHUNK, stride=WORDS), :].astype(jnp.int32)
            row = cell // tile_cols
            col = cell % tile_cols
            m_here = ((col // width) * row_pad + row - half_m).astype(F32)
            m_next = m_here + 1.0
            n_here = (col % width - half_n).astype(F32)
            pieces = []
            for value in (amount, amount * east):
                low = value * (1.0 - north)
                high = value * north
                low_top = low.astype(BF16).astype(F32)
                high_top = high.astype(BF16).astype(F32)
                pieces.append((low_top, high_top))
                pieces.append((low - low_top, high - high_top))
            for j in range(CHUNK):
                at_row = m_index == spread(m_here, j, m_one)
                at_next = m_index == spread(m_next, j, m_one)
                for k, (low, high) in enumerate(pieces):
                    left[k * m_one : (k + 1) * m_one, j * 128 : (j + 1) * 128] = jnp.where(
                        at_row,
                        spread(low, j, m_one),
                        jnp.where(at_next, spread(high, j, m_one), m_zero),
                    )
                right[:, j * 128 : (j + 1) * 128] = jnp.where(
                    n_index == spread(n_here, j, width), n_one, n_zero
                )

        def add(left, right):
            acc[...] += lax.dot_general(
                left[...], right[...], (((1,), (1,)), ((), ())), preferred_element_type=F32
            )

        acc[...] = jnp.zeros((m_all, width), F32)
        build(0, left_a, right_a)

        def turn(i, carry):
            build(2 * i + 1, left_b, right_b)
            add(left_a, right_a)
            build(jnp.minimum(2 * i + 2, steps - 1), left_a, right_a)
            add(left_b, right_b)
            return carry

        lax.fori_loop(0, steps // 2, turn, 0)
        lane = lax.broadcasted_iota(jnp.int32, (row_pad, width), 1)
        before = jnp.zeros((row_pad, 1), F32)
        for g in range(GROUPS):
            s = g * row_pad
            whole = acc[s : s + row_pad] + acc[m_one + s : m_one + s + row_pad]
            part = acc[2 * m_one + s : 2 * m_one + s + row_pad] + acc[3 * m_one + s : 3 * m_one + s + row_pad]
            moved = pltpu.roll(part, 1, 1)
            moved = jnp.where(lane == 0, jnp.broadcast_to(before, (row_pad, width)), moved)
            out[:, g * width : (g + 1) * width] = whole - part + moved
            before = part[:, width - 1 : width]
        edge = lax.broadcasted_iota(jnp.int32, (row_pad, 128), 1)
        out[:, tile_cols : tile_cols + 128] = jnp.where(
            edge == 0, jnp.broadcast_to(before, (row_pad, 128)), 0.0
        )

    return pl.pallas_call(
        kernel,
        out_shape=jax.ShapeDtypeStruct((row_pad, tile_cols + 128), F32),
        in_specs=[vmem()],
        out_specs=vmem(),
        scratch_shapes=[
            pltpu.VMEM((m_all, CHUNK * 128), BF16),
            pltpu.VMEM((m_all, CHUNK * 128), BF16),
            pltpu.VMEM((width, CHUNK * 128), BF16),
            pltpu.VMEM((width, CHUNK * 128), BF16),
            pltpu.VMEM((m_all, width), F32),
        ],
        name="deposit",
    )(arrived)


def two_sum(a, b):
    s = a + b
    t = s - a
    return s, (a - (s - t)) + (b - t)


def quick_sum(a, b):
    s = a + b
    return s, b - (s - a)


def halves(a):
    t = a * 4097.0
    top = t - (t - a)
    return top, a - top


def two_prod(a, b, a_halves, b_halves):
    p = a * b
    a1, a2 = a_halves
    b1, b2 = b_halves
    return p, ((a1 * b1 - p) + a1 * b2 + a2 * b1) + a2 * b2


def pair_add(a, b):
    s, e = two_sum(a[0], b[0])
    return quick_sum(s, e + (a[1] + b[1]))


def pair_mul(a, b):
    p, e = two_prod(a[0], b[0], halves(a[0]), halves(b[0]))
    return quick_sum(p, e + (a[0] * b[1] + a[1] * b[0]))


def pair_neg(a):
    return -a[0], -a[1]


def pair_div(a, b):
    q1 = a[0] / b[0]
    zero = jnp.zeros_like(q1)
    rest = pair_add(a, pair_neg(pair_mul((q1, zero), b)))
    q2 = rest[0] / b[0]
    rest = pair_add(rest, pair_neg(pair_mul((q2, zero), b)))
    q3 = rest[0] / b[0]
    s, e = quick_sum(q1, q2)
    return quick_sum(s, e + q3)


def roll_to(x, step, axis):
    return pltpu.roll(x, step % x.shape[axis], axis)


def apply_pair(v, inertia, east, south):
    h, l = v
    h_cut = halves(h)
    total, e = two_prod(inertia[0], h, inertia[1], h_cut)
    rest = e + inertia[0] * l
    for axis, (face, face_cut) in ((1, east), (0, south)):
        other = roll_to(h, -1, axis)
        d = h - other
        t = d - h
        err = (h - (d - t)) - (other + t)
        low = (l - roll_to(l, -1, axis)) + err
        p, e = two_prod(face, d, face_cut, halves(d))
        low = e + face * low
        total, e = two_sum(total, p)
        rest = rest + (e + low)
        total, e = two_sum(total, -roll_to(p, 1, axis))
        rest = rest + (e - roll_to(low, 1, axis))
    return quick_sum(total, rest)


def apply_plain(v, inertia, east, south):
    total = inertia * v
    for axis, face in ((1, east), (0, south)):
        flow = face * (v - roll_to(v, -1, axis))
        total = total + (flow - roll_to(flow, 1, axis))
    return total


def pair_fold(a):
    while a[0].shape[0] > 8:
        n = a[0].shape[0] // 2
        a = pair_add((a[0][:n], a[1][:n]), (a[0][n:], a[1][n:]))
    while a[0].shape[1] > 128:
        n = a[0].shape[1] // 2
        a = pair_add((a[0][:, :n], a[1][:, :n]), (a[0][:, n:], a[1][:, n:]))
    for step in (4, 2, 1):
        a = pair_add(a, (pltpu.roll(a[0], step, 0), pltpu.roll(a[1], step, 0)))
    return a


def basis_kernel(side, tile, other, ocean, inertia, east, south, forcing, sums):
    rows, cols = inertia.shape[0] - 16, inertia.shape[1] - 128
    first = side[0] == 0
    middle = tile[pl.ds(pl.multiple_of(side[0] * rows, 8), rows), :]
    corner = jnp.where(first, other[8:16, :], 0.0)
    top = jnp.where(first, other[0:8, :], tile[rows - 8 : rows, :])
    bottom = jnp.where(
        first, tile[rows : rows + 8, :], other[0:8, :] + tile[2 * rows : 2 * rows + 8, :]
    )
    start = jnp.concatenate([top, middle[0:8] + corner, middle[8:], bottom], axis=0) * ocean[...]
    forcing[...] = start
    weights = [(w[...], halves(w[...])) for w in (inertia, east, south)]
    vectors = [(start, jnp.zeros_like(start))]
    for k in range(ITERS):
        vectors.append(apply_pair(vectors[-1], *weights))
    inner = [(h[8 : 8 + rows, :cols], l[8 : 8 + rows, :cols]) for h, l in vectors]
    cuts = [halves(h) for h, l in inner]
    lane = lax.broadcasted_iota(jnp.int32, (8, 128), 1)
    tops, lows = [], []
    for k in range(MOMENTS):
        i, j = k // 2, (k + 1) // 2
        a, b = inner[i], inner[j]
        p, e = two_prod(a[0], b[0], cuts[i], cuts[j])
        total = pair_fold((p, e + (a[0] * b[1] + a[1] * b[0])))
        tops.append(total[0][0:1])
        lows.append(total[1][0:1])
    blank = [jnp.zeros((16 - MOMENTS, 128), F32)]
    pair = (jnp.concatenate(tops + blank, 0), jnp.concatenate(lows + blank, 0))
    for step in (64, 32, 16, 8, 4, 2, 1):
        pair = pair_add(pair, (pltpu.roll(pair[0], step, 1), pltpu.roll(pair[1], step, 1)))
    lane = lax.broadcasted_iota(jnp.int32, (16, 128), 1)
    slot = lax.broadcasted_iota(jnp.int32, (16, 128), 0)
    row = jnp.sum(
        jnp.where(lane == slot, pair[0], jnp.where(lane == slot + 64, pair[1], 0.0)),
        axis=0,
        keepdims=True,
    )
    sums[...] = jnp.broadcast_to(row, sums.shape)


def basis(side, tile, other, ocean, inertia, east, south, devices):
    return pl.pallas_call(
        basis_kernel,
        out_shape=(
            jax.ShapeDtypeStruct(inertia.shape, F32),
            jax.ShapeDtypeStruct((devices, 128), F32),
        ),
        in_specs=[smem()] + [vmem()] * 6,
        out_specs=(vmem(), vmem()),
        name="basis",
    )(side, tile, other, ocean, inertia, east, south)


def solve_kernel(sums, forcing, inertia, east, south, field, residual):
    rows, cols = field.shape
    s = sums[...]
    pair = (s, jnp.zeros_like(s))
    while pair[0].shape[0] > 8:
        n = pair[0].shape[0] // 2
        pair = pair_add((pair[0][:n], pair[1][:n]), (pair[0][n:], pair[1][n:]))
    for step in (4, 2, 1):
        pair = pair_add(pair, (pltpu.roll(pair[0], step, 0), pltpu.roll(pair[1], step, 0)))
    pair = quick_sum(pair[0], pair[1] + pltpu.roll(pair[0], 64, 1))

    def entry(k):
        return tuple(jnp.broadcast_to(x[0:1, k : k + 1], (8, 128)) for x in pair)

    right = [entry(k) for k in range(MOMENTS)]
    ahead = list(right)
    steps, ratios = [], []
    for k in range(ITERS):
        step = pair_div(right[k], ahead[k + 1])
        steps.append(step[0])
        if k + 1 < ITERS:
            last = MOMENTS - 1 - k
            new = list(right)
            for m in range(k + 1, last):
                new[m] = pair_add(right[m], pair_neg(pair_mul(step, ahead[m + 1])))
            ratio = pair_neg(pair_mul(step, pair_div(new[k + 1], right[k])))
            for m in range(k + 1, last):
                ahead[m] = pair_add(new[m], pair_mul(ratio, ahead[m]))
            right = new
            ratios.append(ratio[0])
    weights = (inertia[...], east[...], south[...])
    left = forcing[...]
    heading = left
    total = None
    for k in range(ITERS):
        step = steps[k][0:1, 0:1]
        total = step * heading if total is None else total + step * heading
        left = left - step * apply_plain(heading, *weights)
        if k + 1 < ITERS:
            heading = left + ratios[k][0:1, 0:1] * heading
    field[...] = total[8 : 8 + rows, :cols]
    residual[...] = left[8 : 8 + rows, :cols]


def solve(sums, forcing, inertia, east, south, rows, cols):
    shape = jax.ShapeDtypeStruct((rows, cols), F32)
    return pl.pallas_call(
        solve_kernel,
        out_shape=(shape, shape),
        in_specs=[vmem()] * 5,
        out_specs=(vmem(), vmem()),
        name="solve",
    )(sums, forcing, inertia, east, south)


def around(value, axis, steps):
    count = lax.axis_size(axis)
    return lax.ppermute(value, axis, [(i, (i + steps) % count) for i in range(count)])


def body(
    innovation,
    obs_error,
    obs_offset,
    obs_cell,
    obs_owner,
    block_count,
    land_mask,
    inertia,
    sea_depth,
):
    n_lat = lax.axis_size("lat")
    n_lon = lax.axis_size(LON)
    n_obs = lax.axis_size("obs")
    tiles = n_lat * n_lon
    rows, cols = land_mask.shape
    sent = pack(obs_owner, block_count, innovation, obs_error, obs_offset, obs_cell, tiles)
    arrived = lax.all_to_all(
        sent.reshape(tiles, CAP * WORDS, 1, 128), LAT_LON, split_axis=0, concat_axis=0, tiled=True
    ).reshape(tiles * CAP * WORDS, 128)

    conduct = land_mask.astype(F32) * sea_depth
    lane = lax.broadcasted_iota(jnp.int32, (1, 128), 1)
    stacked = jnp.stack([conduct, inertia])
    from_west = around(stacked[:, :, cols - 128 :], LON, 1)
    from_east = around(stacked[:, :, :128], LON, -1)
    wide = jnp.concatenate([stacked, jnp.where(lane < 64, from_east, from_west)], axis=2)
    above = around(wide[:, rows - 8 :], LAT_OBS, 1)
    below = around(wide[:, :8], LAT_OBS, -1)
    conduct, inertia = jnp.concatenate([above, wide, below], axis=1)
    ocean = (conduct > 0.0).astype(F32)
    east = jnp.sqrt(conduct * jnp.roll(conduct, -1, 1))
    south = jnp.sqrt(conduct * jnp.roll(conduct, -1, 0))

    part = deposit(arrived, rows * n_obs, cols)
    tile = part + around(part, "obs", 1)
    spill = tile[:, cols:]
    from_west = around(jnp.where(lane == 0, spill[:, :1], tile[:, cols - 128 : cols]), LON, 1)
    from_east = around(tile[:, :128], LON, -1)
    tile = jnp.concatenate(
        [
            tile[:, :128] + jnp.where(lane == 0, from_west, 0.0),
            tile[:, 128:cols],
            jnp.where(lane < 64, from_east, from_west) + spill,
        ],
        axis=1,
    )
    side = lax.axis_index("obs").astype(jnp.int32)
    outer = jnp.where(side == 0, tile[:16], tile[2 * rows - 8 : 2 * rows + 8])
    swap = []
    for i in range(n_lat):
        swap.append((2 * i + 1, (2 * i + 2) % (2 * n_lat)))
        swap.append((2 * i, (2 * i - 1) % (2 * n_lat)))
    other = lax.ppermute(outer, LAT_OBS, swap)
    forcing, sums = basis(
        side.reshape(1), tile, other, ocean, inertia, east, south, tiles * n_obs
    )
    sums = lax.all_to_all(
        sums.reshape(tiles * n_obs, 1, 128), LAT_LON_OBS, split_axis=0, concat_axis=0, tiled=True
    ).reshape(tiles * n_obs, 128)
    return solve(sums, forcing, inertia, east, south, rows, cols)


def solution(mesh):
    split = Mesh(
        mesh.devices.reshape(mesh.shape["lat"], 4, 4, mesh.shape["obs"]),
        ("lat", "lon_0", "lon_1", "obs"),
    )
    return jax.shard_map(
        body,
        mesh=split,
        in_specs=(
            P(LAT_LON_OBS, None),
            P(LAT_LON_OBS, None),
            P(None, LAT_LON_OBS, None),
            P(LAT_LON_OBS, None),
            P(LAT_LON_OBS, None),
            P(LAT_LON_OBS),
            P(LAT_OBS, LON),
            P(LAT_OBS, LON),
            P(LAT_OBS, LON),
        ),
        out_specs=(P(LAT_OBS, LON), P(LAT_OBS, LON)),
        check_vma=False,
    )
```

time: 617 us -> 137 us (0.22)
  matrix products: 225 us -> 0 us
  blocking collectives: 218 us -> 23 us
  Pallas kernels: 0 us -> 53.9 us
  waiting for transfers between devices: 50.1 us -> 17.6 us
  starting transfers between devices: 66.1 us -> 34.8 us
  between operations: 19.6 us -> 1.39 us
  loops' own time: 12.5 us -> 0 us
  other arithmetic: 10.9 us -> 2.86 us
  local copies, waits for them, and re-layouts: 9.92 us -> 3.38 us
    dot_general x12 -> x0, matrix products: 225 us -> none  [spread(): jnp.dot(row_weights, col_weights, precision=lax.Precision.HIGHEST, prefer...]
    psum x20 -> x0, blocking collectives: 209 us -> none  [by_axis(): value = lax.psum(value, axis)]
    pallas_call x0 -> x4, Pallas kernels: none -> 53.9 us  [the longest x1 39.2 us: deposit(): pl.pallas_call(kernel, out_shape=jax.ShapeDtypeStruct((row_pad, tile_cols...]
    ppermute x26 -> x8, starting transfers between devices: 42.2 us -> 18.4 us  [the longest x7 16.7 us: around(): lax.ppermute(value, axis, [(i, (i + steps) % count) for i in range(count)])]
    all_to_all x2 -> x1, waiting for transfers between devices: 24.8 us -> 3.68 us  [body(): lax.all_to_all(sent.reshape(tiles, CAP * WORDS, 1, 128), LAT_LON, split_a...]
    all_to_all x1, blocking collectives: 9.04 us -> 23 us  [body(): lax.all_to_all(sums.reshape(tiles * n_obs, 1, 128), LAT_LON_OBS, split_ax...]
    another operation x1 -> x0, loops' own time: 12.5 us -> none  [body(): lax.scan(spread, jnp.zeros((tile_rows + 1, wide), jnp.float32), (scaled_i...]
    ppermute x26 -> x8, waiting for transfers between devices: 25.3 us -> 13.9 us  [the longest x7 12.2 us: around(): lax.ppermute(value, axis, [(i, (i + steps) % count) for i in range(count)])]
  transfers between devices with their start and end apart: 28 -> 9, of which waited for: 18 -> 7; matrix products, arithmetic and copies ran while one was open for 1% -> 2% of each run, Pallas kernels for 0% -> 0%
where the time goes in v1:
time: 137 us
  Pallas kernels  53.9 us (39%)
  starting transfers between devices  34.8 us (25%)
  blocking collectives  23 us (17%)
  waiting for transfers between devices  17.6 us (13%)
  local copies, waits for them, and re-layouts  3.38 us (2%)
  other arithmetic  2.86 us (2%)
  between operations  1.39 us (1%)
    pallas_call x1, Pallas kernels, deposit(): pl.pallas_call(kernel, out_shape=jax.ShapeDtypeStruct((row_pad, tile_cols...  39.2 us
    all_to_all x1, blocking collectives, body(): lax.all_to_all(sums.reshape(tiles * n_obs, 1, 128), LAT_LON_OBS, split_ax...  23 us
    ppermute x7, starting transfers between devices, around(): lax.ppermute(value, axis, [(i, (i + steps) % count) for i in range(count)])  16.7 us
    all_to_all x1, starting transfers between devices, body(): lax.all_to_all(sent.reshape(tiles, CAP * WORDS, 1, 128), LAT_LON, split_a...  16.5 us
    ppermute x7, waiting for transfers between devices, around(): lax.ppermute(value, axis, [(i, (i + steps) % count) for i in range(count)])  12.2 us
    pallas_call x1, Pallas kernels, basis(): pl.pallas_call(basis_kernel, out_shape=(jax.ShapeDtypeStruct(inertia.shap...  7.82 us
    all_to_all x1, waiting for transfers between devices, body(): lax.all_to_all(sent.reshape(tiles, CAP * WORDS, 1, 128), LAT_LON, split_a...  3.68 us
    pallas_call x1, Pallas kernels, pack(): pl.pallas_call(pack_kernel, out_shape=jax.ShapeDtypeStruct((tiles * CAP *...  3.45 us
  transfers between devices with their start and end apart: 9, of which 7 were waited for; matrix products, arithmetic and copies ran while one was open for 2% of the time, Pallas kernels for 0%

profile of v1, /device:TPU:1, one launch (start us, length us, event | category | flops | bytes accessed | tf_op | source)
XLA Modules:
  0.0 136.9 jit_solution(7038006912226445621)
XLA Ops:
  1.3 3.5 %pack.1 = f32[1536,128]{1,0:T(8,128)} custom-call(s32[1,128]{1,0:T(1,128)} %owner.1, s32[1]{0:T(128)S(6)} %copy.13.count, f32[128,128]{1,0:T(8,128)} %innovation.1, f32[128,128]{1,0:T(8,128)} %error.1, f32[2,128,128]{2,1,0:T(8,128)} %offset.1, s32[128,128]{1,0:T(8,128)} %cell.1), custom_call_target="tpu_custom_call" | custom-call | tf_op jit(solution)/shard_map/pack/pallas_call | solution.py:60
  4.7 0.0 copy-start.3
  4.7 0.0 copy-start.4
  4.7 16.5 %all-to-all-start = ((f32[128,12,1,128]{3,2,1,0:T(1,128)}), f32[128,12,1,128]{3,2,1,0:T(1,128)S(1)}, u32[]{:S(2)}, u32[]{:S(2)}) async-start(f32[128,12,1,128]{3,2,1,0:T(1,128)} %bitcast.25), calls=%async_computation | async-start | bytes 1572864 | tf_op jit(solution)/shard_map/all_to_all | solution.py:393
  21.2 0.0 copy-done.3
  21.2 0.0 copy-done.4
  21.2 0.0 copy-start.2
  21.3 0.9 copy-done.2
  22.1 3.9 %collective-permute-start.4 = (f32[2,32,128]{2,1,0:T(8,128)S(1)}, f32[2,32,128]{2,1,0:T(8,128)S(1)}, u32[]{:S(2)}, u32[]{:S(2)}) collective-permute-start(f32[2,32,128]{2,1,0:T(8,128)S(1)} %get-tuple-element.17), channel_id=1, source_target_pairs={{0,30},{2,0},{4,2},{6,4},{8,6},{10,8},{12,10},{14,12},{16,14},{18,... | collective-permute-start | bytes 98312 | tf_op jit(solution)/shard_map/ppermute | solution.py:373
  26.0 0.0 collective-permute-start.5
  26.1 1.0 collective-permute-done.4
  27.1 5.8 %collective-permute-done.5 = f32[2,32,128]{2,1,0:T(8,128)S(1)} collective-permute-done((f32[2,32,128]{2,1,0:T(8,128)S(1)}, f32[2,32,128]{2,1,0:T(8,128)S(1)}, u32[]{:S(2)}, u32[]{:S(2)}) %collective-permute-start.5) | collective-permute-done | bytes 32800 | tf_op jit(solution)/shard_map/ppermute | solution.py:373
  32.9 2.1 %collective-permute-start.7 = (f32[2,8,1152]{2,1,0:T(8,128)S(1)}, f32[2,8,1152]{2,1,0:T(8,128)S(1)}, u32[]{:S(2)}, u32[]{:S(2)}) collective-permute-start(f32[2,8,1152]{2,1,0:T(8,128)S(1)} %get-tuple-element.15), channel_id=1, source_target_pairs={{0,225},{1,0},{32,1},{33,32},{64,33},{65,64},{96,65},{97,96},{128,... | collective-permute-start | bytes 221192 | tf_op jit(solution)/shard_map/ppermute | solution.py:373
  35.1 1.5 %collective-permute-start.6 = (f32[2,8,1152]{2,1,0:T(8,128)S(1)}, f32[2,8,1152]{2,1,0:T(8,128)S(1)}, u32[]{:S(2)}, u32[]{:S(2)}) collective-permute-start(f32[2,8,1152]{2,1,0:T(8,128)S(1)} %get-tuple-element.14), channel_id=1, source_target_pairs={{0,1},{1,32},{32,33},{33,64},{64,65},{65,96},{96,97},{97,128},{128... | collective-permute-start | bytes 221192 | tf_op jit(solution)/shard_map/ppermute | solution.py:373
  36.6 3.4 %collective-permute-done.7 = f32[2,8,1152]{2,1,0:T(8,128)S(1)} collective-permute-done((f32[2,8,1152]{2,1,0:T(8,128)S(1)}, f32[2,8,1152]{2,1,0:T(8,128)S(1)}, u32[]{:S(2)}, u32[]{:S(2)}) %collective-permute-start.7) | collective-permute-done | bytes 73760 | tf_op jit(solution)/shard_map/ppermute | solution.py:373
  40.0 0.0 collective-permute-done.6
  40.1 0.7 slice_bitcast_fusion.2
  40.8 0.1 slice.84
  40.9 3.7 %all-to-all-done = f32[128,12,1,128]{3,2,1,0:T(1,128)S(1)} async-done(((f32[128,12,1,128]{3,2,1,0:T(1,128)}), f32[128,12,1,128]{3,2,1,0:T(1,128)S(1)}, u32[]{:S(2)}, u32[]{:S(2)}) %all-to-all-start) | async-done | bytes 786464 | tf_op jit(solution)/shard_map/all_to_all | solution.py:393
  44.6 0.0 copy-start
  44.6 0.9 copy-done
  45.5 39.2 %deposit.1 = f32[72,1152]{1,0:T(8,128)} custom-call(f32[1536,128]{1,0:T(8,128)} %bitcast.24), custom_call_target="tpu_custom_call" | custom-call | tf_op jit(solution)/shard_map/deposit/pallas_call | solution.py:154
  84.7 4.4 %collective-permute-start = (f32[72,1152]{1,0:T(8,128)}, f32[72,1152]{1,0:T(8,128)S(1)}, u32[]{:S(2)}, u32[]{:S(2)}) collective-permute-start(f32[72,1152]{1,0:T(8,128)} %deposit.1), channel_id=1, source_target_pairs={{0,1},{1,0},{2,3},{3,2},{4,5},{5,4},{6,7},{7,6},{8,9},{9,8},{10,11... | collective-permute-start | bytes 995336 | tf_op jit(solution)/shard_map/ppermute | solution.py:373
  89.1 1.5 %collective-permute-done = f32[72,1152]{1,0:T(8,128)S(1)} collective-permute-done((f32[72,1152]{1,0:T(8,128)}, f32[72,1152]{1,0:T(8,128)S(1)}, u32[]{:S(2)}, u32[]{:S(2)}) %collective-permute-start) | collective-permute-done | bytes 331808 | tf_op jit(solution)/shard_map/ppermute | solution.py:373
  90.5 1.0 add.9
  91.6 0.1 slice_reduce_fusion
  91.7 0.1 slice_select_fusion.1
  91.7 0.5 collective-permute-start.1
  92.2 4.4 %collective-permute-start.2 = (f32[72,128]{1,0:T(8,128)S(1)}, f32[72,128]{1,0:T(8,128)S(1)}, u32[]{:S(2)}, u32[]{:S(2)}) collective-permute-start(f32[72,128]{1,0:T(8,128)S(1)} %get-tuple-element.13), channel_id=1, source_target_pairs={{0,30},{2,0},{4,2},{6,4},{8,6},{10,8},{12,10},{14,12},{16,14},{18,... | collective-permute-start | bytes 110600 | tf_op jit(solution)/shard_map/ppermute | solution.py:373
  96.6 0.9 fusion.1
  97.5 0.4 collective-permute-done.1
  97.9 0.0 collective-permute-done.2
  98.0 0.0 copy-start.1
  98.0 1.6 %collective-permute-start.3 = (f32[16,1152]{1,0:T(8,128)S(1)}, f32[16,1152]{1,0:T(8,128)S(1)}, u32[]{:S(2)}, u32[]{:S(2)}) collective-permute-start(f32[16,1152]{1,0:T(8,128)S(1)} %slice_select_fusion), channel_id=1, source_target_pairs={{1,32},{0,225},{33,64},{32,1},{65,96},{64,33},{97,128},{96,65},{12... | collective-permute-start | bytes 221192 | tf_op jit(solution)/shard_map/ppermute | solution.py:429
  99.6 0.7 compare_convert_fusion.ocean
  100.3 0.0 copy-done.1
  100.3 1.7 %collective-permute-done.3.other = f32[16,1152]{1,0:T(8,128)S(1)} collective-permute-done((f32[16,1152]{1,0:T(8,128)S(1)}, f32[16,1152]{1,0:T(8,128)S(1)}, u32[]{:S(2)}, u32[]{:S(2)}) %collective-permute-start.3) | collective-permute-done | bytes 73760 | tf_op jit(solution)/shard_map/ppermute | solution.py:429
  102.0 0.0 copy-start.5
  102.0 0.6 copy-done.5
  102.7 7.8 %basis.1 = (f32[48,1152]{1,0:T(8,128)}, f32[256,128]{1,0:T(8,128)}) custom-call(s32[1]{0:T(128)} %bitcast.side, f32[72,1152]{1,0:T(8,128)} %copy-done.1, f32[16,1152]{1,0:T(8,128)} %copy-done.5, f32[48,1152]{1,0:T(8,128)} %compare_convert_fusion.ocean, f32[48,1152]{1,0:T(8,128)} %get-tuple-element.9.inertia, f32[48,1152]{1,0:T(8,128)} %get-tuple-element.7.east, ...), custom_call_target="tpu_custom_call" | custom-call | tf_op jit(solution)/shard_map/basis/pallas_call | solution.py:304
  110.5 23.0 %all_to_all.10 = f32[256,1,128]{2,1,0:T(1,128)} all-to-all(f32[256,1,128]{2,1,0:T(1,128)} %bitcast.30), channel_id=1, replica_groups=mesh['lat'=8,'lon_0'=4,'lon_1'=4,'obs'=2] {'lat','lon_0','lon_1','obs'}, dimensions={0} | all-to-all | bytes 262144 | tf_op jit(solution)/shard_map/all_to_all | solution.py:433
  133.5 3.4 %solve.1 = (f32[32,1024]{1,0:T(8,128)}, f32[32,1024]{1,0:T(8,128)}) custom-call(f32[256,128]{1,0:T(8,128)} %bitcast.29, f32[48,1152]{1,0:T(8,128)} %get-tuple-element.5.forcing, f32[48,1152]{1,0:T(8,128)} %get-tuple-element.9.inertia, f32[48,1152]{1,0:T(8,128)} %get-tuple-element.7.east, f32[48,1152]{1,0:T(8,128)} %get-tuple-element.6.south), custom_call_target="tpu_custom_call" | custom-call | tf_op jit(solution)/shard_map/solve/pallas_call | solution.py:362
  (14 shorter events, 0.2 us)
Async XLA Ops:
  4.7 16.5 %copy-start.3 = (f32[32,1024]{1,0:T(8,128)S(1)}, f32[32,1024]{1,0:T(8,128)}, u32[]{:S(2)}) copy-start(f32[32,1024]{1,0:T(8,128)} %param.17) | copy-start | bytes 393220
  4.7 16.5 %copy-start.4 = (s32[32,1024]{1,0:T(8,128)S(1)}, s32[32,1024]{1,0:T(8,128)}, u32[]{:S(2)}) copy-start(s32[32,1024]{1,0:T(8,128)} %param.15) | copy-start | bytes 393220
  4.7 39.9 %all-to-all-start = ((f32[128,12,1,128]{3,2,1,0:T(1,128)}), f32[128,12,1,128]{3,2,1,0:T(1,128)S(1)}, u32[]{:S(2)}, u32[]{:S(2)}) async-start(f32[128,12,1,128]{3,2,1,0:T(1,128)} %bitcast.25), calls=%async_computation | async-start | bytes 1572864 | tf_op jit(solution)/shard_map/all_to_all | solution.py:393
  21.2 0.9 copy-start.2
  22.1 5.0 %collective-permute-start.4 = (f32[2,32,128]{2,1,0:T(8,128)S(1)}, f32[2,32,128]{2,1,0:T(8,128)S(1)}, u32[]{:S(2)}, u32[]{:S(2)}) collective-permute-start(f32[2,32,128]{2,1,0:T(8,128)S(1)} %get-tuple-element.17), channel_id=1, source_target_pairs={{0,30},{2,0},{4,2},{6,4},{8,6},{10,8},{12,10},{14,12},{16,14},{18,... | collective-permute-start | bytes 98312 | tf_op jit(solution)/shard_map/ppermute | solution.py:373
  26.0 6.9 %collective-permute-start.5 = (f32[2,32,128]{2,1,0:T(8,128)S(1)}, f32[2,32,128]{2,1,0:T(8,128)S(1)}, u32[]{:S(2)}, u32[]{:S(2)}) collective-permute-start(f32[2,32,128]{2,1,0:T(8,128)S(1)} %get-tuple-element.16), channel_id=1, source_target_pairs={{0,2},{2,4},{4,6},{6,8},{8,10},{10,12},{12,14},{14,16},{16,18},{18... | collective-permute-start | bytes 98312 | tf_op jit(solution)/shard_map/ppermute | solution.py:373
  32.9 7.1 %collective-permute-start.7 = (f32[2,8,1152]{2,1,0:T(8,128)S(1)}, f32[2,8,1152]{2,1,0:T(8,128)S(1)}, u32[]{:S(2)}, u32[]{:S(2)}) collective-permute-start(f32[2,8,1152]{2,1,0:T(8,128)S(1)} %get-tuple-element.15), channel_id=1, source_target_pairs={{0,225},{1,0},{32,1},{33,32},{64,33},{65,64},{96,65},{97,96},{128,... | collective-permute-start | bytes 221192 | tf_op jit(solution)/shard_map/ppermute | solution.py:373
  35.1 4.9 %collective-permute-start.6 = (f32[2,8,1152]{2,1,0:T(8,128)S(1)}, f32[2,8,1152]{2,1,0:T(8,128)S(1)}, u32[]{:S(2)}, u32[]{:S(2)}) collective-permute-start(f32[2,8,1152]{2,1,0:T(8,128)S(1)} %get-tuple-element.14), channel_id=1, source_target_pairs={{0,1},{1,32},{32,33},{33,64},{64,65},{65,96},{96,97},{97,128},{128... | collective-permute-start | bytes 221192 | tf_op jit(solution)/shard_map/ppermute | solution.py:373
  44.6 0.9 copy-start
  84.7 5.8 %collective-permute-start = (f32[72,1152]{1,0:T(8,128)}, f32[72,1152]{1,0:T(8,128)S(1)}, u32[]{:S(2)}, u32[]{:S(2)}) collective-permute-start(f32[72,1152]{1,0:T(8,128)} %deposit.1), channel_id=1, source_target_pairs={{0,1},{1,0},{2,3},{3,2},{4,5},{5,4},{6,7},{7,6},{8,9},{9,8},{10,11... | collective-permute-start | bytes 995336 | tf_op jit(solution)/shard_map/ppermute | solution.py:373
  91.7 6.2 %collective-permute-start.1 = (f32[72,128]{1,0:T(8,128)S(1)}, f32[72,128]{1,0:T(8,128)S(1)}, u32[]{:S(2)}, u32[]{:S(2)}) collective-permute-start(f32[72,128]{1,0:T(8,128)S(1)} %get-tuple-element.12), channel_id=1, source_target_pairs={{0,2},{2,4},{4,6},{6,8},{8,10},{10,12},{12,14},{14,16},{16,18},{18... | collective-permute-start | bytes 110600 | tf_op jit(solution)/shard_map/ppermute | solution.py:373
  92.2 5.7 %collective-permute-start.2 = (f32[72,128]{1,0:T(8,128)S(1)}, f32[72,128]{1,0:T(8,128)S(1)}, u32[]{:S(2)}, u32[]{:S(2)}) collective-permute-start(f32[72,128]{1,0:T(8,128)S(1)} %get-tuple-element.13), channel_id=1, source_target_pairs={{0,30},{2,0},{4,2},{6,4},{8,6},{10,8},{12,10},{14,12},{16,14},{18,... | collective-permute-start | bytes 110600 | tf_op jit(solution)/shard_map/ppermute | solution.py:373
  98.0 2.4 %copy-start.1 = (f32[72,1152]{1,0:T(8,128)}, f32[72,1152]{1,0:T(8,128)S(1)}, u32[]{:S(2)}) copy-start(f32[72,1152]{1,0:T(8,128)S(1)} %pad_maximum_fusion.1.tile) | copy-start | bytes 995332
  98.0 4.0 %collective-permute-start.3 = (f32[16,1152]{1,0:T(8,128)S(1)}, f32[16,1152]{1,0:T(8,128)S(1)}, u32[]{:S(2)}, u32[]{:S(2)}) collective-permute-start(f32[16,1152]{1,0:T(8,128)S(1)} %slice_select_fusion), channel_id=1, source_target_pairs={{1,32},{0,225},{33,64},{32,1},{65,96},{64,33},{97,128},{96,65},{12... | collective-permute-start | bytes 221192 | tf_op jit(solution)/shard_map/ppermute | solution.py:429
  102.0 0.6 copy-start.5

commit v2 on v1

--- a/solution.py
+++ b/solution.py
@@ -16,8 +16,10 @@
 LAT_LON = ("lat", "lon_0", "lon_1")
 F32 = jnp.float32
 BF16 = jnp.bfloat16
-GROUPS = 2
-CHUNK = 8
+GROUPS = 4
+CHUNK = 16
+EDGE = 16
+EARLY = 2
 
 
 def vmem():
@@ -28,15 +30,16 @@
     return pl.BlockSpec(memory_space=pltpu.SMEM)
 
 
-def pack_kernel(owner, count, innovation, error, offset, cell, out, rows, seen):
+def pack_kernel(owner, count, innovation, error, offset, cell, early, late, rows, seen):
     blocks = innovation.shape[0]
-    tiles = out.shape[0] // (CAP * WORDS)
+    tiles = early.shape[0] // (EARLY * WORDS)
     err = error[...]
     rows[pl.ds(0, blocks, stride=WORDS), :] = innovation[...] / (err * err)
     rows[pl.ds(1, blocks, stride=WORDS), :] = offset[0]
     rows[pl.ds(2, blocks, stride=WORDS), :] = offset[1]
     rows[pl.ds(3, blocks, stride=WORDS), :] = cell[...].astype(F32)
-    out[...] = jnp.zeros(out.shape, F32)
+    early[...] = jnp.zeros(early.shape, F32)
+    late[...] = jnp.zeros(late.shape, F32)
 
     def clear(tile, carry):
         seen[tile] = 0
@@ -48,8 +51,16 @@
         tile = owner[0, block]
         rank = seen[tile]
         seen[tile] = rank + 1
-        slot = tile * CAP + rank
-        out[pl.ds(slot * WORDS, WORDS), :] = rows[pl.ds(block * WORDS, WORDS), :]
+        values = rows[pl.ds(block * WORDS, WORDS), :]
+
+        @pl.when(rank < EARLY)
+        def _():
+            early[pl.ds((tile * EARLY + rank) * WORDS, WORDS), :] = values
+
+        @pl.when(rank >= EARLY)
+        def _():
+            late[pl.ds((tile * (CAP - EARLY) + rank - EARLY) * WORDS, WORDS), :] = values
+
         return carry
 
     lax.fori_loop(0, count[0], place, 0)
@@ -59,30 +70,44 @@
     blocks = innovation.shape[0]
     return pl.pallas_call(
         pack_kernel,
-        out_shape=jax.ShapeDtypeStruct((tiles * CAP * WORDS, 128), F32),
+        out_shape=(
+            jax.ShapeDtypeStruct((tiles * EARLY * WORDS, 128), F32),
+            jax.ShapeDtypeStruct((tiles * (CAP - EARLY) * WORDS, 128), F32),
+        ),
         in_specs=[smem(), smem(), vmem(), vmem(), vmem(), vmem()],
-        out_specs=vmem(),
+        out_specs=(vmem(), vmem()),
         scratch_shapes=[pltpu.VMEM((blocks * WORDS, 128), F32), pltpu.SMEM((tiles,), jnp.int32)],
         name="pack",
     )(owner, count, innovation, error, offset, cell)
 
 
-def deposit(arrived, tile_rows, tile_cols):
+def rows_of(count):
+    return (count + 1 + 7) // 8 * 8
+
+
+def deposit_step(arrived, sofar, tile_rows, tile_cols, last):
     slots = arrived.shape[0] // WORDS
-    row_pad = (tile_rows + 1 + 7) // 8 * 8
-    m_one = (GROUPS * row_pad + 15) // 16 * 16
     width = tile_cols // GROUPS
-    m_all = 4 * m_one
+    m_one = GROUPS * tile_rows
+    m_all = 2 * (2 * m_one + EDGE)
     steps = slots // CHUNK
     half_m = m_one // 2
     half_n = width // 2
-
-    def kernel(src, out, left_a, left_b, right_a, right_b, acc):
+    low_at = 2 * m_one + EDGE
+    row_pad = rows_of(tile_rows)
+
+    def kernel(*refs):
+        if sofar is None:
+            src, out, left_a, left_b, right_a, right_b, acc = refs
+        else:
+            src, before_ref, out, left_a, left_b, right_a, right_b, acc = refs
         m_index = (lax.broadcasted_iota(jnp.int32, (m_one, 128), 0) - half_m).astype(F32).astype(BF16)
         n_index = (lax.broadcasted_iota(jnp.int32, (width, 128), 0) - half_n).astype(F32).astype(BF16)
+        e_index = lax.broadcasted_iota(jnp.int32, (EDGE, 128), 0).astype(F32).astype(BF16)
         n_one = jnp.ones((width, 128), BF16)
         n_zero = jnp.zeros((width, 128), BF16)
         m_zero = jnp.zeros((m_one, 128), BF16)
+        e_zero = jnp.zeros((EDGE, 128), BF16)
 
         def spread(x, j, n):
             row = jnp.broadcast_to(x[j : j + 1, :], (16, 128)).astype(BF16)
@@ -96,36 +121,52 @@
             cell = src[pl.ds(base + 3, CHUNK, stride=WORDS), :].astype(jnp.int32)
             row = cell // tile_cols
             col = cell % tile_cols
-            m_here = ((col // width) * row_pad + row - half_m).astype(F32)
-            m_next = m_here + 1.0
+            group = col // width
+            at_edge = row == tile_rows - 1
+            m_here = (group * tile_rows + row - half_m).astype(F32)
+            m_next = jnp.where(at_edge, 1.0e4, m_here + 1.0)
             n_here = (col % width - half_n).astype(F32)
+            e_here = jnp.where(at_edge, group, 4 * EDGE).astype(F32)
             pieces = []
             for value in (amount, amount * east):
                 low = value * (1.0 - north)
                 high = value * north
                 low_top = low.astype(BF16).astype(F32)
                 high_top = high.astype(BF16).astype(F32)
-                pieces.append((low_top, high_top))
-                pieces.append((low - low_top, high - high_top))
+                pieces.append(((low_top, high_top), (low - low_top, high - high_top)))
             for j in range(CHUNK):
                 at_row = m_index == spread(m_here, j, m_one)
                 at_next = m_index == spread(m_next, j, m_one)
-                for k, (low, high) in enumerate(pieces):
-                    left[k * m_one : (k + 1) * m_one, j * 128 : (j + 1) * 128] = jnp.where(
-                        at_row,
-                        spread(low, j, m_one),
-                        jnp.where(at_next, spread(high, j, m_one), m_zero),
+                whole_edge = e_index == spread(e_here, j, EDGE)
+                part_edge = e_index == spread(e_here + GROUPS, j, EDGE)
+                for k in range(2):
+                    start = k * low_at
+                    for field in range(2):
+                        low, high = pieces[field][k]
+                        left[j, start + field * m_one : start + (field + 1) * m_one] = jnp.where(
+                            at_row,
+                            spread(low, j, m_one),
+                            jnp.where(at_next, spread(high, j, m_one), m_zero),
+                        )
+                    left[j, start + 2 * m_one : start + low_at] = jnp.where(
+                        whole_edge,
+                        spread(pieces[0][k][1], j, EDGE),
+                        jnp.where(part_edge, spread(pieces[1][k][1], j, EDGE), e_zero),
                     )
-                right[:, j * 128 : (j + 1) * 128] = jnp.where(
-                    n_index == spread(n_here, j, width), n_one, n_zero
-                )
+                right[j] = jnp.where(n_index == spread(n_here, j, width), n_one, n_zero)
+
+        def joined(ref):
+            return jnp.concatenate([ref[j] for j in range(CHUNK)], axis=1)
 
         def add(left, right):
             acc[...] += lax.dot_general(
-                left[...], right[...], (((1,), (1,)), ((), ())), preferred_element_type=F32
+                joined(left), joined(right), (((1,), (1,)), ((), ())), preferred_element_type=F32
             )
 
-        acc[...] = jnp.zeros((m_all, width), F32)
+        if sofar is None:
+            acc[...] = jnp.zeros((m_all, width), F32)
+        else:
+            acc[...] = before_ref[...]
         build(0, left_a, right_a)
 
         def turn(i, carry):
@@ -136,12 +177,22 @@
             return carry
 
         lax.fori_loop(0, steps // 2, turn, 0)
+        if not last:
+            out[...] = acc[...]
+            return
+        acc[0:low_at] = acc[0:low_at] + acc[low_at:m_all]
         lane = lax.broadcasted_iota(jnp.int32, (row_pad, width), 1)
         before = jnp.zeros((row_pad, 1), F32)
+        blank = jnp.zeros((row_pad - tile_rows - 1, width), F32)
+
+        def field_of(g, field):
+            top = field * m_one + g * tile_rows
+            edge = 2 * m_one + field * GROUPS + g
+            return jnp.concatenate([acc[top : top + tile_rows], acc[edge : edge + 1], blank], 0)
+
         for g in range(GROUPS):
-            s = g * row_pad
-            whole = acc[s : s + row_pad] + acc[m_one + s : m_one + s + row_pad]
-            part = acc[2 * m_one + s : 2 * m_one + s + row_pad] + acc[3 * m_one + s : 3 * m_one + s + row_pad]
+            whole = field_of(g, 0)
+            part = field_of(g, 1)
             moved = pltpu.roll(part, 1, 1)
             moved = jnp.where(lane == 0, jnp.broadcast_to(before, (row_pad, width)), moved)
             out[:, g * width : (g + 1) * width] = whole - part + moved
@@ -151,20 +202,22 @@
             edge == 0, jnp.broadcast_to(before, (row_pad, 128)), 0.0
         )
 
+    shape = (row_pad, tile_cols + 128) if last else (m_all, width)
+    operands = (arrived,) if sofar is None else (arrived, sofar)
     return pl.pallas_call(
         kernel,
-        out_shape=jax.ShapeDtypeStruct((row_pad, tile_cols + 128), F32),
-        in_specs=[vmem()],
+        out_shape=jax.ShapeDtypeStruct(shape, F32),
+        in_specs=[vmem()] * len(operands),
         out_specs=vmem(),
         scratch_shapes=[
-            pltpu.VMEM((m_all, CHUNK * 128), BF16),
-            pltpu.VMEM((m_all, CHUNK * 128), BF16),
-            pltpu.VMEM((width, CHUNK * 128), BF16),
-            pltpu.VMEM((width, CHUNK * 128), BF16),
+            pltpu.VMEM((CHUNK, m_all, 128), BF16),
+            pltpu.VMEM((CHUNK, m_all, 128), BF16),
+            pltpu.VMEM((CHUNK, width, 128), BF16),
+            pltpu.VMEM((CHUNK, width, 128), BF16),
             pltpu.VMEM((m_all, width), F32),
         ],
-        name="deposit",
-    )(arrived)
+        name="deposit_last" if last else "deposit_first",
+    )(*operands)
 
 
 def two_sum(a, b):
@@ -390,9 +443,12 @@
     tiles = n_lat * n_lon
     rows, cols = land_mask.shape
     sent = pack(obs_owner, block_count, innovation, obs_error, obs_offset, obs_cell, tiles)
-    arrived = lax.all_to_all(
-        sent.reshape(tiles, CAP * WORDS, 1, 128), LAT_LON, split_axis=0, concat_axis=0, tiled=True
-    ).reshape(tiles * CAP * WORDS, 128)
+    arrived = [
+        lax.all_to_all(
+            part.reshape(tiles, -1, 1, 128), LAT_LON, split_axis=0, concat_axis=0, tiled=True
+        ).reshape(-1, 128)
+        for part in sent
+    ]
 
     conduct = land_mask.astype(F32) * sea_depth
     lane = lax.broadcasted_iota(jnp.int32, (1, 128), 1)
@@ -407,7 +463,8 @@
     east = jnp.sqrt(conduct * jnp.roll(conduct, -1, 1))
     south = jnp.sqrt(conduct * jnp.roll(conduct, -1, 0))
 
-    part = deposit(arrived, rows * n_obs, cols)
+    part = deposit_step(arrived[0], None, rows * n_obs, cols, False)
+    part = deposit_step(arrived[1], part, rows * n_obs, cols, True)
     tile = part + around(part, "obs", 1)
     spill = tile[:, cols:]
     from_west = around(jnp.where(lane == 0, spill[:, :1], tile[:, cols - 128 : cols]), LON, 1)

time: 137 us -> 145 us (1.058)
  starting transfers between devices: 34.8 us -> 42 us
  blocking collectives: 23 us -> 27.3 us
  waiting for transfers between devices: 17.6 us -> 13.9 us
    all_to_all x1 -> x2, starting transfers between devices: 16.5 us -> 24.9 us  [body(): lax.all_to_all(part.reshape(tiles, -1, 1, 128), LAT_LON, split_axis=0, co...]
    all_to_all x1, blocking collectives: 23 us -> 27.3 us  [body(): lax.all_to_all(sums.reshape(tiles * n_obs, 1, 128), LAT_LON_OBS, split_ax...]
    ppermute x7, starting transfers between devices: 16.7 us -> 14.7 us  [around(): lax.ppermute(value, axis, [(i, (i + steps) % count) for i in range(count)])]
    all_to_all x1 -> x2, waiting for transfers between devices: 3.68 us -> 1.71 us  [body(): lax.all_to_all(part.reshape(tiles, -1, 1, 128), LAT_LON, split_axis=0, co...]
    pallas_call x2 -> x3, Pallas kernels: 42.6 us -> 43.5 us  [the longest x2 39.3 us: deposit_step(): pl.pallas_call(kernel, out_shape=jax.ShapeDtypeStruct(shape, F32), in_spe...]
  transfers between devices with their start and end apart: 9 -> 10, of which waited for: 7 -> 7; matrix products, arithmetic and copies ran while one was open for 2% -> 2% of each run, Pallas kernels for 0% -> 17%
where the time goes in v2:
time: 145 us
  Pallas kernels  54.8 us (38%)
  starting transfers between devices  42 us (29%)
  blocking collectives  27.3 us (19%)
  waiting for transfers between devices  13.9 us (10%)
  other arithmetic  2.84 us (2%)
  local copies, waits for them, and re-layouts  2.34 us (2%)
  between operations  1.49 us (1%)
    pallas_call x2, Pallas kernels, deposit_step(): pl.pallas_call(kernel, out_shape=jax.ShapeDtypeStruct(shape, F32), in_spe...  39.3 us
    all_to_all x1, blocking collectives, body(): lax.all_to_all(sums.reshape(tiles * n_obs, 1, 128), LAT_LON_OBS, split_ax...  27.3 us
    all_to_all x2, starting transfers between devices, body(): lax.all_to_all(part.reshape(tiles, -1, 1, 128), LAT_LON, split_axis=0, co...  24.9 us
    ppermute x7, starting transfers between devices, around(): lax.ppermute(value, axis, [(i, (i + steps) % count) for i in range(count)])  14.7 us
    ppermute x7, waiting for transfers between devices, around(): lax.ppermute(value, axis, [(i, (i + steps) % count) for i in range(count)])  10.8 us
    pallas_call x1, Pallas kernels, basis(): pl.pallas_call(basis_kernel, out_shape=(jax.ShapeDtypeStruct(inertia.shap...  7.82 us
    pallas_call x1, Pallas kernels, pack(): pl.pallas_call(pack_kernel, out_shape=(jax.ShapeDtypeStruct((tiles * EARL...  4.2 us
    pallas_call x1, Pallas kernels, solve(): pl.pallas_call(solve_kernel, out_shape=(shape, shape), in_specs=[vmem()]...  3.43 us
  transfers between devices with their start and end apart: 10, of which 7 were waited for; matrix products, arithmetic and copies ran while one was open for 2% of the time, Pallas kernels for 17%

profile of v2, /device:TPU:1, one launch (start us, length us, event | category | flops | bytes accessed | tf_op | source)
XLA Modules:
  0.0 144.6 jit_solution(959771421239094228)
XLA Ops:
  0.6 0.0 copy-start.4
  0.6 0.0 copy-start.5
  0.7 0.0 copy-start.2
  1.4 4.2 %pack.1 = (f32[1024,128]{1,0:T(8,128)}, f32[512,128]{1,0:T(8,128)}) custom-call(s32[1,128]{1,0:T(1,128)} %owner.1, s32[1]{0:T(128)S(6)} %copy.14.count, f32[128,128]{1,0:T(8,128)} %innovation.1, f32[128,128]{1,0:T(8,128)} %error.1, f32[2,128,128]{2,1,0:T(8,128)} %offset.1, s32[128,128]{1,0:T(8,128)} %cell.1), custom_call_target="tpu_custom_call" | custom-call | tf_op jit(solution)/shard_map/pack/pallas_call | solution.py:71
  5.6 16.9 %all-to-all-start.1 = ((f32[128,8,1,128]{3,1,2,0:T(8,128)}), f32[128,8,1,128]{3,1,2,0:T(8,128)S(1)}, u32[]{:S(2)}, u32[]{:S(2)}) async-start(f32[128,8,1,128]{3,1,2,0:T(8,128)} %bitcast.35), calls=%async_computation.1 | async-start | bytes 1048576 | tf_op jit(solution)/shard_map/all_to_all | solution.py:447
  22.5 0.0 copy-done.4
  22.5 0.0 copy-done.5
  22.5 0.0 copy-done.2
  22.5 4.0 %collective-permute-start.4 = (f32[2,32,128]{2,1,0:T(8,128)S(1)}, f32[2,32,128]{2,1,0:T(8,128)S(1)}, u32[]{:S(2)}, u32[]{:S(2)}) collective-permute-start(f32[2,32,128]{2,1,0:T(8,128)S(1)} %get-tuple-element.21), channel_id=1, source_target_pairs={{0,30},{2,0},{4,2},{6,4},{8,6},{10,8},{12,10},{14,12},{16,14},{18,... | collective-permute-start | bytes 98312 | tf_op jit(solution)/shard_map/ppermute | solution.py:426
  26.5 0.0 collective-permute-start.5
  26.5 1.1 collective-permute-done.4
  27.7 5.5 %collective-permute-done.5 = f32[2,32,128]{2,1,0:T(8,128)S(1)} collective-permute-done((f32[2,32,128]{2,1,0:T(8,128)S(1)}, f32[2,32,128]{2,1,0:T(8,128)S(1)}, u32[]{:S(2)}, u32[]{:S(2)}) %collective-permute-start.5) | collective-permute-done | bytes 32800 | tf_op jit(solution)/shard_map/ppermute | solution.py:426
  33.2 2.6 %collective-permute-start.7 = (f32[2,8,1152]{2,1,0:T(8,128)S(1)}, f32[2,8,1152]{2,1,0:T(8,128)S(1)}, u32[]{:S(2)}, u32[]{:S(2)}) collective-permute-start(f32[2,8,1152]{2,1,0:T(8,128)S(1)} %get-tuple-element.19), channel_id=1, source_target_pairs={{0,225},{1,0},{32,1},{33,32},{64,33},{65,64},{96,65},{97,96},{128,... | collective-permute-start | bytes 221192 | tf_op jit(solution)/shard_map/ppermute | solution.py:426
  35.8 1.0 collective-permute-start.6
  36.9 2.3 %collective-permute-done.7 = f32[2,8,1152]{2,1,0:T(8,128)S(1)} collective-permute-done((f32[2,8,1152]{2,1,0:T(8,128)S(1)}, f32[2,8,1152]{2,1,0:T(8,128)S(1)}, u32[]{:S(2)}, u32[]{:S(2)}) %collective-permute-start.7) | collective-permute-done | bytes 73760 | tf_op jit(solution)/shard_map/ppermute | solution.py:426
  39.2 0.0 collective-permute-done.6
  39.2 1.7 %all-to-all-done.1 = f32[128,8,1,128]{3,1,2,0:T(8,128)S(1)} async-done(((f32[128,8,1,128]{3,1,2,0:T(8,128)}), f32[128,8,1,128]{3,1,2,0:T(8,128)S(1)}, u32[]{:S(2)}, u32[]{:S(2)}) %all-to-all-start.1) | async-done | bytes 524320 | tf_op jit(solution)/shard_map/all_to_all | solution.py:447
  40.9 0.0 copy-start
  40.9 8.0 %all-to-all-start = ((f32[128,4,1,128]{3,1,2,0:T(4,128)}), f32[128,4,1,128]{3,1,2,0:T(4,128)S(1)}, u32[]{:S(2)}, u32[]{:S(2)}) async-start(f32[128,4,1,128]{3,1,2,0:T(4,128)} %bitcast.2), calls=%async_computation | async-start | bytes 524288 | tf_op jit(solution)/shard_map/all_to_all | solution.py:447
  48.9 0.7 slice_bitcast_fusion.2
  49.6 0.1 slice.84
  49.8 0.0 copy-done
  49.8 25.1 %deposit_first.1.refs_1_ = f32[1056,256]{1,0:T(8,128)} custom-call(f32[1024,128]{1,0:T(8,128)} %bitcast.30), custom_call_target="tpu_custom_call" | custom-call | tf_op jit(solution)/shard_map/deposit_first/pallas_call | solution.py:207
  74.9 0.0 all-to-all-done
  74.9 0.0 copy-start.3
  74.9 0.7 copy-done.3
  75.6 14.3 %deposit_last.1 = f32[72,1152]{1,0:T(8,128)} custom-call(f32[512,128]{1,0:T(8,128)} %bitcast.34, f32[1056,256]{1,0:T(8,128)} %deposit_first.1.refs_1_), custom_call_target="tpu_custom_call" | custom-call | tf_op jit(solution)/shard_map/deposit_last/pallas_call | solution.py:207
  89.9 2.2 %collective-permute-start = (f32[72,1152]{1,0:T(8,128)}, f32[72,1152]{1,0:T(8,128)S(1)}, u32[]{:S(2)}, u32[]{:S(2)}) collective-permute-start(f32[72,1152]{1,0:T(8,128)} %deposit_last.1), channel_id=1, source_target_pairs={{0,1},{1,0},{2,3},{3,2},{4,5},{5,4},{6,7},{7,6},{8,9},{9,8},{10,11... | collective-permute-start | bytes 995336 | tf_op jit(solution)/shard_map/ppermute | solution.py:426
  92.1 1.5 %collective-permute-done = f32[72,1152]{1,0:T(8,128)S(1)} collective-permute-done((f32[72,1152]{1,0:T(8,128)}, f32[72,1152]{1,0:T(8,128)S(1)}, u32[]{:S(2)}, u32[]{:S(2)}) %collective-permute-start) | collective-permute-done | bytes 331808 | tf_op jit(solution)/shard_map/ppermute | solution.py:426
  93.6 1.0 add.9
  94.6 0.1 slice_reduce_fusion
  94.7 0.1 slice_select_fusion.1
  94.8 0.6 collective-permute-start.1
  95.4 4.2 %collective-permute-start.2 = (f32[72,128]{1,0:T(8,128)S(1)}, f32[72,128]{1,0:T(8,128)S(1)}, u32[]{:S(2)}, u32[]{:S(2)}) collective-permute-start(f32[72,128]{1,0:T(8,128)S(1)} %get-tuple-element.17), channel_id=1, source_target_pairs={{0,30},{2,0},{4,2},{6,4},{8,6},{10,8},{12,10},{14,12},{16,14},{18,... | collective-permute-start | bytes 110600 | tf_op jit(solution)/shard_map/ppermute | solution.py:426
  99.6 0.9 fusion.1
  100.5 0.4 collective-permute-done.1
  100.9 0.0 collective-permute-done.2
  101.0 0.0 copy-start.1
  101.0 2.4 %collective-permute-start.3 = (f32[16,1152]{1,0:T(8,128)S(1)}, f32[16,1152]{1,0:T(8,128)S(1)}, u32[]{:S(2)}, u32[]{:S(2)}) collective-permute-start(f32[16,1152]{1,0:T(8,128)S(1)} %slice_select_fusion), channel_id=1, source_target_pairs={{1,32},{0,225},{33,64},{32,1},{65,96},{64,33},{97,128},{96,65},{12... | collective-permute-start | bytes 221192 | tf_op jit(solution)/shard_map/ppermute | solution.py:486
  103.4 0.7 compare_convert_fusion.ocean
  104.1 1.3 collective-permute-done.3.other
  105.4 0.0 copy-start.6
  105.4 0.0 copy-done.1
  105.5 0.6 copy-done.6
  106.1 7.8 %basis.1 = (f32[48,1152]{1,0:T(8,128)}, f32[256,128]{1,0:T(8,128)}) custom-call(s32[1]{0:T(128)} %bitcast.side, f32[72,1152]{1,0:T(8,128)} %copy-done.1, f32[16,1152]{1,0:T(8,128)} %copy-done.6, f32[48,1152]{1,0:T(8,128)} %compare_convert_fusion.ocean, f32[48,1152]{1,0:T(8,128)} %get-tuple-element.13.inertia, f32[48,1152]{1,0:T(8,128)} %get-tuple-element.11.east, ...), custom_call_target="tpu_custom_call" | custom-call | tf_op jit(solution)/shard_map/basis/pallas_call | solution.py:357
  113.9 27.3 %all_to_all.15 = f32[256,1,128]{2,1,0:T(1,128)} all-to-all(f32[256,1,128]{2,1,0:T(1,128)} %bitcast.37), channel_id=1, replica_groups=mesh['lat'=8,'lon_0'=4,'lon_1'=4,'obs'=2] {'lat','lon_0','lon_1','obs'}, dimensions={0} | all-to-all | bytes 262144 | tf_op jit(solution)/shard_map/all_to_all | solution.py:490
  141.2 3.4 %solve.1 = (f32[32,1024]{1,0:T(8,128)}, f32[32,1024]{1,0:T(8,128)}) custom-call(f32[256,128]{1,0:T(8,128)} %bitcast.36, f32[48,1152]{1,0:T(8,128)} %get-tuple-element.9.forcing, f32[48,1152]{1,0:T(8,128)} %get-tuple-element.13.inertia, f32[48,1152]{1,0:T(8,128)} %get-tuple-element.11.east, f32[48,1152]{1,0:T(8,128)} %get-tuple-element.10.south), custom_call_target="tpu_custom_call" | custom-call | tf_op jit(solution)/shard_map/solve/pallas_call | solution.py:415
  (14 shorter events, 0.2 us)
Async XLA Ops:
  0.6 21.8 %copy-start.4 = (f32[32,1024]{1,0:T(8,128)S(1)}, f32[32,1024]{1,0:T(8,128)}, u32[]{:S(2)}) copy-start(f32[32,1024]{1,0:T(8,128)} %param.17) | copy-start | bytes 393220
  0.6 21.8 %copy-start.5 = (s32[32,1024]{1,0:T(8,128)S(1)}, s32[32,1024]{1,0:T(8,128)}, u32[]{:S(2)}) copy-start(s32[32,1024]{1,0:T(8,128)} %param.15) | copy-start | bytes 393220
  0.7 21.9 %copy-start.2 = (f32[32,1024]{1,0:T(8,128)S(1)}, f32[32,1024]{1,0:T(8,128)}, u32[]{:S(2)}) copy-start(f32[32,1024]{1,0:T(8,128)} %param.16) | copy-start | bytes 393220
  5.6 35.3 %all-to-all-start.1 = ((f32[128,8,1,128]{3,1,2,0:T(8,128)}), f32[128,8,1,128]{3,1,2,0:T(8,128)S(1)}, u32[]{:S(2)}, u32[]{:S(2)}) async-start(f32[128,8,1,128]{3,1,2,0:T(8,128)} %bitcast.35), calls=%async_computation.1 | async-start | bytes 1048576 | tf_op jit(solution)/shard_map/all_to_all | solution.py:447
  22.5 5.1 %collective-permute-start.4 = (f32[2,32,128]{2,1,0:T(8,128)S(1)}, f32[2,32,128]{2,1,0:T(8,128)S(1)}, u32[]{:S(2)}, u32[]{:S(2)}) collective-permute-start(f32[2,32,128]{2,1,0:T(8,128)S(1)} %get-tuple-element.21), channel_id=1, source_target_pairs={{0,30},{2,0},{4,2},{6,4},{8,6},{10,8},{12,10},{14,12},{16,14},{18,... | collective-permute-start | bytes 98312 | tf_op jit(solution)/shard_map/ppermute | solution.py:426
  26.5 6.6 %collective-permute-start.5 = (f32[2,32,128]{2,1,0:T(8,128)S(1)}, f32[2,32,128]{2,1,0:T(8,128)S(1)}, u32[]{:S(2)}, u32[]{:S(2)}) collective-permute-start(f32[2,32,128]{2,1,0:T(8,128)S(1)} %get-tuple-element.20), channel_id=1, source_target_pairs={{0,2},{2,4},{4,6},{6,8},{8,10},{10,12},{12,14},{14,16},{16,18},{18... | collective-permute-start | bytes 98312 | tf_op jit(solution)/shard_map/ppermute | solution.py:426
  33.2 6.0 %collective-permute-start.7 = (f32[2,8,1152]{2,1,0:T(8,128)S(1)}, f32[2,8,1152]{2,1,0:T(8,128)S(1)}, u32[]{:S(2)}, u32[]{:S(2)}) collective-permute-start(f32[2,8,1152]{2,1,0:T(8,128)S(1)} %get-tuple-element.19), channel_id=1, source_target_pairs={{0,225},{1,0},{32,1},{33,32},{64,33},{65,64},{96,65},{97,96},{128,... | collective-permute-start | bytes 221192 | tf_op jit(solution)/shard_map/ppermute | solution.py:426
  35.8 3.4 %collective-permute-start.6 = (f32[2,8,1152]{2,1,0:T(8,128)S(1)}, f32[2,8,1152]{2,1,0:T(8,128)S(1)}, u32[]{:S(2)}, u32[]{:S(2)}) collective-permute-start(f32[2,8,1152]{2,1,0:T(8,128)S(1)} %get-tuple-element.18), channel_id=1, source_target_pairs={{0,1},{1,32},{32,33},{33,64},{64,65},{65,96},{96,97},{97,128},{128... | collective-permute-start | bytes 221192 | tf_op jit(solution)/shard_map/ppermute | solution.py:426
  40.9 8.9 %copy-start = (f32[128,8,1,128]{3,1,2,0:T(8,128)}, f32[128,8,1,128]{3,1,2,0:T(8,128)S(1)}, u32[]{:S(2)}) copy-start(f32[128,8,1,128]{3,1,2,0:T(8,128)S(1)} %all-to-all-done.1) | copy-start | bytes 1572868
  40.9 34.0 %all-to-all-start = ((f32[128,4,1,128]{3,1,2,0:T(4,128)}), f32[128,4,1,128]{3,1,2,0:T(4,128)S(1)}, u32[]{:S(2)}, u32[]{:S(2)}) async-start(f32[128,4,1,128]{3,1,2,0:T(4,128)} %bitcast.2), calls=%async_computation | async-start | bytes 524288 | tf_op jit(solution)/shard_map/all_to_all | solution.py:447
  74.9 0.7 copy-start.3
  89.9 3.7 %collective-permute-start = (f32[72,1152]{1,0:T(8,128)}, f32[72,1152]{1,0:T(8,128)S(1)}, u32[]{:S(2)}, u32[]{:S(2)}) collective-permute-start(f32[72,1152]{1,0:T(8,128)} %deposit_last.1), channel_id=1, source_target_pairs={{0,1},{1,0},{2,3},{3,2},{4,5},{5,4},{6,7},{7,6},{8,9},{9,8},{10,11... | collective-permute-start | bytes 995336 | tf_op jit(solution)/shard_map/ppermute | solution.py:426
  94.8 6.2 %collective-permute-start.1 = (f32[72,128]{1,0:T(8,128)S(1)}, f32[72,128]{1,0:T(8,128)S(1)}, u32[]{:S(2)}, u32[]{:S(2)}) collective-permute-start(f32[72,128]{1,0:T(8,128)S(1)} %get-tuple-element.16), channel_id=1, source_target_pairs={{0,2},{2,4},{4,6},{6,8},{8,10},{10,12},{12,14},{14,16},{16,18},{18... | collective-permute-start | bytes 110600 | tf_op jit(solution)/shard_map/ppermute | solution.py:426
  95.4 5.6 %collective-permute-start.2 = (f32[72,128]{1,0:T(8,128)S(1)}, f32[72,128]{1,0:T(8,128)S(1)}, u32[]{:S(2)}, u32[]{:S(2)}) collective-permute-start(f32[72,128]{1,0:T(8,128)S(1)} %get-tuple-element.17), channel_id=1, source_target_pairs={{0,30},{2,0},{4,2},{6,4},{8,6},{10,8},{12,10},{14,12},{16,14},{18,... | collective-permute-start | bytes 110600 | tf_op jit(solution)/shard_map/ppermute | solution.py:426
  101.0 4.5 %copy-start.1 = (f32[72,1152]{1,0:T(8,128)}, f32[72,1152]{1,0:T(8,128)S(1)}, u32[]{:S(2)}) copy-start(f32[72,1152]{1,0:T(8,128)S(1)} %pad_maximum_fusion.1.tile) | copy-start | bytes 995332
  101.0 4.4 %collective-permute-start.3 = (f32[16,1152]{1,0:T(8,128)S(1)}, f32[16,1152]{1,0:T(8,128)S(1)}, u32[]{:S(2)}, u32[]{:S(2)}) collective-permute-start(f32[16,1152]{1,0:T(8,128)S(1)} %slice_select_fusion), channel_id=1, source_target_pairs={{1,32},{0,225},{33,64},{32,1},{65,96},{64,33},{97,128},{96,65},{12... | collective-permute-start | bytes 221192 | tf_op jit(solution)/shard_map/ppermute | solution.py:486
  105.4 0.6 copy-start.6

commit v3 on v1

--- a/solution.py
+++ b/solution.py
@@ -16,8 +16,9 @@
 LAT_LON = ("lat", "lon_0", "lon_1")
 F32 = jnp.float32
 BF16 = jnp.bfloat16
-GROUPS = 2
-CHUNK = 8
+GROUPS = 4
+WINDOW = 24
+STEP = 16
 
 
 def vmem():
@@ -67,81 +68,246 @@
     )(owner, count, innovation, error, offset, cell)
 
 
+SORT_8 = (
+    (0, 1), (2, 3), (4, 5), (6, 7), (0, 2), (1, 3), (4, 6), (5, 7), (1, 2), (5, 6),
+    (0, 4), (1, 5), (2, 6), (3, 7), (2, 4), (3, 5), (1, 2), (3, 4), (5, 6),
+)
+CLEAN_8 = (
+    (0, 4), (1, 5), (2, 6), (3, 7), (0, 2), (1, 3), (4, 6), (5, 7), (0, 1), (2, 3), (4, 5), (6, 7),
+)
+
+
+def quotient(x, n):
+    return x >> (n.bit_length() - 1) if n & (n - 1) == 0 else x // n
+
+
+def remainder(x, n):
+    return x & (n - 1) if n & (n - 1) == 0 else x % n
+
+
 def deposit(arrived, tile_rows, tile_cols):
     slots = arrived.shape[0] // WORDS
+    width = tile_cols // GROUPS
+    m_one = GROUPS * WINDOW
+    m_all = 4 * m_one
+    depth = tile_rows + WINDOW - 8
+    filled = -(-slots // 8)
+    regs = 8
+    while regs < filled:
+        regs *= 2
+    total = -(-slots // 8)
     row_pad = (tile_rows + 1 + 7) // 8 * 8
-    m_one = (GROUPS * row_pad + 15) // 16 * 16
-    width = tile_cols // GROUPS
-    m_all = 4 * m_one
-    steps = slots // CHUNK
-    half_m = m_one // 2
-    half_n = width // 2
-
-    def kernel(src, out, left_a, left_b, right_a, right_b, acc):
-        m_index = (lax.broadcasted_iota(jnp.int32, (m_one, 128), 0) - half_m).astype(F32).astype(BF16)
-        n_index = (lax.broadcasted_iota(jnp.int32, (width, 128), 0) - half_n).astype(F32).astype(BF16)
-        n_one = jnp.ones((width, 128), BF16)
-        n_zero = jnp.zeros((width, 128), BF16)
-        m_zero = jnp.zeros((m_one, 128), BF16)
-
-        def spread(x, j, n):
-            row = jnp.broadcast_to(x[j : j + 1, :], (16, 128)).astype(BF16)
-            return jnp.broadcast_to(row[None], (n // 16, 16, 128)).reshape(n, 128)
-
-        def build(chunk, left, right):
-            base = chunk * (CHUNK * WORDS)
-            amount = src[pl.ds(base, CHUNK, stride=WORDS), :]
-            north = src[pl.ds(base + 1, CHUNK, stride=WORDS), :]
-            east = src[pl.ds(base + 2, CHUNK, stride=WORDS), :]
-            cell = src[pl.ds(base + 3, CHUNK, stride=WORDS), :].astype(jnp.int32)
-            row = cell // tile_cols
-            col = cell % tile_cols
-            m_here = ((col // width) * row_pad + row - half_m).astype(F32)
+    index_rows = max(m_one, width)
+    middle = index_rows // 2
+    last_cell = float(tile_rows * tile_cols - 1)
+    parts = regs // 8
+    entries = total * (tile_rows // STEP + 1) + 8
+
+    def kernel(src, out, held, left_a, left_b, right_a, right_b, acc, index, span_v, span_s, at, row_of, room, sem):
+        index[...] = (lax.broadcasted_iota(jnp.int32, index.shape, 0) - middle).astype(F32).astype(BF16)
+        acc[...] = jnp.zeros(acc.shape, F32)
+        sub = lax.broadcasted_iota(jnp.int32, (8, 128), 0)
+
+        def load(p):
+            return [held[w, p] for w in range(WORDS)]
+
+        def store(p, x):
+            for w in range(WORDS):
+                held[w, p] = x[w]
+
+        def ordered(a, b):
+            m = a[3] <= b[3]
+            return (
+                [jnp.where(m, x, y) for x, y in zip(a, b)],
+                [jnp.where(m, y, x) for x, y in zip(a, b)],
+            )
+
+        def network(places, pairs):
+            xs = [load(p) for p in places]
+            for a, b in pairs:
+                xs[a], xs[b] = ordered(xs[a], xs[b])
+            for p, x in zip(places, xs):
+                store(p, x)
+
+        def first(g, carry):
+            xs = []
+            for i in range(8):
+                base = pl.multiple_of((g * 8 + i) * 8 * WORDS, 8 * WORDS)
+                xs.append([src[pl.ds(base + w, 8, stride=WORDS), :] for w in range(WORDS)])
+            for a, b in SORT_8:
+                xs[a], xs[b] = ordered(xs[a], xs[b])
+            for i in range(8):
+                store(g * 8 + i, xs[i])
+            return carry
+
+        lax.fori_loop(0, filled // 8, first, 0)
+        for p in range(filled, regs):
+            for w in range(WORDS):
+                held[w, p] = jnp.full((8, 128), 1.0e9 if w == 3 else 0.0, F32)
+
+        def near(g, carry):
+            network([g * 8 + i for i in range(8)], CLEAN_8)
+            return carry
+
+        def several(pairs):
+            for p, q in pairs:
+                x, y = ordered(load(p), load(q))
+                store(p, x)
+                store(q, y)
+
+        size = 16
+        while size <= regs:
+            h = size // 2
+            several([(t // h * size + t % h, t // h * size + size - 1 - t % h) for t in range(regs // 2)])
+            d = h // 2
+            while d >= 8:
+                several([(t // d * 2 * d + t % d, t // d * 2 * d + t % d + d) for t in range(regs // 2)])
+                d //= 2
+            lax.fori_loop(0, regs // 8, near, 0)
+            size *= 2
+
+        def turned(x, mask):
+            return jnp.take_along_axis(x, sub ^ mask, axis=0, mode="promise_in_bounds")
+
+        for k in range(3):
+            mask = (2 << k) - 1
+            low = (sub & (1 << k)) == 0
+            for p in range(regs // 2):
+                a = load(p)
+                b = [turned(x, mask) for x in load(regs - 1 - p)]
+                m = (a[3] <= b[3]) == low
+                store(p, [jnp.where(m, x, y) for x, y in zip(a, b)])
+                store(regs - 1 - p, [turned(jnp.where(m, y, x), mask) for x, y in zip(a, b)])
+            for bit in range(k - 1, -1, -1):
+                low_bit = (sub & (1 << bit)) == 0
+                for p in range(regs):
+                    a = load(p)
+                    c = [turned(x, 1 << bit) for x in a]
+                    m = jnp.where(low_bit, a[3], c[3]) <= jnp.where(low_bit, c[3], a[3])
+                    store(p, [jnp.where(m, x, y) for x, y in zip(a, c)])
+            d = regs // 2
+            while d >= 8:
+                if d == 32:
+
+                    def far(g, carry):
+                        network([g + 8 * i for i in range(8)], CLEAN_8)
+                        return carry
+
+                    lax.fori_loop(0, 8, far, 0)
+                    d = 4
+                else:
+                    several([(t // d * 2 * d + t % d, t // d * 2 * d + t % d + d) for t in range(regs // 2)])
+                    d //= 2
+            lax.fori_loop(0, regs // 8, near, 0)
+
+        lane = lax.broadcasted_iota(jnp.int32, (8, 128), 1)
+        spans = jnp.zeros((8, 128), jnp.int32)
+        for i in range(parts):
+            low = jnp.min(jnp.minimum(held[3, 8 * i], last_cell), axis=1, keepdims=True)
+            high = jnp.max(jnp.minimum(held[3, 8 * i + 7], last_cell), axis=1, keepdims=True)
+            low = quotient(low.astype(jnp.int32), tile_cols)
+            high = quotient(high.astype(jnp.int32), tile_cols)
+            spans = jnp.where(lane == i, low, jnp.where(lane == 64 + i, high, spans))
+        span_v[...] = spans
+        copy = pltpu.make_async_copy(span_v, span_s, sem)
+        copy.start()
+        copy.wait()
+
+        def plan(c, t):
+            s = c // parts
+            i = c % parts
+            low = span_s[s, i]
+            high = span_s[s, 64 + i]
+
+            def note(t, row, rows):
+                at[t] = c
+                row_of[t] = row
+                room[t] = rows
+
+            def further(x):
+                note(x[1], x[0], STEP)
+                return x[0] + STEP, x[1] + 1
+
+            row, t = lax.while_loop(lambda x: high - x[0] >= WINDOW - 1, further, (low // 8 * 8, t))
+            note(t, row, WINDOW - 1)
+            return t + 1
+
+        count = lax.fori_loop(0, -(-slots // regs) * parts, plan, jnp.int32(0))
+        for e in range(3):
+            at[count + e] = 0
+            row_of[count + e] = 0
+            room[count + e] = 0
+
+        def spread(x, j):
+            pair = jnp.concatenate([x[2 * j : 2 * j + 1], x[2 * j + 1 : 2 * j + 2]], axis=1)
+            return jnp.broadcast_to(pair, (16, 256)).astype(BF16)
+
+        def build(t, left, right):
+            c = at[t]
+            s = c // parts
+            i = c % parts
+            amount, north, east, cell = [held[w, pl.ds(i * 8, 8), s, :] for w in range(WORDS)]
+            cell = cell.astype(jnp.int32)
+            row = quotient(cell, tile_cols) - row_of[t]
+            col = remainder(cell, tile_cols)
+            inside = (row >= 0) & (row < room[t])
+            place = quotient(col, width) * WINDOW + row - middle
+            m_here = jnp.where(inside, place, 8 * index_rows).astype(F32)
             m_next = m_here + 1.0
-            n_here = (col % width - half_n).astype(F32)
+            n_here = (remainder(col, width) - middle).astype(F32)
             pieces = []
             for value in (amount, amount * east):
                 low = value * (1.0 - north)
                 high = value * north
                 low_top = low.astype(BF16).astype(F32)
                 high_top = high.astype(BF16).astype(F32)
-                pieces.append((low_top, high_top))
-                pieces.append((low - low_top, high - high_top))
-            for j in range(CHUNK):
-                at_row = m_index == spread(m_here, j, m_one)
-                at_next = m_index == spread(m_next, j, m_one)
-                for k, (low, high) in enumerate(pieces):
-                    left[k * m_one : (k + 1) * m_one, j * 128 : (j + 1) * 128] = jnp.where(
-                        at_row,
-                        spread(low, j, m_one),
-                        jnp.where(at_next, spread(high, j, m_one), m_zero),
+                pieces += [(low_top, high_top), (low - low_top, high - high_top)]
+            zero = jnp.zeros((16, 256), BF16)
+            one = jnp.ones((16, 256), BF16)
+            for j in range(4):
+                here = spread(m_here, j)
+                after = spread(m_next, j)
+                column = spread(n_here, j)
+                values = [(spread(x, j), spread(y, j)) for x, y in pieces]
+                for q in range(m_one // 16):
+                    own = index[q * 16 : (q + 1) * 16]
+                    at_row = own == here
+                    at_next = own == after
+                    for f, (low, high) in enumerate(values):
+                        left[j, f * m_one + q * 16 : f * m_one + (q + 1) * 16] = jnp.where(
+                            at_row, low, jnp.where(at_next, high, zero)
+                        )
+                for q in range(width // 16):
+                    right[j, q * 16 : (q + 1) * 16] = jnp.where(
+                        index[q * 16 : (q + 1) * 16] == column, one, zero
                     )
-                right[:, j * 128 : (j + 1) * 128] = jnp.where(
-                    n_index == spread(n_here, j, width), n_one, n_zero
-                )
-
-        def add(left, right):
-            acc[...] += lax.dot_general(
-                left[...], right[...], (((1,), (1,)), ((), ())), preferred_element_type=F32
+
+        def joined(ref):
+            return jnp.concatenate([ref[j] for j in range(4)], axis=1)
+
+        def add(t, left, right):
+            row = pl.multiple_of(row_of[t], 8)
+            product = lax.dot_general(
+                joined(left), joined(right), (((1,), (1,)), ((), ())), preferred_element_type=F32
             )
-
-        acc[...] = jnp.zeros((m_all, width), F32)
+            for q in range(4 * GROUPS):
+                acc[q, pl.ds(row, WINDOW), :] += product[q * WINDOW : (q + 1) * WINDOW]
+
         build(0, left_a, right_a)
 
         def turn(i, carry):
             build(2 * i + 1, left_b, right_b)
-            add(left_a, right_a)
-            build(jnp.minimum(2 * i + 2, steps - 1), left_a, right_a)
-            add(left_b, right_b)
+            add(2 * i, left_a, right_a)
+            build(2 * i + 2, left_a, right_a)
+            add(2 * i + 1, left_b, right_b)
             return carry
 
-        lax.fori_loop(0, steps // 2, turn, 0)
+        lax.fori_loop(0, (count + 1) // 2, turn, 0)
         lane = lax.broadcasted_iota(jnp.int32, (row_pad, width), 1)
         before = jnp.zeros((row_pad, 1), F32)
         for g in range(GROUPS):
-            s = g * row_pad
-            whole = acc[s : s + row_pad] + acc[m_one + s : m_one + s + row_pad]
-            part = acc[2 * m_one + s : 2 * m_one + s + row_pad] + acc[3 * m_one + s : 3 * m_one + s + row_pad]
+            whole = acc[g, 0:row_pad] + acc[GROUPS + g, 0:row_pad]
+            part = acc[2 * GROUPS + g, 0:row_pad] + acc[3 * GROUPS + g, 0:row_pad]
             moved = pltpu.roll(part, 1, 1)
             moved = jnp.where(lane == 0, jnp.broadcast_to(before, (row_pad, width)), moved)
             out[:, g * width : (g + 1) * width] = whole - part + moved
@@ -157,11 +323,19 @@
         in_specs=[vmem()],
         out_specs=vmem(),
         scratch_shapes=[
-            pltpu.VMEM((m_all, CHUNK * 128), BF16),
-            pltpu.VMEM((m_all, CHUNK * 128), BF16),
-            pltpu.VMEM((width, CHUNK * 128), BF16),
-            pltpu.VMEM((width, CHUNK * 128), BF16),
-            pltpu.VMEM((m_all, width), F32),
+            pltpu.VMEM((WORDS, regs, 8, 128), F32),
+            pltpu.VMEM((4, m_all, 256), BF16),
+            pltpu.VMEM((4, m_all, 256), BF16),
+            pltpu.VMEM((4, width, 256), BF16),
+            pltpu.VMEM((4, width, 256), BF16),
+            pltpu.VMEM((4 * GROUPS, depth, width), F32),
+            pltpu.VMEM((index_rows, 256), BF16),
+            pltpu.VMEM((8, 128), jnp.int32),
+            pltpu.SMEM((8, 128), jnp.int32),
+            pltpu.SMEM((entries,), jnp.int32),
+            pltpu.SMEM((entries,), jnp.int32),
+            pltpu.SMEM((entries,), jnp.int32),
+            pltpu.SemaphoreType.DMA,
         ],
         name="deposit",
     )(arrived)
@@ -260,7 +434,7 @@
     return a
 
 
-def basis_kernel(side, tile, other, ocean, inertia, east, south, forcing, sums):
+def basis_kernel(side, tile, other, ocean, inertia, east, south, forcing, sums, high, low, cut, tops, lows):
     rows, cols = inertia.shape[0] - 16, inertia.shape[1] - 128
     first = side[0] == 0
     middle = tile[pl.ds(pl.multiple_of(side[0] * rows, 8), rows), :]
@@ -271,23 +445,35 @@
     )
     start = jnp.concatenate([top, middle[0:8] + corner, middle[8:], bottom], axis=0) * ocean[...]
     forcing[...] = start
-    weights = [(w[...], halves(w[...])) for w in (inertia, east, south)]
-    vectors = [(start, jnp.zeros_like(start))]
-    for k in range(ITERS):
-        vectors.append(apply_pair(vectors[-1], *weights))
-    inner = [(h[8 : 8 + rows, :cols], l[8 : 8 + rows, :cols]) for h, l in vectors]
-    cuts = [halves(h) for h, l in inner]
-    lane = lax.broadcasted_iota(jnp.int32, (8, 128), 1)
-    tops, lows = [], []
-    for k in range(MOMENTS):
-        i, j = k // 2, (k + 1) // 2
-        a, b = inner[i], inner[j]
-        p, e = two_prod(a[0], b[0], cuts[i], cuts[j])
-        total = pair_fold((p, e + (a[0] * b[1] + a[1] * b[0])))
-        tops.append(total[0][0:1])
-        lows.append(total[1][0:1])
-    blank = [jnp.zeros((16 - MOMENTS, 128), F32)]
-    pair = (jnp.concatenate(tops + blank, 0), jnp.concatenate(lows + blank, 0))
+    high[...] = start
+    low[...] = jnp.zeros_like(start)
+    fields = (inertia, east, south)
+    for k, w in enumerate(fields):
+        cut[2 * k], cut[2 * k + 1] = halves(w[...])
+    tops[...] = jnp.zeros(tops.shape, F32)
+    lows[...] = jnp.zeros(lows.shape, F32)
+
+    def inner(v):
+        return v[0][8 : 8 + rows, :cols], v[1][8 : 8 + rows, :cols]
+
+    def product(a, b, a_cut, b_cut):
+        p, e = two_prod(a[0], b[0], a_cut, b_cut)
+        return pair_fold((p, e + (a[0] * b[1] + a[1] * b[0])))
+
+    def turn(k, carry):
+        old = (high[...], low[...])
+        weights = [(w[...], (cut[2 * i], cut[2 * i + 1])) for i, w in enumerate(fields)]
+        new = apply_pair(old, *weights)
+        high[...], low[...] = new
+        a, b = inner(old), inner(new)
+        a_cut, b_cut = halves(a[0]), halves(b[0])
+        for place, total in ((2 * k, product(a, a, a_cut, a_cut)), (2 * k + 1, product(a, b, a_cut, b_cut))):
+            tops[pl.ds(place, 1), :] = total[0][0:1]
+            lows[pl.ds(place, 1), :] = total[1][0:1]
+        return carry
+
+    lax.fori_loop(0, ITERS, turn, 0)
+    pair = (tops[...], lows[...])
     for step in (64, 32, 16, 8, 4, 2, 1):
         pair = pair_add(pair, (pltpu.roll(pair[0], step, 1), pltpu.roll(pair[1], step, 1)))
     lane = lax.broadcasted_iota(jnp.int32, (16, 128), 1)
@@ -309,11 +495,18 @@
         ),
         in_specs=[smem()] + [vmem()] * 6,
         out_specs=(vmem(), vmem()),
+        scratch_shapes=[
+            pltpu.VMEM(inertia.shape, F32),
+            pltpu.VMEM(inertia.shape, F32),
+            pltpu.VMEM((6,) + inertia.shape, F32),
+            pltpu.VMEM((16, 128), F32),
+            pltpu.VMEM((16, 128), F32),
+        ],
         name="basis",
     )(side, tile, other, ocean, inertia, east, south)
 
 
-def solve_kernel(sums, forcing, inertia, east, south, field, residual):
+def solve_kernel(sums, forcing, inertia, east, south, field, residual, total, left, heading, coefs):
     rows, cols = field.shape
     s = sums[...]
     pair = (s, jnp.zeros_like(s))
@@ -343,16 +536,24 @@
                 ahead[m] = pair_add(new[m], pair_mul(ratio, ahead[m]))
             right = new
             ratios.append(ratio[0])
-    weights = (inertia[...], east[...], south[...])
-    left = forcing[...]
-    heading = left
-    total = None
     for k in range(ITERS):
-        step = steps[k][0:1, 0:1]
-        total = step * heading if total is None else total + step * heading
-        left = left - step * apply_plain(heading, *weights)
-        if k + 1 < ITERS:
-            heading = left + ratios[k][0:1, 0:1] * heading
+        coefs[k : k + 1, :] = steps[k][0:1]
+        coefs[8 + k : 9 + k, :] = ratios[k][0:1] if k + 1 < ITERS else jnp.zeros((1, 128), F32)
+    left[...] = forcing[...]
+    heading[...] = forcing[...]
+    total[...] = jnp.zeros(total.shape, F32)
+
+    def turn(k, carry):
+        step = coefs[pl.ds(k, 1), 0:1]
+        ratio = coefs[pl.ds(8 + k, 1), 0:1]
+        p = heading[...]
+        total[...] += step * p
+        r = left[...] - step * apply_plain(p, inertia[...], east[...], south[...])
+        left[...] = r
+        heading[...] = r + ratio * p
+        return carry
+
+    lax.fori_loop(0, ITERS, turn, 0)
     field[...] = total[8 : 8 + rows, :cols]
     residual[...] = left[8 : 8 + rows, :cols]
 
@@ -364,6 +565,7 @@
         out_shape=(shape, shape),
         in_specs=[vmem()] * 5,
         out_specs=(vmem(), vmem()),
+        scratch_shapes=[pltpu.VMEM(inertia.shape, F32)] * 3 + [pltpu.VMEM((16, 128), F32)],
         name="solve",
     )(sums, forcing, inertia, east, south)
 

time: 137 us -> 125 us (0.912)
  Pallas kernels: 53.9 us -> 40.7 us
    pallas_call x1, Pallas kernels: 39.2 us -> 24.4 us  [deposit(): pl.pallas_call(kernel, out_shape=jax.ShapeDtypeStruct((row_pad, tile_cols...]
where the time goes in v3:
time: 125 us; the launch traced here: 124 us
  Pallas kernels  40.7 us (33%)
  starting transfers between devices  35.3 us (28%)
  blocking collectives  22.6 us (18%)
  waiting for transfers between devices  17.7 us (14%)
  local copies, waits for them, and re-layouts  3.38 us (3%)
  other arithmetic  2.86 us (2%)
  between operations  1.4 us (1%)
    pallas_call x1, Pallas kernels, deposit(): pl.pallas_call(kernel, out_shape=jax.ShapeDtypeStruct((row_pad, tile_cols...  24.4 us
    all_to_all x1, blocking collectives, body(): lax.all_to_all(sums.reshape(tiles * n_obs, 1, 128), LAT_LON_OBS, split_ax...  22.6 us
    ppermute x7, starting transfers between devices, around(): lax.ppermute(value, axis, [(i, (i + steps) % count) for i in range(count)])  16.2 us
    all_to_all x1, starting transfers between devices, body(): lax.all_to_all(sent.reshape(tiles, CAP * WORDS, 1, 128), LAT_LON, split_a...  16.2 us
    ppermute x7, waiting for transfers between devices, around(): lax.ppermute(value, axis, [(i, (i + steps) % count) for i in range(count)])  12.5 us
    pallas_call x1, Pallas kernels, basis(): pl.pallas_call(basis_kernel, out_shape=(jax.ShapeDtypeStruct(inertia.shap...  8.27 us
    pallas_call x1, Pallas kernels, solve(): pl.pallas_call(solve_kernel, out_shape=(shape, shape), in_specs=[vmem()]...  4.23 us
    all_to_all x1, waiting for transfers between devices, body(): lax.all_to_all(sent.reshape(tiles, CAP * WORDS, 1, 128), LAT_LON, split_a...  3.91 us
  transfers between devices with their start and end apart: 9, of which 7 were waited for; matrix products, arithmetic and copies ran while one was open for 2% of the time, Pallas kernels for 0%

profile of v3, /device:TPU:1, one launch (start us, length us, event | category | flops | bytes accessed | tf_op | source)
XLA Modules:
  0.0 124.1 jit_solution(5153515866537533520)
XLA Ops:
  1.3 3.8 %pack.1 = f32[1536,128]{1,0:T(8,128)} custom-call(s32[1,128]{1,0:T(1,128)} %owner.1, s32[1]{0:T(128)S(6)} %copy.13.count, f32[128,128]{1,0:T(8,128)} %innovation.1, f32[128,128]{1,0:T(8,128)} %error.1, f32[2,128,128]{2,1,0:T(8,128)} %offset.1, s32[128,128]{1,0:T(8,128)} %cell.1), custom_call_target="tpu_custom_call" | custom-call | tf_op jit(solution)/shard_map/pack/pallas_call | solution.py:61
  5.1 0.0 copy-start.3
  5.1 0.0 copy-start.4
  5.1 16.2 %all-to-all-start = ((f32[128,12,1,128]{3,2,1,0:T(1,128)}), f32[128,12,1,128]{3,2,1,0:T(1,128)S(1)}, u32[]{:S(2)}, u32[]{:S(2)}) async-start(f32[128,12,1,128]{3,2,1,0:T(1,128)} %bitcast.25), calls=%async_computation | async-start | bytes 1572864 | tf_op jit(solution)/shard_map/all_to_all | solution.py:595
  21.3 0.0 copy-done.3
  21.3 0.0 copy-done.4
  21.3 0.0 copy-start.2
  21.4 0.9 copy-done.2
  22.3 3.9 %collective-permute-start.4 = (f32[2,32,128]{2,1,0:T(8,128)S(1)}, f32[2,32,128]{2,1,0:T(8,128)S(1)}, u32[]{:S(2)}, u32[]{:S(2)}) collective-permute-start(f32[2,32,128]{2,1,0:T(8,128)S(1)} %get-tuple-element.17), channel_id=1, source_target_pairs={{0,30},{2,0},{4,2},{6,4},{8,6},{10,8},{12,10},{14,12},{16,14},{18,... | collective-permute-start | bytes 98312 | tf_op jit(solution)/shard_map/ppermute | solution.py:575
  26.2 0.0 collective-permute-start.5
  26.2 1.1 collective-permute-done.4
  27.3 5.7 %collective-permute-done.5 = f32[2,32,128]{2,1,0:T(8,128)S(1)} collective-permute-done((f32[2,32,128]{2,1,0:T(8,128)S(1)}, f32[2,32,128]{2,1,0:T(8,128)S(1)}, u32[]{:S(2)}, u32[]{:S(2)}) %collective-permute-start.5) | collective-permute-done | bytes 32800 | tf_op jit(solution)/shard_map/ppermute | solution.py:575
  33.0 2.3 %collective-permute-start.7 = (f32[2,8,1152]{2,1,0:T(8,128)S(1)}, f32[2,8,1152]{2,1,0:T(8,128)S(1)}, u32[]{:S(2)}, u32[]{:S(2)}) collective-permute-start(f32[2,8,1152]{2,1,0:T(8,128)S(1)} %get-tuple-element.15), channel_id=1, source_target_pairs={{0,225},{1,0},{32,1},{33,32},{64,33},{65,64},{96,65},{97,96},{128,... | collective-permute-start | bytes 221192 | tf_op jit(solution)/shard_map/ppermute | solution.py:575
  35.3 1.0 collective-permute-start.6
  36.3 3.8 %collective-permute-done.7 = f32[2,8,1152]{2,1,0:T(8,128)S(1)} collective-permute-done((f32[2,8,1152]{2,1,0:T(8,128)S(1)}, f32[2,8,1152]{2,1,0:T(8,128)S(1)}, u32[]{:S(2)}, u32[]{:S(2)}) %collective-permute-start.7) | collective-permute-done | bytes 73760 | tf_op jit(solution)/shard_map/ppermute | solution.py:575
  40.1 0.0 collective-permute-done.6
  40.2 0.7 slice_bitcast_fusion.2
  40.9 0.1 slice.84
  41.0 3.9 %all-to-all-done = f32[128,12,1,128]{3,2,1,0:T(1,128)S(1)} async-done(((f32[128,12,1,128]{3,2,1,0:T(1,128)}), f32[128,12,1,128]{3,2,1,0:T(1,128)S(1)}, u32[]{:S(2)}, u32[]{:S(2)}) %all-to-all-start) | async-done | bytes 786464 | tf_op jit(solution)/shard_map/all_to_all | solution.py:595
  44.9 0.0 copy-start
  44.9 0.9 copy-done
  45.8 24.4 %deposit.1 = f32[72,1152]{1,0:T(8,128)} custom-call(f32[1536,128]{1,0:T(8,128)} %bitcast.24), custom_call_target="tpu_custom_call" | custom-call | tf_op jit(solution)/shard_map/deposit/pallas_call | solution.py:320
  70.3 4.2 %collective-permute-start = (f32[72,1152]{1,0:T(8,128)}, f32[72,1152]{1,0:T(8,128)S(1)}, u32[]{:S(2)}, u32[]{:S(2)}) collective-permute-start(f32[72,1152]{1,0:T(8,128)} %deposit.1), channel_id=1, source_target_pairs={{0,1},{1,0},{2,3},{3,2},{4,5},{5,4},{6,7},{7,6},{8,9},{9,8},{10,11... | collective-permute-start | bytes 995336 | tf_op jit(solution)/shard_map/ppermute | solution.py:575
  74.5 1.5 %collective-permute-done = f32[72,1152]{1,0:T(8,128)S(1)} collective-permute-done((f32[72,1152]{1,0:T(8,128)}, f32[72,1152]{1,0:T(8,128)S(1)}, u32[]{:S(2)}, u32[]{:S(2)}) %collective-permute-start) | collective-permute-done | bytes 331808 | tf_op jit(solution)/shard_map/ppermute | solution.py:575
  75.9 1.0 add.9
  76.9 0.1 slice_reduce_fusion
  77.1 0.1 slice_select_fusion.1
  77.1 1.7 %collective-permute-start.1 = (f32[72,128]{1,0:T(8,128)S(1)}, f32[72,128]{1,0:T(8,128)S(1)}, u32[]{:S(2)}, u32[]{:S(2)}) collective-permute-start(f32[72,128]{1,0:T(8,128)S(1)} %get-tuple-element.12), channel_id=1, source_target_pairs={{0,2},{2,4},{4,6},{6,8},{8,10},{10,12},{12,14},{14,16},{16,18},{18... | collective-permute-start | bytes 110600 | tf_op jit(solution)/shard_map/ppermute | solution.py:575
  78.8 3.2 %collective-permute-start.2 = (f32[72,128]{1,0:T(8,128)S(1)}, f32[72,128]{1,0:T(8,128)S(1)}, u32[]{:S(2)}, u32[]{:S(2)}) collective-permute-start(f32[72,128]{1,0:T(8,128)S(1)} %get-tuple-element.13), channel_id=1, source_target_pairs={{0,30},{2,0},{4,2},{6,4},{8,6},{10,8},{12,10},{14,12},{16,14},{18,... | collective-permute-start | bytes 110600 | tf_op jit(solution)/shard_map/ppermute | solution.py:575
  82.0 0.9 fusion.1
  82.9 0.4 collective-permute-done.1
  83.3 0.0 collective-permute-done.2
  83.4 0.0 copy-start.1
  83.4 2.9 %collective-permute-start.3 = (f32[16,1152]{1,0:T(8,128)S(1)}, f32[16,1152]{1,0:T(8,128)S(1)}, u32[]{:S(2)}, u32[]{:S(2)}) collective-permute-start(f32[16,1152]{1,0:T(8,128)S(1)} %slice_select_fusion), channel_id=1, source_target_pairs={{1,32},{0,225},{33,64},{32,1},{65,96},{64,33},{97,128},{96,65},{12... | collective-permute-start | bytes 221192 | tf_op jit(solution)/shard_map/ppermute | solution.py:631
  86.3 0.7 compare_convert_fusion.ocean
  87.0 0.0 copy-done.1
  87.0 1.3 %collective-permute-done.3.other = f32[16,1152]{1,0:T(8,128)S(1)} collective-permute-done((f32[16,1152]{1,0:T(8,128)S(1)}, f32[16,1152]{1,0:T(8,128)S(1)}, u32[]{:S(2)}, u32[]{:S(2)}) %collective-permute-start.3) | collective-permute-done | bytes 73760 | tf_op jit(solution)/shard_map/ppermute | solution.py:631
  88.3 0.0 copy-start.5
  88.3 0.6 copy-done.5
  88.9 8.3 %basis.1 = (f32[48,1152]{1,0:T(8,128)}, f32[256,128]{1,0:T(8,128)}) custom-call(s32[1]{0:T(128)} %bitcast.side, f32[72,1152]{1,0:T(8,128)} %copy-done.1, f32[16,1152]{1,0:T(8,128)} %copy-done.5, f32[48,1152]{1,0:T(8,128)} %compare_convert_fusion.ocean, f32[48,1152]{1,0:T(8,128)} %get-tuple-element.9.inertia, f32[48,1152]{1,0:T(8,128)} %get-tuple-element.7.east, ...), custom_call_target="tpu_custom_call" | custom-call | tf_op jit(solution)/shard_map/basis/pallas_call | solution.py:490
  97.2 22.6 %all_to_all.10 = f32[256,1,128]{2,1,0:T(1,128)} all-to-all(f32[256,1,128]{2,1,0:T(1,128)} %bitcast.30), channel_id=1, replica_groups=mesh['lat'=8,'lon_0'=4,'lon_1'=4,'obs'=2] {'lat','lon_0','lon_1','obs'}, dimensions={0} | all-to-all | bytes 262144 | tf_op jit(solution)/shard_map/all_to_all | solution.py:635
  119.8 4.2 %solve.1 = (f32[32,1024]{1,0:T(8,128)}, f32[32,1024]{1,0:T(8,128)}) custom-call(f32[256,128]{1,0:T(8,128)} %bitcast.29, f32[48,1152]{1,0:T(8,128)} %get-tuple-element.5.forcing, f32[48,1152]{1,0:T(8,128)} %get-tuple-element.9.inertia, f32[48,1152]{1,0:T(8,128)} %get-tuple-element.7.east, f32[48,1152]{1,0:T(8,128)} %get-tuple-element.6.south), custom_call_target="tpu_custom_call" | custom-call | tf_op jit(solution)/shard_map/solve/pallas_call | solution.py:563
  (14 shorter events, 0.2 us)
Async XLA Ops:
  5.1 16.2 %copy-start.3 = (f32[32,1024]{1,0:T(8,128)S(1)}, f32[32,1024]{1,0:T(8,128)}, u32[]{:S(2)}) copy-start(f32[32,1024]{1,0:T(8,128)} %param.17) | copy-start | bytes 393220
  5.1 16.2 %copy-start.4 = (s32[32,1024]{1,0:T(8,128)S(1)}, s32[32,1024]{1,0:T(8,128)}, u32[]{:S(2)}) copy-start(s32[32,1024]{1,0:T(8,128)} %param.15) | copy-start | bytes 393220
  5.1 39.8 %all-to-all-start = ((f32[128,12,1,128]{3,2,1,0:T(1,128)}), f32[128,12,1,128]{3,2,1,0:T(1,128)S(1)}, u32[]{:S(2)}, u32[]{:S(2)}) async-start(f32[128,12,1,128]{3,2,1,0:T(1,128)} %bitcast.25), calls=%async_computation | async-start | bytes 1572864 | tf_op jit(solution)/shard_map/all_to_all | solution.py:595
  21.3 0.9 copy-start.2
  22.3 5.0 %collective-permute-start.4 = (f32[2,32,128]{2,1,0:T(8,128)S(1)}, f32[2,32,128]{2,1,0:T(8,128)S(1)}, u32[]{:S(2)}, u32[]{:S(2)}) collective-permute-start(f32[2,32,128]{2,1,0:T(8,128)S(1)} %get-tuple-element.17), channel_id=1, source_target_pairs={{0,30},{2,0},{4,2},{6,4},{8,6},{10,8},{12,10},{14,12},{16,14},{18,... | collective-permute-start | bytes 98312 | tf_op jit(solution)/shard_map/ppermute | solution.py:575
  26.2 6.8 %collective-permute-start.5 = (f32[2,32,128]{2,1,0:T(8,128)S(1)}, f32[2,32,128]{2,1,0:T(8,128)S(1)}, u32[]{:S(2)}, u32[]{:S(2)}) collective-permute-start(f32[2,32,128]{2,1,0:T(8,128)S(1)} %get-tuple-element.16), channel_id=1, source_target_pairs={{0,2},{2,4},{4,6},{6,8},{8,10},{10,12},{12,14},{14,16},{16,18},{18... | collective-permute-start | bytes 98312 | tf_op jit(solution)/shard_map/ppermute | solution.py:575
  33.0 7.2 %collective-permute-start.7 = (f32[2,8,1152]{2,1,0:T(8,128)S(1)}, f32[2,8,1152]{2,1,0:T(8,128)S(1)}, u32[]{:S(2)}, u32[]{:S(2)}) collective-permute-start(f32[2,8,1152]{2,1,0:T(8,128)S(1)} %get-tuple-element.15), channel_id=1, source_target_pairs={{0,225},{1,0},{32,1},{33,32},{64,33},{65,64},{96,65},{97,96},{128,... | collective-permute-start | bytes 221192 | tf_op jit(solution)/shard_map/ppermute | solution.py:575
  35.3 4.8 %collective-permute-start.6 = (f32[2,8,1152]{2,1,0:T(8,128)S(1)}, f32[2,8,1152]{2,1,0:T(8,128)S(1)}, u32[]{:S(2)}, u32[]{:S(2)}) collective-permute-start(f32[2,8,1152]{2,1,0:T(8,128)S(1)} %get-tuple-element.14), channel_id=1, source_target_pairs={{0,1},{1,32},{32,33},{33,64},{64,65},{65,96},{96,97},{97,128},{128... | collective-permute-start | bytes 221192 | tf_op jit(solution)/shard_map/ppermute | solution.py:575
  44.9 0.9 copy-start
  70.3 5.6 %collective-permute-start = (f32[72,1152]{1,0:T(8,128)}, f32[72,1152]{1,0:T(8,128)S(1)}, u32[]{:S(2)}, u32[]{:S(2)}) collective-permute-start(f32[72,1152]{1,0:T(8,128)} %deposit.1), channel_id=1, source_target_pairs={{0,1},{1,0},{2,3},{3,2},{4,5},{5,4},{6,7},{7,6},{8,9},{9,8},{10,11... | collective-permute-start | bytes 995336 | tf_op jit(solution)/shard_map/ppermute | solution.py:575
  77.1 6.2 %collective-permute-start.1 = (f32[72,128]{1,0:T(8,128)S(1)}, f32[72,128]{1,0:T(8,128)S(1)}, u32[]{:S(2)}, u32[]{:S(2)}) collective-permute-start(f32[72,128]{1,0:T(8,128)S(1)} %get-tuple-element.12), channel_id=1, source_target_pairs={{0,2},{2,4},{4,6},{6,8},{8,10},{10,12},{12,14},{14,16},{16,18},{18... | collective-permute-start | bytes 110600 | tf_op jit(solution)/shard_map/ppermute | solution.py:575
  78.8 4.5 %collective-permute-start.2 = (f32[72,128]{1,0:T(8,128)S(1)}, f32[72,128]{1,0:T(8,128)S(1)}, u32[]{:S(2)}, u32[]{:S(2)}) collective-permute-start(f32[72,128]{1,0:T(8,128)S(1)} %get-tuple-element.13), channel_id=1, source_target_pairs={{0,30},{2,0},{4,2},{6,4},{8,6},{10,8},{12,10},{14,12},{16,14},{18,... | collective-permute-start | bytes 110600 | tf_op jit(solution)/shard_map/ppermute | solution.py:575
  83.4 3.6 %copy-start.1 = (f32[72,1152]{1,0:T(8,128)}, f32[72,1152]{1,0:T(8,128)S(1)}, u32[]{:S(2)}) copy-start(f32[72,1152]{1,0:T(8,128)S(1)} %pad_maximum_fusion.1.tile) | copy-start | bytes 995332
  83.4 4.9 %collective-permute-start.3 = (f32[16,1152]{1,0:T(8,128)S(1)}, f32[16,1152]{1,0:T(8,128)S(1)}, u32[]{:S(2)}, u32[]{:S(2)}) collective-permute-start(f32[16,1152]{1,0:T(8,128)S(1)} %slice_select_fusion), channel_id=1, source_target_pairs={{1,32},{0,225},{33,64},{32,1},{65,96},{64,33},{97,128},{96,65},{12... | collective-permute-start | bytes 221192 | tf_op jit(solution)/shard_map/ppermute | solution.py:631
  88.3 0.6 copy-start.5

commit v4 on v3

--- a/solution.py
+++ b/solution.py
@@ -27,6 +27,14 @@
 
 def smem():
     return pl.BlockSpec(memory_space=pltpu.SMEM)
+
+
+def on_chip(*values):
+    return [pltpu.with_memory_space_constraint(v, pltpu.MemorySpace.VMEM) for v in values]
+
+
+def limit(mib):
+    return pltpu.CompilerParams(vmem_limit_bytes=mib * 2**20)
 
 
 def pack_kernel(owner, count, innovation, error, offset, cell, out, rows, seen):
@@ -319,7 +327,8 @@
 
     return pl.pallas_call(
         kernel,
-        out_shape=jax.ShapeDtypeStruct((row_pad, tile_cols + 128), F32),
+        out_shape=pltpu.VMEM((row_pad, tile_cols + 128), F32),
+        compiler_params=limit(24),
         in_specs=[vmem()],
         out_specs=vmem(),
         scratch_shapes=[
@@ -338,7 +347,7 @@
             pltpu.SemaphoreType.DMA,
         ],
         name="deposit",
-    )(arrived)
+    )(*on_chip(arrived))
 
 
 def two_sum(a, b):
@@ -434,7 +443,7 @@
     return a
 
 
-def basis_kernel(side, tile, other, ocean, inertia, east, south, forcing, sums, high, low, cut, tops, lows):
+def basis_kernel(side, tile, other, ocean, inertia, east, south, forcing, sums):
     rows, cols = inertia.shape[0] - 16, inertia.shape[1] - 128
     first = side[0] == 0
     middle = tile[pl.ds(pl.multiple_of(side[0] * rows, 8), rows), :]
@@ -445,35 +454,23 @@
     )
     start = jnp.concatenate([top, middle[0:8] + corner, middle[8:], bottom], axis=0) * ocean[...]
     forcing[...] = start
-    high[...] = start
-    low[...] = jnp.zeros_like(start)
-    fields = (inertia, east, south)
-    for k, w in enumerate(fields):
-        cut[2 * k], cut[2 * k + 1] = halves(w[...])
-    tops[...] = jnp.zeros(tops.shape, F32)
-    lows[...] = jnp.zeros(lows.shape, F32)
-
-    def inner(v):
-        return v[0][8 : 8 + rows, :cols], v[1][8 : 8 + rows, :cols]
-
-    def product(a, b, a_cut, b_cut):
-        p, e = two_prod(a[0], b[0], a_cut, b_cut)
-        return pair_fold((p, e + (a[0] * b[1] + a[1] * b[0])))
-
-    def turn(k, carry):
-        old = (high[...], low[...])
-        weights = [(w[...], (cut[2 * i], cut[2 * i + 1])) for i, w in enumerate(fields)]
-        new = apply_pair(old, *weights)
-        high[...], low[...] = new
-        a, b = inner(old), inner(new)
-        a_cut, b_cut = halves(a[0]), halves(b[0])
-        for place, total in ((2 * k, product(a, a, a_cut, a_cut)), (2 * k + 1, product(a, b, a_cut, b_cut))):
-            tops[pl.ds(place, 1), :] = total[0][0:1]
-            lows[pl.ds(place, 1), :] = total[1][0:1]
-        return carry
-
-    lax.fori_loop(0, ITERS, turn, 0)
-    pair = (tops[...], lows[...])
+    weights = [(w[...], halves(w[...])) for w in (inertia, east, south)]
+    vectors = [(start, jnp.zeros_like(start))]
+    for k in range(ITERS):
+        vectors.append(apply_pair(vectors[-1], *weights))
+    inner = [(h[8 : 8 + rows, :cols], l[8 : 8 + rows, :cols]) for h, l in vectors]
+    cuts = [halves(h) for h, l in inner]
+    lane = lax.broadcasted_iota(jnp.int32, (8, 128), 1)
+    tops, lows = [], []
+    for k in range(MOMENTS):
+        i, j = k // 2, (k + 1) // 2
+        a, b = inner[i], inner[j]
+        p, e = two_prod(a[0], b[0], cuts[i], cuts[j])
+        total = pair_fold((p, e + (a[0] * b[1] + a[1] * b[0])))
+        tops.append(total[0][0:1])
+        lows.append(total[1][0:1])
+    blank = [jnp.zeros((16 - MOMENTS, 128), F32)]
+    pair = (jnp.concatenate(tops + blank, 0), jnp.concatenate(lows + blank, 0))
     for step in (64, 32, 16, 8, 4, 2, 1):
         pair = pair_add(pair, (pltpu.roll(pair[0], step, 1), pltpu.roll(pair[1], step, 1)))
     lane = lax.broadcasted_iota(jnp.int32, (16, 128), 1)
@@ -490,23 +487,17 @@
     return pl.pallas_call(
         basis_kernel,
         out_shape=(
-            jax.ShapeDtypeStruct(inertia.shape, F32),
-            jax.ShapeDtypeStruct((devices, 128), F32),
+            pltpu.VMEM(inertia.shape, F32),
+            pltpu.VMEM((devices, 128), F32),
         ),
+        compiler_params=limit(24),
         in_specs=[smem()] + [vmem()] * 6,
         out_specs=(vmem(), vmem()),
-        scratch_shapes=[
-            pltpu.VMEM(inertia.shape, F32),
-            pltpu.VMEM(inertia.shape, F32),
-            pltpu.VMEM((6,) + inertia.shape, F32),
-            pltpu.VMEM((16, 128), F32),
-            pltpu.VMEM((16, 128), F32),
-        ],
         name="basis",
-    )(side, tile, other, ocean, inertia, east, south)
-
-
-def solve_kernel(sums, forcing, inertia, east, south, field, residual, total, left, heading, coefs):
+    )(side, *on_chip(tile, other, ocean, inertia, east, south))
+
+
+def solve_kernel(sums, forcing, inertia, east, south, field, residual):
     rows, cols = field.shape
     s = sums[...]
     pair = (s, jnp.zeros_like(s))
@@ -536,24 +527,16 @@
                 ahead[m] = pair_add(new[m], pair_mul(ratio, ahead[m]))
             right = new
             ratios.append(ratio[0])
+    weights = (inertia[...], east[...], south[...])
+    left = forcing[...]
+    heading = left
+    total = None
     for k in range(ITERS):
-        coefs[k : k + 1, :] = steps[k][0:1]
-        coefs[8 + k : 9 + k, :] = ratios[k][0:1] if k + 1 < ITERS else jnp.zeros((1, 128), F32)
-    left[...] = forcing[...]
-    heading[...] = forcing[...]
-    total[...] = jnp.zeros(total.shape, F32)
-
-    def turn(k, carry):
-        step = coefs[pl.ds(k, 1), 0:1]
-        ratio = coefs[pl.ds(8 + k, 1), 0:1]
-        p = heading[...]
-        total[...] += step * p
-        r = left[...] - step * apply_plain(p, inertia[...], east[...], south[...])
-        left[...] = r
-        heading[...] = r + ratio * p
-        return carry
-
-    lax.fori_loop(0, ITERS, turn, 0)
+        step = steps[k][0:1, 0:1]
+        total = step * heading if total is None else total + step * heading
+        left = left - step * apply_plain(heading, *weights)
+        if k + 1 < ITERS:
+            heading = left + ratios[k][0:1, 0:1] * heading
     field[...] = total[8 : 8 + rows, :cols]
     residual[...] = left[8 : 8 + rows, :cols]
 
@@ -563,11 +546,11 @@
     return pl.pallas_call(
         solve_kernel,
         out_shape=(shape, shape),
+        compiler_params=limit(16),
         in_specs=[vmem()] * 5,
         out_specs=(vmem(), vmem()),
-        scratch_shapes=[pltpu.VMEM(inertia.shape, F32)] * 3 + [pltpu.VMEM((16, 128), F32)],
         name="solve",
-    )(sums, forcing, inertia, east, south)
+    )(*on_chip(sums, forcing, inertia, east, south))
 
 
 def around(value, axis, steps):

time: 125 us -> 116 us (0.928)
  Pallas kernels: 40.7 us -> 35.8 us
  other arithmetic: 2.86 us -> 0.41 us
  local copies, waits for them, and re-layouts: 3.38 us -> 1.18 us
    pallas_call x3, Pallas kernels: 36.9 us -> 32.1 us  [the longest x1 24 us: deposit(): pl.pallas_call(kernel, out_shape=pltpu.VMEM((row_pad, tile_cols + 128), F...]
    unnamed x12 -> x6, local copies, waits for them, and re-layouts: 2.41 us -> 0.88 us
  transfers between devices with their start and end apart: 9 -> 9, of which waited for: 7 -> 7; matrix products, arithmetic and copies ran while one was open for 2% -> 0% of each run, Pallas kernels for 0% -> 0%
where the time goes in v4:
time: 116 us
  Pallas kernels  35.8 us (31%)
  starting transfers between devices  35.7 us (31%)
  blocking collectives  22.5 us (19%)
  waiting for transfers between devices  18.9 us (16%)
  between operations  1.42 us (1%)
  local copies, waits for them, and re-layouts  1.18 us (1%)
    pallas_call x1, Pallas kernels, deposit(): pl.pallas_call(kernel, out_shape=pltpu.VMEM((row_pad, tile_cols + 128), F...  24 us
    all_to_all x1, blocking collectives, body(): lax.all_to_all(sums.reshape(tiles * n_obs, 1, 128), LAT_LON_OBS, split_ax...  22.5 us
    ppermute x7, starting transfers between devices, around(): lax.ppermute(value, axis, [(i, (i + steps) % count) for i in range(count)])  17.1 us
    all_to_all x1, starting transfers between devices, body(): lax.all_to_all(sent.reshape(tiles, CAP * WORDS, 1, 128), LAT_LON, split_a...  16.3 us
    ppermute x7, waiting for transfers between devices, around(): lax.ppermute(value, axis, [(i, (i + steps) % count) for i in range(count)])  12.6 us
    pallas_call x1, Pallas kernels, basis(): pl.pallas_call(basis_kernel, out_shape=(pltpu.VMEM(inertia.shape, F32), p...  5.91 us
    all_to_all x1, waiting for transfers between devices, body(): lax.all_to_all(sent.reshape(tiles, CAP * WORDS, 1, 128), LAT_LON, split_a...  4.29 us
    pallas_call x1, Pallas kernels, pack(): pl.pallas_call(pack_kernel, out_shape=jax.ShapeDtypeStruct((tiles * CAP *...  3.69 us
  transfers between devices with their start and end apart: 9, of which 7 were waited for; matrix products, arithmetic and copies ran while one was open for 0% of the time, Pallas kernels for 0%

profile of v4, /device:TPU:1, one launch (start us, length us, event | category | flops | bytes accessed | tf_op | source)
XLA Modules:
  0.0 115.9 jit_solution(283557527323973882)
XLA Ops:
  1.3 3.7 %pack.1 = f32[1536,128]{1,0:T(8,128)} custom-call(s32[1,128]{1,0:T(1,128)} %owner.1, s32[1]{0:T(128)S(6)} %copy.13.count, f32[128,128]{1,0:T(8,128)} %innovation.1, f32[128,128]{1,0:T(8,128)} %error.1, f32[2,128,128]{2,1,0:T(8,128)} %offset.1, s32[128,128]{1,0:T(8,128)} %cell.1), custom_call_target="tpu_custom_call" | custom-call | tf_op jit(solution)/shard_map/pack/pallas_call | solution.py:69
  5.0 0.0 copy-start.1
  5.0 0.0 copy-start.2
  5.0 16.3 %all-to-all-start = ((f32[128,12,1,128]{3,2,1,0:T(1,128)}), f32[128,12,1,128]{3,2,1,0:T(1,128)S(1)}, u32[]{:S(2)}, u32[]{:S(2)}) async-start(f32[128,12,1,128]{3,2,1,0:T(1,128)} %bitcast.27), calls=%async_computation | async-start | bytes 1572864 | tf_op jit(solution)/shard_map/all_to_all | solution.py:578
  21.3 0.0 copy-done.1
  21.3 0.0 copy-done.2
  21.3 0.0 copy-start
  21.3 0.9 copy-done
  22.2 3.9 %collective-permute-start.4 = (f32[2,32,128]{2,1,0:T(8,128)S(1)}, f32[2,32,128]{2,1,0:T(8,128)S(1)}, u32[]{:S(2)}, u32[]{:S(2)}) collective-permute-start(f32[2,32,128]{2,1,0:T(8,128)S(1)} %get-tuple-element.17), channel_id=1, source_target_pairs={{0,30},{2,0},{4,2},{6,4},{8,6},{10,8},{12,10},{14,12},{16,14},{18,... | collective-permute-start | bytes 98312 | tf_op jit(solution)/shard_map/ppermute | solution.py:558
  26.1 0.0 collective-permute-start.5
  26.1 1.0 collective-permute-done.4
  27.1 5.7 %collective-permute-done.5 = f32[2,32,128]{2,1,0:T(8,128)S(1)} collective-permute-done((f32[2,32,128]{2,1,0:T(8,128)S(1)}, f32[2,32,128]{2,1,0:T(8,128)S(1)}, u32[]{:S(2)}, u32[]{:S(2)}) %collective-permute-start.5) | collective-permute-done | bytes 32800 | tf_op jit(solution)/shard_map/ppermute | solution.py:558
  32.8 2.4 %collective-permute-start.7 = (f32[2,8,1152]{2,1,0:T(8,128)S(1)}, f32[2,8,1152]{2,1,0:T(8,128)S(1)}, u32[]{:S(2)}, u32[]{:S(2)}) collective-permute-start(f32[2,8,1152]{2,1,0:T(8,128)S(1)} %get-tuple-element.15), channel_id=1, source_target_pairs={{0,225},{1,0},{32,1},{33,32},{64,33},{65,64},{96,65},{97,96},{128,... | collective-permute-start | bytes 221192 | tf_op jit(solution)/shard_map/ppermute | solution.py:558
  35.2 1.4 %collective-permute-start.6 = (f32[2,8,1152]{2,1,0:T(8,128)S(1)}, f32[2,8,1152]{2,1,0:T(8,128)S(1)}, u32[]{:S(2)}, u32[]{:S(2)}) collective-permute-start(f32[2,8,1152]{2,1,0:T(8,128)S(1)} %get-tuple-element.14), channel_id=1, source_target_pairs={{0,1},{1,32},{32,33},{33,64},{64,65},{65,96},{96,97},{97,128},{128... | collective-permute-start | bytes 221192 | tf_op jit(solution)/shard_map/ppermute | solution.py:558
  36.7 3.4 %collective-permute-done.7 = f32[2,8,1152]{2,1,0:T(8,128)S(1)} collective-permute-done((f32[2,8,1152]{2,1,0:T(8,128)S(1)}, f32[2,8,1152]{2,1,0:T(8,128)S(1)}, u32[]{:S(2)}, u32[]{:S(2)}) %collective-permute-start.7) | collective-permute-done | bytes 73760 | tf_op jit(solution)/shard_map/ppermute | solution.py:558
  40.1 0.0 collective-permute-done.6
  40.2 0.1 slice.84
  40.3 4.3 %all-to-all-done = f32[128,12,1,128]{3,2,1,0:T(1,128)S(1)} async-done(((f32[128,12,1,128]{3,2,1,0:T(1,128)}), f32[128,12,1,128]{3,2,1,0:T(1,128)S(1)}, u32[]{:S(2)}, u32[]{:S(2)}) %all-to-all-start) | async-done | bytes 786464 | tf_op jit(solution)/shard_map/all_to_all | solution.py:578
  44.6 24.0 %deposit.1 = f32[72,1152]{1,0:T(8,128)S(1)} custom-call(f32[1536,128]{1,0:T(8,128)S(1)} %bitcast.24), custom_call_target="tpu_custom_call" | custom-call | tf_op jit(solution)/shard_map/deposit/pallas_call | solution.py:328
  68.6 4.6 %collective-permute-start = (f32[72,1152]{1,0:T(8,128)S(1)}, f32[72,1152]{1,0:T(8,128)S(1)}, u32[]{:S(2)}, u32[]{:S(2)}) collective-permute-start(f32[72,1152]{1,0:T(8,128)S(1)} %deposit.1), channel_id=1, source_target_pairs={{0,1},{1,0},{2,3},{3,2},{4,5},{5,4},{6,7},{7,6},{8,9},{9,8},{10,11... | collective-permute-start | bytes 995336 | tf_op jit(solution)/shard_map/ppermute | solution.py:558
  73.2 1.3 %collective-permute-done = f32[72,1152]{1,0:T(8,128)S(1)} collective-permute-done((f32[72,1152]{1,0:T(8,128)S(1)}, f32[72,1152]{1,0:T(8,128)S(1)}, u32[]{:S(2)}, u32[]{:S(2)}) %collective-permute-start) | collective-permute-done | bytes 331808 | tf_op jit(solution)/shard_map/ppermute | solution.py:558
  74.5 0.1 slice_reduce_fusion
  74.7 0.1 slice_select_fusion.1
  74.7 1.1 collective-permute-start.1
  75.8 3.7 %collective-permute-start.2 = (f32[72,128]{1,0:T(8,128)S(1)}, f32[72,128]{1,0:T(8,128)S(1)}, u32[]{:S(2)}, u32[]{:S(2)}) collective-permute-start(f32[72,128]{1,0:T(8,128)S(1)} %get-tuple-element.13), channel_id=1, source_target_pairs={{0,30},{2,0},{4,2},{6,4},{8,6},{10,8},{12,10},{14,12},{16,14},{18,... | collective-permute-start | bytes 110600 | tf_op jit(solution)/shard_map/ppermute | solution.py:558
  79.6 0.1 fusion.1
  79.7 1.2 %collective-permute-done.1 = f32[72,128]{1,0:T(8,128)S(1)} collective-permute-done((f32[72,128]{1,0:T(8,128)S(1)}, f32[72,128]{1,0:T(8,128)S(1)}, u32[]{:S(2)}, u32[]{:S(2)}) %collective-permute-start.1) | collective-permute-done | bytes 36896 | tf_op jit(solution)/shard_map/ppermute | solution.py:558
  80.9 0.0 collective-permute-done.2
  81.0 2.2 %collective-permute-start.3 = (f32[16,1152]{1,0:T(8,128)S(1)}, f32[16,1152]{1,0:T(8,128)S(1)}, u32[]{:S(2)}, u32[]{:S(2)}) collective-permute-start(f32[16,1152]{1,0:T(8,128)S(1)} %slice_select_fusion), channel_id=1, source_target_pairs={{1,32},{0,225},{33,64},{32,1},{65,96},{64,33},{97,128},{96,65},{12... | collective-permute-start | bytes 221192 | tf_op jit(solution)/shard_map/ppermute | solution.py:614
  83.2 2.0 %collective-permute-done.3.other = f32[16,1152]{1,0:T(8,128)S(1)} collective-permute-done((f32[16,1152]{1,0:T(8,128)S(1)}, f32[16,1152]{1,0:T(8,128)S(1)}, u32[]{:S(2)}, u32[]{:S(2)}) %collective-permute-start.3) | collective-permute-done | bytes 73760 | tf_op jit(solution)/shard_map/ppermute | solution.py:614
  85.2 5.9 %basis.1 = (f32[48,1152]{1,0:T(8,128)S(1)}, f32[256,128]{1,0:T(8,128)S(1)}) custom-call(s32[1]{0:T(128)} %bitcast.side, f32[72,1152]{1,0:T(8,128)S(1)} %pad_maximum_fusion.1.tile, f32[16,1152]{1,0:T(8,128)S(1)} %collective-permute-done.3.other, f32[48,1152]{1,0:T(8,128)S(1)} %compare_convert_fusion.ocean, f32[48,1152]{1,0:T(8,128)S(1)} %get-tuple-element.9.inertia, ...), custom_call_target="tpu_custom_call" | custom-call | tf_op jit(solution)/shard_map/basis/pallas_call | solution.py:487
  91.2 22.5 %all_to_all.10 = f32[256,1,128]{2,1,0:T(1,128)S(1)} all-to-all(f32[256,1,128]{2,1,0:T(1,128)S(1)} %bitcast.26), channel_id=1, replica_groups=mesh['lat'=8,'lon_0'=4,'lon_1'=4,'obs'=2] {'lat','lon_0','lon_1','obs'}, dimensions={0} | all-to-all | bytes 262144 | tf_op jit(solution)/shard_map/all_to_all | solution.py:618
  113.7 2.2 %solve.1 = (f32[32,1024]{1,0:T(8,128)}, f32[32,1024]{1,0:T(8,128)}) custom-call(f32[256,128]{1,0:T(8,128)S(1)} %bitcast.25, f32[48,1152]{1,0:T(8,128)S(1)} %get-tuple-element.5.forcing, f32[48,1152]{1,0:T(8,128)S(1)} %get-tuple-element.9.inertia, f32[48,1152]{1,0:T(8,128)S(1)} %get-tuple-element.7.east, f32[48,1152]{1,0:T(8,128)S(1)} %get-tuple-element.6.south), custom_call_target="tpu_custom_call" | custom-call | tf_op jit(solution)/shard_map/solve/pallas_call | solution.py:546
  (17 shorter events, 0.3 us)
Async XLA Ops:
  5.0 16.3 %copy-start.1 = (f32[32,1024]{1,0:T(8,128)S(1)}, f32[32,1024]{1,0:T(8,128)}, u32[]{:S(2)}) copy-start(f32[32,1024]{1,0:T(8,128)} %param.17) | copy-start | bytes 393220
  5.0 16.3 %copy-start.2 = (s32[32,1024]{1,0:T(8,128)S(1)}, s32[32,1024]{1,0:T(8,128)}, u32[]{:S(2)}) copy-start(s32[32,1024]{1,0:T(8,128)} %param.15) | copy-start | bytes 393220
  5.0 39.6 %all-to-all-start = ((f32[128,12,1,128]{3,2,1,0:T(1,128)}), f32[128,12,1,128]{3,2,1,0:T(1,128)S(1)}, u32[]{:S(2)}, u32[]{:S(2)}) async-start(f32[128,12,1,128]{3,2,1,0:T(1,128)} %bitcast.27), calls=%async_computation | async-start | bytes 1572864 | tf_op jit(solution)/shard_map/all_to_all | solution.py:578
  21.3 0.9 copy-start
  22.2 4.9 %collective-permute-start.4 = (f32[2,32,128]{2,1,0:T(8,128)S(1)}, f32[2,32,128]{2,1,0:T(8,128)S(1)}, u32[]{:S(2)}, u32[]{:S(2)}) collective-permute-start(f32[2,32,128]{2,1,0:T(8,128)S(1)} %get-tuple-element.17), channel_id=1, source_target_pairs={{0,30},{2,0},{4,2},{6,4},{8,6},{10,8},{12,10},{14,12},{16,14},{18,... | collective-permute-start | bytes 98312 | tf_op jit(solution)/shard_map/ppermute | solution.py:558
  26.1 6.7 %collective-permute-start.5 = (f32[2,32,128]{2,1,0:T(8,128)S(1)}, f32[2,32,128]{2,1,0:T(8,128)S(1)}, u32[]{:S(2)}, u32[]{:S(2)}) collective-permute-start(f32[2,32,128]{2,1,0:T(8,128)S(1)} %get-tuple-element.16), channel_id=1, source_target_pairs={{0,2},{2,4},{4,6},{6,8},{8,10},{10,12},{12,14},{14,16},{16,18},{18... | collective-permute-start | bytes 98312 | tf_op jit(solution)/shard_map/ppermute | solution.py:558
  32.8 7.2 %collective-permute-start.7 = (f32[2,8,1152]{2,1,0:T(8,128)S(1)}, f32[2,8,1152]{2,1,0:T(8,128)S(1)}, u32[]{:S(2)}, u32[]{:S(2)}) collective-permute-start(f32[2,8,1152]{2,1,0:T(8,128)S(1)} %get-tuple-element.15), channel_id=1, source_target_pairs={{0,225},{1,0},{32,1},{33,32},{64,33},{65,64},{96,65},{97,96},{128,... | collective-permute-start | bytes 221192 | tf_op jit(solution)/shard_map/ppermute | solution.py:558
  35.2 4.9 %collective-permute-start.6 = (f32[2,8,1152]{2,1,0:T(8,128)S(1)}, f32[2,8,1152]{2,1,0:T(8,128)S(1)}, u32[]{:S(2)}, u32[]{:S(2)}) collective-permute-start(f32[2,8,1152]{2,1,0:T(8,128)S(1)} %get-tuple-element.14), channel_id=1, source_target_pairs={{0,1},{1,32},{32,33},{33,64},{64,65},{65,96},{96,97},{97,128},{128... | collective-permute-start | bytes 221192 | tf_op jit(solution)/shard_map/ppermute | solution.py:558
  68.6 5.9 %collective-permute-start = (f32[72,1152]{1,0:T(8,128)S(1)}, f32[72,1152]{1,0:T(8,128)S(1)}, u32[]{:S(2)}, u32[]{:S(2)}) collective-permute-start(f32[72,1152]{1,0:T(8,128)S(1)} %deposit.1), channel_id=1, source_target_pairs={{0,1},{1,0},{2,3},{3,2},{4,5},{5,4},{6,7},{7,6},{8,9},{9,8},{10,11... | collective-permute-start | bytes 995336 | tf_op jit(solution)/shard_map/ppermute | solution.py:558
  74.7 6.2 %collective-permute-start.1 = (f32[72,128]{1,0:T(8,128)S(1)}, f32[72,128]{1,0:T(8,128)S(1)}, u32[]{:S(2)}, u32[]{:S(2)}) collective-permute-start(f32[72,128]{1,0:T(8,128)S(1)} %get-tuple-element.12), channel_id=1, source_target_pairs={{0,2},{2,4},{4,6},{6,8},{8,10},{10,12},{12,14},{14,16},{16,18},{18... | collective-permute-start | bytes 110600 | tf_op jit(solution)/shard_map/ppermute | solution.py:558
  75.8 5.1 %collective-permute-start.2 = (f32[72,128]{1,0:T(8,128)S(1)}, f32[72,128]{1,0:T(8,128)S(1)}, u32[]{:S(2)}, u32[]{:S(2)}) collective-permute-start(f32[72,128]{1,0:T(8,128)S(1)} %get-tuple-element.13), channel_id=1, source_target_pairs={{0,30},{2,0},{4,2},{6,4},{8,6},{10,8},{12,10},{14,12},{16,14},{18,... | collective-permute-start | bytes 110600 | tf_op jit(solution)/shard_map/ppermute | solution.py:558
  81.0 4.3 %collective-permute-start.3 = (f32[16,1152]{1,0:T(8,128)S(1)}, f32[16,1152]{1,0:T(8,128)S(1)}, u32[]{:S(2)}, u32[]{:S(2)}) collective-permute-start(f32[16,1152]{1,0:T(8,128)S(1)} %slice_select_fusion), channel_id=1, source_target_pairs={{1,32},{0,225},{33,64},{32,1},{65,96},{64,33},{97,128},{96,65},{12... | collective-permute-start | bytes 221192 | tf_op jit(solution)/shard_map/ppermute | solution.py:614

commit v5 on v4

--- a/solution.py
+++ b/solution.py
@@ -51,17 +51,21 @@
         seen[tile] = 0
         return carry
 
-    lax.fori_loop(0, tiles, clear, 0)
+    lax.fori_loop(0, tiles, clear, 0, unroll=8)
+
+    live_total = count[0]
 
     def place(block, carry):
+        live = block < live_total
         tile = owner[0, block]
         rank = seen[tile]
-        seen[tile] = rank + 1
-        slot = tile * CAP + rank
-        out[pl.ds(slot * WORDS, WORDS), :] = rows[pl.ds(block * WORDS, WORDS), :]
+        seen[tile] = rank + live.astype(jnp.int32)
+        source = jnp.where(live, block, 0)
+        slot = jnp.where(live, tile * CAP + rank, owner[0, 0] * CAP)
+        out[pl.ds(slot * WORDS, WORDS), :] = rows[pl.ds(source * WORDS, WORDS), :]
         return carry
 
-    lax.fori_loop(0, count[0], place, 0)
+    lax.fori_loop(0, blocks, place, 0, unroll=8)
 
 
 def pack(owner, count, innovation, error, offset, cell, tiles):
@@ -587,13 +591,13 @@
     wide = jnp.concatenate([stacked, jnp.where(lane < 64, from_east, from_west)], axis=2)
     above = around(wide[:, rows - 8 :], LAT_OBS, 1)
     below = around(wide[:, :8], LAT_OBS, -1)
+    part = deposit(arrived, rows * n_obs, cols)
+    tile = part + around(part, "obs", 1)
+    tile, above, below = lax.optimization_barrier((tile, above, below))
     conduct, inertia = jnp.concatenate([above, wide, below], axis=1)
     ocean = (conduct > 0.0).astype(F32)
     east = jnp.sqrt(conduct * jnp.roll(conduct, -1, 1))
     south = jnp.sqrt(conduct * jnp.roll(conduct, -1, 0))
-
-    part = deposit(arrived, rows * n_obs, cols)
-    tile = part + around(part, "obs", 1)
     spill = tile[:, cols:]
     from_west = around(jnp.where(lane == 0, spill[:, :1], tile[:, cols - 128 : cols]), LON, 1)
     from_east = around(tile[:, :128], LON, -1)

time: 116 us -> 120 us (1.034)
  waiting for transfers between devices: 18.9 us -> 26.8 us
  starting transfers between devices: 35.7 us -> 30.4 us
    all_to_all x1, waiting for transfers between devices: 4.29 us -> 11.9 us  [body(): lax.all_to_all(sent.reshape(tiles, CAP * WORDS, 1, 128), LAT_LON, split_a...]
    ppermute x7, starting transfers between devices: 17.1 us -> 12.9 us  [around(): lax.ppermute(value, axis, [(i, (i + steps) % count) for i in range(count)])]
    all_to_all x1, blocking collectives: 22.5 us -> 23.7 us  [body(): lax.all_to_all(sums.reshape(tiles * n_obs, 1, 128), LAT_LON_OBS, split_ax...]
  transfers between devices with their start and end apart: 9 -> 9, of which waited for: 7 -> 8; matrix products, arithmetic and copies ran while one was open for 0% -> 0% of each run, Pallas kernels for 0% -> 0%
where the time goes in v5:
time: 120 us
  Pallas kernels  35.6 us (30%)
  starting transfers between devices  30.4 us (25%)
  waiting for transfers between devices  26.8 us (22%)
  blocking collectives  23.7 us (20%)
  between operations  1.43 us (1%)
    pallas_call x1, Pallas kernels, deposit(): pl.pallas_call(kernel, out_shape=pltpu.VMEM((row_pad, tile_cols + 128), F...  24.7 us
    all_to_all x1, blocking collectives, body(): lax.all_to_all(sums.reshape(tiles * n_obs, 1, 128), LAT_LON_OBS, split_ax...  23.7 us
    all_to_all x1, starting transfers between devices, body(): lax.all_to_all(sent.reshape(tiles, CAP * WORDS, 1, 128), LAT_LON, split_a...  16.5 us
    ppermute x7, starting transfers between devices, around(): lax.ppermute(value, axis, [(i, (i + steps) % count) for i in range(count)])  12.9 us
    ppermute x7, waiting for transfers between devices, around(): lax.ppermute(value, axis, [(i, (i + steps) % count) for i in range(count)])  12 us
    all_to_all x1, waiting for transfers between devices, body(): lax.all_to_all(sent.reshape(tiles, CAP * WORDS, 1, 128), LAT_LON, split_a...  11.9 us
    pallas_call x1, Pallas kernels, basis(): pl.pallas_call(basis_kernel, out_shape=(pltpu.VMEM(inertia.shape, F32), p...  5.95 us
    ppermute x1, waiting for transfers between devices, body(): other = lax.ppermute(outer, LAT_OBS, swap)  2.9 us
  transfers between devices with their start and end apart: 9, of which 8 were waited for; matrix products, arithmetic and copies ran while one was open for 0% of the time, Pallas kernels for 0%

profile of v5, /device:TPU:1, one launch (start us, length us, event | category | flops | bytes accessed | tf_op | source)
XLA Modules:
  0.0 119.6 jit_solution(1053044737786798044)
XLA Ops:
  1.3 2.8 %pack.1 = f32[1536,128]{1,0:T(8,128)} custom-call(s32[1,128]{1,0:T(1,128)} %owner.1, s32[1]{0:T(128)S(6)} %copy.13.count, f32[128,128]{1,0:T(8,128)} %innovation.1, f32[128,128]{1,0:T(8,128)} %error.1, f32[2,128,128]{2,1,0:T(8,128)} %offset.1, s32[128,128]{1,0:T(8,128)} %cell.1), custom_call_target="tpu_custom_call" | custom-call | tf_op jit(solution)/shard_map/pack/pallas_call | solution.py:73
  4.0 0.0 copy-start.1
  4.0 0.0 copy-start.2
  4.0 16.5 %all-to-all-start = ((f32[128,12,1,128]{3,2,1,0:T(1,128)}), f32[128,12,1,128]{3,2,1,0:T(1,128)S(1)}, u32[]{:S(2)}, u32[]{:S(2)}) async-start(f32[128,12,1,128]{3,2,1,0:T(1,128)} %bitcast.27), calls=%async_computation | async-start | bytes 1572864 | tf_op jit(solution)/shard_map/all_to_all | solution.py:582
  20.5 0.0 copy-done.1
  20.5 0.0 copy-done.2
  20.5 0.0 copy-start
  20.6 0.9 copy-done
  21.4 3.9 %collective-permute-start.1 = (f32[2,32,128]{2,1,0:T(8,128)S(1)}, f32[2,32,128]{2,1,0:T(8,128)S(1)}, u32[]{:S(2)}, u32[]{:S(2)}) collective-permute-start(f32[2,32,128]{2,1,0:T(8,128)S(1)} %get-tuple-element.23), channel_id=1, source_target_pairs={{0,30},{2,0},{4,2},{6,4},{8,6},{10,8},{12,10},{14,12},{16,14},{18,... | collective-permute-start | bytes 98312 | tf_op jit(solution)/shard_map/ppermute | solution.py:562
  25.3 0.0 collective-permute-start.2
  25.3 1.0 collective-permute-done.1
  26.4 5.8 %collective-permute-done.2 = f32[2,32,128]{2,1,0:T(8,128)S(1)} collective-permute-done((f32[2,32,128]{2,1,0:T(8,128)S(1)}, f32[2,32,128]{2,1,0:T(8,128)S(1)}, u32[]{:S(2)}, u32[]{:S(2)}) %collective-permute-start.2) | collective-permute-done | bytes 32800 | tf_op jit(solution)/shard_map/ppermute | solution.py:562
  32.2 11.9 %all-to-all-done = f32[128,12,1,128]{3,2,1,0:T(1,128)S(1)} async-done(((f32[128,12,1,128]{3,2,1,0:T(1,128)}), f32[128,12,1,128]{3,2,1,0:T(1,128)S(1)}, u32[]{:S(2)}, u32[]{:S(2)}) %all-to-all-start) | async-done | bytes 786464 | tf_op jit(solution)/shard_map/all_to_all | solution.py:582
  44.1 24.7 %deposit.1 = f32[72,1152]{1,0:T(8,128)S(1)} custom-call(f32[1536,128]{1,0:T(8,128)S(1)} %bitcast.24), custom_call_target="tpu_custom_call" | custom-call | tf_op jit(solution)/shard_map/deposit/pallas_call | solution.py:332
  68.8 3.6 %collective-permute-start = (f32[72,1152]{1,0:T(8,128)S(1)}, f32[72,1152]{1,0:T(8,128)S(1)}, u32[]{:S(2)}, u32[]{:S(2)}) collective-permute-start(f32[72,1152]{1,0:T(8,128)S(1)} %deposit.1), channel_id=1, source_target_pairs={{0,1},{1,0},{2,3},{3,2},{4,5},{5,4},{6,7},{7,6},{8,9},{9,8},{10,11... | collective-permute-start | bytes 995336 | tf_op jit(solution)/shard_map/ppermute | solution.py:562
  72.4 0.6 collective-permute-start.3
  73.0 0.0 collective-permute-start.4
  73.0 0.7 collective-permute-done
  73.7 0.7 collective-permute-done.3
  74.4 2.7 %collective-permute-done.4 = f32[2,8,1152]{2,1,0:T(8,128)S(1)} collective-permute-done((f32[2,8,1152]{2,1,0:T(8,128)S(1)}, f32[2,8,1152]{2,1,0:T(8,128)S(1)}, u32[]{:S(2)}, u32[]{:S(2)}) %collective-permute-start.4) | collective-permute-done | bytes 73760 | tf_op jit(solution)/shard_map/ppermute | solution.py:562
  77.1 0.1 slice.79
  77.3 0.1 slice_reduce_fusion
  77.4 0.1 slice_select_fusion.1
  77.5 0.0 collective-permute-start.5
  77.5 4.8 %collective-permute-start.6 = (f32[72,128]{1,0:T(8,128)S(1)}, f32[72,128]{1,0:T(8,128)S(1)}, u32[]{:S(2)}, u32[]{:S(2)}) collective-permute-start(f32[72,128]{1,0:T(8,128)S(1)} %get-tuple-element.19), channel_id=1, source_target_pairs={{0,30},{2,0},{4,2},{6,4},{8,6},{10,8},{12,10},{14,12},{16,14},{18,... | collective-permute-start | bytes 110600 | tf_op jit(solution)/shard_map/ppermute | solution.py:562
  82.3 0.1 fusion.1
  82.5 1.2 collective-permute-done.5
  83.6 0.0 collective-permute-done.6
  83.7 1.1 collective-permute-start.7
  84.9 2.9 %collective-permute-done.7.other = f32[16,1152]{1,0:T(8,128)S(1)} collective-permute-done((f32[16,1152]{1,0:T(8,128)S(1)}, f32[16,1152]{1,0:T(8,128)S(1)}, u32[]{:S(2)}, u32[]{:S(2)}) %collective-permute-start.7) | collective-permute-done | bytes 73760 | tf_op jit(solution)/shard_map/ppermute | solution.py:618
  87.8 5.9 %basis.1 = (f32[48,1152]{1,0:T(8,128)S(1)}, f32[256,128]{1,0:T(8,128)S(1)}) custom-call(s32[1]{0:T(128)} %bitcast.side, f32[72,1152]{1,0:T(8,128)S(1)} %pad_maximum_fusion.1.tile, f32[16,1152]{1,0:T(8,128)S(1)} %collective-permute-done.7.other, f32[48,1152]{1,0:T(8,128)S(1)} %compare_convert_fusion.ocean, f32[48,1152]{1,0:T(8,128)S(1)} %get-tuple-element.15.inertia, ...), custom_call_target="tpu_custom_call" | custom-call | tf_op jit(solution)/shard_map/basis/pallas_call | solution.py:491
  93.7 23.7 %all_to_all.10 = f32[256,1,128]{2,1,0:T(1,128)S(1)} all-to-all(f32[256,1,128]{2,1,0:T(1,128)S(1)} %bitcast.26), channel_id=1, replica_groups=mesh['lat'=8,'lon_0'=4,'lon_1'=4,'obs'=2] {'lat','lon_0','lon_1','obs'}, dimensions={0} | all-to-all | bytes 262144 | tf_op jit(solution)/shard_map/all_to_all | solution.py:622
  117.5 2.2 %solve.1 = (f32[32,1024]{1,0:T(8,128)}, f32[32,1024]{1,0:T(8,128)}) custom-call(f32[256,128]{1,0:T(8,128)S(1)} %bitcast.25, f32[48,1152]{1,0:T(8,128)S(1)} %get-tuple-element.11.forcing, f32[48,1152]{1,0:T(8,128)S(1)} %get-tuple-element.15.inertia, f32[48,1152]{1,0:T(8,128)S(1)} %get-tuple-element.13.east, f32[48,1152]{1,0:T(8,128)S(1)} %get-tuple-element.12.south), custom_call_target="tpu_custom_call" | custom-call | tf_op jit(solution)/shard_map/solve/pallas_call | solution.py:550
  (17 shorter events, 0.3 us)
Async XLA Ops:
  4.0 16.5 %copy-start.1 = (f32[32,1024]{1,0:T(8,128)S(1)}, f32[32,1024]{1,0:T(8,128)}, u32[]{:S(2)}) copy-start(f32[32,1024]{1,0:T(8,128)} %param.17) | copy-start | bytes 393220
  4.0 16.5 %copy-start.2 = (s32[32,1024]{1,0:T(8,128)S(1)}, s32[32,1024]{1,0:T(8,128)}, u32[]{:S(2)}) copy-start(s32[32,1024]{1,0:T(8,128)} %param.15) | copy-start | bytes 393220
  4.0 40.0 %all-to-all-start = ((f32[128,12,1,128]{3,2,1,0:T(1,128)}), f32[128,12,1,128]{3,2,1,0:T(1,128)S(1)}, u32[]{:S(2)}, u32[]{:S(2)}) async-start(f32[128,12,1,128]{3,2,1,0:T(1,128)} %bitcast.27), calls=%async_computation | async-start | bytes 1572864 | tf_op jit(solution)/shard_map/all_to_all | solution.py:582
  20.5 0.9 copy-start
  21.4 4.9 %collective-permute-start.1 = (f32[2,32,128]{2,1,0:T(8,128)S(1)}, f32[2,32,128]{2,1,0:T(8,128)S(1)}, u32[]{:S(2)}, u32[]{:S(2)}) collective-permute-start(f32[2,32,128]{2,1,0:T(8,128)S(1)} %get-tuple-element.23), channel_id=1, source_target_pairs={{0,30},{2,0},{4,2},{6,4},{8,6},{10,8},{12,10},{14,12},{16,14},{18,... | collective-permute-start | bytes 98312 | tf_op jit(solution)/shard_map/ppermute | solution.py:562
  25.3 6.8 %collective-permute-start.2 = (f32[2,32,128]{2,1,0:T(8,128)S(1)}, f32[2,32,128]{2,1,0:T(8,128)S(1)}, u32[]{:S(2)}, u32[]{:S(2)}) collective-permute-start(f32[2,32,128]{2,1,0:T(8,128)S(1)} %get-tuple-element.22), channel_id=1, source_target_pairs={{0,2},{2,4},{4,6},{6,8},{8,10},{10,12},{12,14},{14,16},{16,18},{18... | collective-permute-start | bytes 98312 | tf_op jit(solution)/shard_map/ppermute | solution.py:562
  68.8 4.8 %collective-permute-start = (f32[72,1152]{1,0:T(8,128)S(1)}, f32[72,1152]{1,0:T(8,128)S(1)}, u32[]{:S(2)}, u32[]{:S(2)}) collective-permute-start(f32[72,1152]{1,0:T(8,128)S(1)} %deposit.1), channel_id=1, source_target_pairs={{0,1},{1,0},{2,3},{3,2},{4,5},{5,4},{6,7},{7,6},{8,9},{9,8},{10,11... | collective-permute-start | bytes 995336 | tf_op jit(solution)/shard_map/ppermute | solution.py:562
  72.4 2.0 %collective-permute-start.3 = (f32[2,8,1152]{2,1,0:T(8,128)S(1)}, f32[2,8,1152]{2,1,0:T(8,128)S(1)}, u32[]{:S(2)}, u32[]{:S(2)}) collective-permute-start(f32[2,8,1152]{2,1,0:T(8,128)S(1)} %get-tuple-element.21), channel_id=1, source_target_pairs={{0,1},{1,32},{32,33},{33,64},{64,65},{65,96},{96,97},{97,128},{128... | collective-permute-start | bytes 221192 | tf_op jit(solution)/shard_map/ppermute | solution.py:562
  73.0 4.1 %collective-permute-start.4 = (f32[2,8,1152]{2,1,0:T(8,128)S(1)}, f32[2,8,1152]{2,1,0:T(8,128)S(1)}, u32[]{:S(2)}, u32[]{:S(2)}) collective-permute-start(f32[2,8,1152]{2,1,0:T(8,128)S(1)} %get-tuple-element.20), channel_id=1, source_target_pairs={{0,225},{1,0},{32,1},{33,32},{64,33},{65,64},{96,65},{97,96},{128,... | collective-permute-start | bytes 221192 | tf_op jit(solution)/shard_map/ppermute | solution.py:562
  77.5 6.2 %collective-permute-start.5 = (f32[72,128]{1,0:T(8,128)S(1)}, f32[72,128]{1,0:T(8,128)S(1)}, u32[]{:S(2)}, u32[]{:S(2)}) collective-permute-start(f32[72,128]{1,0:T(8,128)S(1)} %get-tuple-element.18), channel_id=1, source_target_pairs={{0,2},{2,4},{4,6},{6,8},{8,10},{10,12},{12,14},{14,16},{16,18},{18... | collective-permute-start | bytes 110600 | tf_op jit(solution)/shard_map/ppermute | solution.py:562
  77.5 6.1 %collective-permute-start.6 = (f32[72,128]{1,0:T(8,128)S(1)}, f32[72,128]{1,0:T(8,128)S(1)}, u32[]{:S(2)}, u32[]{:S(2)}) collective-permute-start(f32[72,128]{1,0:T(8,128)S(1)} %get-tuple-element.19), channel_id=1, source_target_pairs={{0,30},{2,0},{4,2},{6,4},{8,6},{10,8},{12,10},{14,12},{16,14},{18,... | collective-permute-start | bytes 110600 | tf_op jit(solution)/shard_map/ppermute | solution.py:562
  83.7 4.0 %collective-permute-start.7 = (f32[16,1152]{1,0:T(8,128)S(1)}, f32[16,1152]{1,0:T(8,128)S(1)}, u32[]{:S(2)}, u32[]{:S(2)}) collective-permute-start(f32[16,1152]{1,0:T(8,128)S(1)} %slice_select_fusion), channel_id=1, source_target_pairs={{1,32},{0,225},{33,64},{32,1},{65,96},{64,33},{97,128},{96,65},{12... | collective-permute-start | bytes 221192 | tf_op jit(solution)/shard_map/ppermute | solution.py:618

commit v6 on v5

--- a/solution.py
+++ b/solution.py
@@ -592,6 +592,7 @@
     above = around(wide[:, rows - 8 :], LAT_OBS, 1)
     below = around(wide[:, :8], LAT_OBS, -1)
     part = deposit(arrived, rows * n_obs, cols)
+    part, above, below = lax.optimization_barrier((part, above, below))
     tile = part + around(part, "obs", 1)
     tile, above, below = lax.optimization_barrier((tile, above, below))
     conduct, inertia = jnp.concatenate([above, wide, below], axis=1)
@@ -599,8 +600,18 @@
     east = jnp.sqrt(conduct * jnp.roll(conduct, -1, 1))
     south = jnp.sqrt(conduct * jnp.roll(conduct, -1, 0))
     spill = tile[:, cols:]
-    from_west = around(jnp.where(lane == 0, spill[:, :1], tile[:, cols - 128 : cols]), LON, 1)
-    from_east = around(tile[:, :128], LON, -1)
+    side = lax.axis_index("obs").astype(jnp.int32)
+    leaving = jnp.where(
+        side == 0, jnp.where(lane == 0, spill[:, :1], tile[:, cols - 128 : cols]), tile[:, :128]
+    )
+    split = []
+    for i in range(n_lon):
+        split.append((2 * i, 2 * ((i + 1) % n_lon)))
+        split.append((2 * i + 1, 2 * ((i - 1) % n_lon) + 1))
+    came = lax.ppermute(leaving, LON + ("obs",), split)
+    swapped = around(came, "obs", 1)
+    from_west = jnp.where(side == 0, came, swapped)
+    from_east = jnp.where(side == 0, swapped, came)
     tile = jnp.concatenate(
         [
             tile[:, :128] + jnp.where(lane == 0, from_west, 0.0),
@@ -609,7 +620,6 @@
         ],
         axis=1,
     )
-    side = lax.axis_index("obs").astype(jnp.int32)
     outer = jnp.where(side == 0, tile[:16], tile[2 * rows - 8 : 2 * rows + 8])
     swap = []
     for i in range(n_lat):

time: 120 us -> 115 us (0.958)
  blocking collectives: 23.7 us -> 19.4 us
  waiting for transfers between devices: 26.8 us -> 23.6 us
  starting transfers between devices: 30.4 us -> 33.2 us
    all_to_all x1, blocking collectives: 23.7 us -> 19.4 us  [body(): lax.all_to_all(sums.reshape(tiles * n_obs, 1, 128), LAT_LON_OBS, split_ax...]
    ppermute x7 -> x6, starting transfers between devices: 12.9 us -> 16.4 us  [around(): lax.ppermute(value, axis, [(i, (i + steps) % count) for i in range(count)])]
    all_to_all x1, waiting for transfers between devices: 11.9 us -> 8.44 us  [body(): lax.all_to_all(sent.reshape(tiles, CAP * WORDS, 1, 128), LAT_LON, split_a...]
    ppermute x7 -> x6, waiting for transfers between devices: 12 us -> 8.78 us  [around(): lax.ppermute(value, axis, [(i, (i + steps) % count) for i in range(count)])]
    ppermute x0 -> x1, waiting for transfers between devices: none -> 2.65 us  [body(): came = lax.ppermute(leaving, LON + ('obs',), split)]
  transfers between devices with their start and end apart: 9 -> 9, of which waited for: 8 -> 7; matrix products, arithmetic and copies ran while one was open for 0% -> 0% of each run, Pallas kernels for 0% -> 22%
where the time goes in v6:
time: 115 us
  Pallas kernels  35.6 us (31%)
  starting transfers between devices  33.2 us (29%)
  waiting for transfers between devices  23.6 us (21%)
  blocking collectives  19.4 us (17%)
  between operations  1.47 us (1%)
  local copies, waits for them, and re-layouts  1.18 us (1%)
    pallas_call x1, Pallas kernels, deposit(): pl.pallas_call(kernel, out_shape=pltpu.VMEM((row_pad, tile_cols + 128), F...  24.7 us
    all_to_all x1, blocking collectives, body(): lax.all_to_all(sums.reshape(tiles * n_obs, 1, 128), LAT_LON_OBS, split_ax...  19.4 us
    all_to_all x1, starting transfers between devices, body(): lax.all_to_all(sent.reshape(tiles, CAP * WORDS, 1, 128), LAT_LON, split_a...  16.5 us
    ppermute x6, starting transfers between devices, around(): lax.ppermute(value, axis, [(i, (i + steps) % count) for i in range(count)])  16.4 us
    ppermute x6, waiting for transfers between devices, around(): lax.ppermute(value, axis, [(i, (i + steps) % count) for i in range(count)])  8.78 us
    all_to_all x1, waiting for transfers between devices, body(): lax.all_to_all(sent.reshape(tiles, CAP * WORDS, 1, 128), LAT_LON, split_a...  8.44 us
    pallas_call x1, Pallas kernels, basis(): pl.pallas_call(basis_kernel, out_shape=(pltpu.VMEM(inertia.shape, F32), p...  5.95 us
    ppermute x1, waiting for transfers between devices, body(): other = lax.ppermute(outer, LAT_OBS, swap)  3.74 us
  transfers between devices with their start and end apart: 9, of which 7 were waited for; matrix products, arithmetic and copies ran while one was open for 0% of the time, Pallas kernels for 22%

profile of v6, /device:TPU:1, one launch (start us, length us, event | category | flops | bytes accessed | tf_op | source)
XLA Modules:
  0.0 115.0 jit_solution(2746232280069124672)
XLA Ops:
  1.3 2.8 %pack.1 = f32[1536,128]{1,0:T(8,128)} custom-call(s32[1,128]{1,0:T(1,128)} %owner.1, s32[1]{0:T(128)S(6)} %copy.13.count, f32[128,128]{1,0:T(8,128)} %innovation.1, f32[128,128]{1,0:T(8,128)} %error.1, f32[2,128,128]{2,1,0:T(8,128)} %offset.1, s32[128,128]{1,0:T(8,128)} %cell.1), custom_call_target="tpu_custom_call" | custom-call | tf_op jit(solution)/shard_map/pack/pallas_call | solution.py:73
  4.0 0.0 copy-start.1
  4.0 0.0 copy-start.2
  4.0 16.5 %all-to-all-start = ((f32[128,12,1,128]{3,2,1,0:T(1,128)}), f32[128,12,1,128]{3,2,1,0:T(1,128)S(1)}, u32[]{:S(2)}, u32[]{:S(2)}) async-start(f32[128,12,1,128]{3,2,1,0:T(1,128)} %bitcast.27), calls=%async_computation | async-start | bytes 1572864 | tf_op jit(solution)/shard_map/all_to_all | solution.py:582
  20.5 0.0 copy-done.1
  20.5 0.0 copy-done.2
  20.5 0.0 copy-start
  20.6 0.9 copy-done
  21.4 3.9 %collective-permute-start = (f32[2,32,128]{2,1,0:T(8,128)S(1)}, f32[2,32,128]{2,1,0:T(8,128)S(1)}, u32[]{:S(2)}, u32[]{:S(2)}) collective-permute-start(f32[2,32,128]{2,1,0:T(8,128)S(1)} %get-tuple-element.27), channel_id=1, source_target_pairs={{0,30},{2,0},{4,2},{6,4},{8,6},{10,8},{12,10},{14,12},{16,14},{18,... | collective-permute-start | bytes 98312 | tf_op jit(solution)/shard_map/ppermute | solution.py:562
  25.3 0.0 collective-permute-start.1
  25.3 1.0 collective-permute-done
  26.4 5.8 %collective-permute-done.1 = f32[2,32,128]{2,1,0:T(8,128)S(1)} collective-permute-done((f32[2,32,128]{2,1,0:T(8,128)S(1)}, f32[2,32,128]{2,1,0:T(8,128)S(1)}, u32[]{:S(2)}, u32[]{:S(2)}) %collective-permute-start.1) | collective-permute-done | bytes 32800 | tf_op jit(solution)/shard_map/ppermute | solution.py:562
  32.2 3.4 %collective-permute-start.2 = (f32[2,8,1152]{2,1,0:T(8,128)S(1)}, f32[2,8,1152]{2,1,0:T(8,128)S(1)}, u32[]{:S(2)}, u32[]{:S(2)}) collective-permute-start(f32[2,8,1152]{2,1,0:T(8,128)S(1)} %get-tuple-element.25), channel_id=1, source_target_pairs={{0,1},{1,32},{32,33},{33,64},{64,65},{65,96},{96,97},{97,128},{128... | collective-permute-start | bytes 221192 | tf_op jit(solution)/shard_map/ppermute | solution.py:562
  35.6 0.0 collective-permute-start.3
  35.6 8.4 %all-to-all-done = f32[128,12,1,128]{3,2,1,0:T(1,128)S(1)} async-done(((f32[128,12,1,128]{3,2,1,0:T(1,128)}), f32[128,12,1,128]{3,2,1,0:T(1,128)S(1)}, u32[]{:S(2)}, u32[]{:S(2)}) %all-to-all-start) | async-done | bytes 786464 | tf_op jit(solution)/shard_map/all_to_all | solution.py:582
  44.0 24.7 %deposit.1 = f32[72,1152]{1,0:T(8,128)S(1)} custom-call(f32[1536,128]{1,0:T(8,128)S(1)} %bitcast.24), custom_call_target="tpu_custom_call" | custom-call | tf_op jit(solution)/shard_map/deposit/pallas_call | solution.py:332
  68.8 0.0 collective-permute-done.2
  68.8 0.0 collective-permute-done.3
  68.8 4.3 %collective-permute-start.4 = (f32[72,1152]{1,0:T(8,128)S(1)}, f32[72,1152]{1,0:T(8,128)S(1)}, u32[]{:S(2)}, u32[]{:S(2)}) collective-permute-start(f32[72,1152]{1,0:T(8,128)S(1)} %deposit.1), channel_id=1, source_target_pairs={{0,1},{1,0},{2,3},{3,2},{4,5},{5,4},{6,7},{7,6},{8,9},{9,8},{10,11... | collective-permute-start | bytes 995336 | tf_op jit(solution)/shard_map/ppermute | solution.py:562
  73.1 1.3 %collective-permute-done.4 = f32[72,1152]{1,0:T(8,128)S(1)} collective-permute-done((f32[72,1152]{1,0:T(8,128)S(1)}, f32[72,1152]{1,0:T(8,128)S(1)}, u32[]{:S(2)}, u32[]{:S(2)}) %collective-permute-start.4) | collective-permute-done | bytes 331808 | tf_op jit(solution)/shard_map/ppermute | solution.py:562
  74.5 0.1 slice_reduce_fusion
  74.6 0.1 select_select_fusion
  74.7 0.1 collective-permute-start.5
  74.8 0.1 slice.79
  74.9 2.6 %collective-permute-done.5 = f32[72,128]{1,0:T(8,128)S(1)} collective-permute-done((f32[72,128]{1,0:T(8,128)S(1)}, f32[72,128]{1,0:T(8,128)S(1)}, u32[]{:S(2)}, u32[]{:S(2)}) %collective-permute-start.5) | collective-permute-done | bytes 36896 | tf_op jit(solution)/shard_map/ppermute | solution.py:611
  77.6 4.8 %collective-permute-start.6 = (f32[72,128]{1,0:T(8,128)S(1)}, f32[72,128]{1,0:T(8,128)S(1)}, u32[]{:S(2)}, u32[]{:S(2)}) collective-permute-start(f32[72,128]{1,0:T(8,128)S(1)} %collective-permute-done.5), channel_id=1, source_target_pairs={{0,1},{1,0},{2,3},{3,2},{4,5},{5,4},{6,7},{7,6},{8,9},{9,8},{10,11... | collective-permute-start | bytes 110600 | tf_op jit(solution)/shard_map/ppermute | solution.py:562
  82.4 0.1 fusion.1
  82.6 0.7 collective-permute-done.6
  83.4 0.3 collective-permute-start.7
  83.7 3.7 %collective-permute-done.7.other = f32[16,1152]{1,0:T(8,128)S(1)} collective-permute-done((f32[16,1152]{1,0:T(8,128)S(1)}, f32[16,1152]{1,0:T(8,128)S(1)}, u32[]{:S(2)}, u32[]{:S(2)}) %collective-permute-start.7) | collective-permute-done | bytes 73760 | tf_op jit(solution)/shard_map/ppermute | solution.py:628
  87.4 5.9 %basis.1 = (f32[48,1152]{1,0:T(8,128)S(1)}, f32[256,128]{1,0:T(8,128)S(1)}) custom-call(s32[1]{0:T(128)} %bitcast.side, f32[72,1152]{1,0:T(8,128)S(1)} %pad_maximum_fusion.1.tile, f32[16,1152]{1,0:T(8,128)S(1)} %collective-permute-done.7.other, f32[48,1152]{1,0:T(8,128)S(1)} %compare_convert_fusion.ocean, f32[48,1152]{1,0:T(8,128)S(1)} %get-tuple-element.21.inertia, ...), custom_call_target="tpu_custom_call" | custom-call | tf_op jit(solution)/shard_map/basis/pallas_call | solution.py:491
  93.4 19.4 %all_to_all.10 = f32[256,1,128]{2,1,0:T(1,128)S(1)} all-to-all(f32[256,1,128]{2,1,0:T(1,128)S(1)} %bitcast.26), channel_id=1, replica_groups=mesh['lat'=8,'lon_0'=4,'lon_1'=4,'obs'=2] {'lat','lon_0','lon_1','obs'}, dimensions={0} | all-to-all | bytes 262144 | tf_op jit(solution)/shard_map/all_to_all | solution.py:632
  112.8 2.2 %solve.1 = (f32[32,1024]{1,0:T(8,128)}, f32[32,1024]{1,0:T(8,128)}) custom-call(f32[256,128]{1,0:T(8,128)S(1)} %bitcast.25, f32[48,1152]{1,0:T(8,128)S(1)} %get-tuple-element.17.forcing, f32[48,1152]{1,0:T(8,128)S(1)} %get-tuple-element.21.inertia, f32[48,1152]{1,0:T(8,128)S(1)} %get-tuple-element.19.east, f32[48,1152]{1,0:T(8,128)S(1)} %get-tuple-element.18.south), custom_call_target="tpu_custom_call" | custom-call | tf_op jit(solution)/shard_map/solve/pallas_call | solution.py:550
  (17 shorter events, 0.3 us)
Async XLA Ops:
  4.0 16.5 %copy-start.1 = (f32[32,1024]{1,0:T(8,128)S(1)}, f32[32,1024]{1,0:T(8,128)}, u32[]{:S(2)}) copy-start(f32[32,1024]{1,0:T(8,128)} %param.17) | copy-start | bytes 393220
  4.0 16.5 %copy-start.2 = (s32[32,1024]{1,0:T(8,128)S(1)}, s32[32,1024]{1,0:T(8,128)}, u32[]{:S(2)}) copy-start(s32[32,1024]{1,0:T(8,128)} %param.15) | copy-start | bytes 393220
  4.0 40.0 %all-to-all-start = ((f32[128,12,1,128]{3,2,1,0:T(1,128)}), f32[128,12,1,128]{3,2,1,0:T(1,128)S(1)}, u32[]{:S(2)}, u32[]{:S(2)}) async-start(f32[128,12,1,128]{3,2,1,0:T(1,128)} %bitcast.27), calls=%async_computation | async-start | bytes 1572864 | tf_op jit(solution)/shard_map/all_to_all | solution.py:582
  20.5 0.9 copy-start
  21.4 4.9 %collective-permute-start = (f32[2,32,128]{2,1,0:T(8,128)S(1)}, f32[2,32,128]{2,1,0:T(8,128)S(1)}, u32[]{:S(2)}, u32[]{:S(2)}) collective-permute-start(f32[2,32,128]{2,1,0:T(8,128)S(1)} %get-tuple-element.27), channel_id=1, source_target_pairs={{0,30},{2,0},{4,2},{6,4},{8,6},{10,8},{12,10},{14,12},{16,14},{18,... | collective-permute-start | bytes 98312 | tf_op jit(solution)/shard_map/ppermute | solution.py:562
  25.3 6.8 %collective-permute-start.1 = (f32[2,32,128]{2,1,0:T(8,128)S(1)}, f32[2,32,128]{2,1,0:T(8,128)S(1)}, u32[]{:S(2)}, u32[]{:S(2)}) collective-permute-start(f32[2,32,128]{2,1,0:T(8,128)S(1)} %get-tuple-element.26), channel_id=1, source_target_pairs={{0,2},{2,4},{4,6},{6,8},{8,10},{10,12},{12,14},{14,16},{16,18},{18... | collective-permute-start | bytes 98312 | tf_op jit(solution)/shard_map/ppermute | solution.py:562
  32.2 36.6 %collective-permute-start.2 = (f32[2,8,1152]{2,1,0:T(8,128)S(1)}, f32[2,8,1152]{2,1,0:T(8,128)S(1)}, u32[]{:S(2)}, u32[]{:S(2)}) collective-permute-start(f32[2,8,1152]{2,1,0:T(8,128)S(1)} %get-tuple-element.25), channel_id=1, source_target_pairs={{0,1},{1,32},{32,33},{33,64},{64,65},{65,96},{96,97},{97,128},{128... | collective-permute-start | bytes 221192 | tf_op jit(solution)/shard_map/ppermute | solution.py:562
  35.6 33.2 %collective-permute-start.3 = (f32[2,8,1152]{2,1,0:T(8,128)S(1)}, f32[2,8,1152]{2,1,0:T(8,128)S(1)}, u32[]{:S(2)}, u32[]{:S(2)}) collective-permute-start(f32[2,8,1152]{2,1,0:T(8,128)S(1)} %get-tuple-element.24), channel_id=1, source_target_pairs={{0,225},{1,0},{32,1},{33,32},{64,33},{65,64},{96,65},{97,96},{128,... | collective-permute-start | bytes 221192 | tf_op jit(solution)/shard_map/ppermute | solution.py:562
  68.8 5.5 %collective-permute-start.4 = (f32[72,1152]{1,0:T(8,128)S(1)}, f32[72,1152]{1,0:T(8,128)S(1)}, u32[]{:S(2)}, u32[]{:S(2)}) collective-permute-start(f32[72,1152]{1,0:T(8,128)S(1)} %deposit.1), channel_id=1, source_target_pairs={{0,1},{1,0},{2,3},{3,2},{4,5},{5,4},{6,7},{7,6},{8,9},{9,8},{10,11... | collective-permute-start | bytes 995336 | tf_op jit(solution)/shard_map/ppermute | solution.py:562
  74.7 2.9 %collective-permute-start.5 = (f32[72,128]{1,0:T(8,128)S(1)}, f32[72,128]{1,0:T(8,128)S(1)}, u32[]{:S(2)}, u32[]{:S(2)}) collective-permute-start(f32[72,128]{1,0:T(8,128)S(1)} %select_select_fusion), channel_id=1, source_target_pairs={{0,2},{1,31},{2,4},{3,1},{4,6},{5,3},{6,8},{7,5},{8,10},{9,7},{10,... | collective-permute-start | bytes 110600 | tf_op jit(solution)/shard_map/ppermute | solution.py:611
  77.6 5.7 %collective-permute-start.6 = (f32[72,128]{1,0:T(8,128)S(1)}, f32[72,128]{1,0:T(8,128)S(1)}, u32[]{:S(2)}, u32[]{:S(2)}) collective-permute-start(f32[72,128]{1,0:T(8,128)S(1)} %collective-permute-done.5), channel_id=1, source_target_pairs={{0,1},{1,0},{2,3},{3,2},{4,5},{5,4},{6,7},{7,6},{8,9},{9,8},{10,11... | collective-permute-start | bytes 110600 | tf_op jit(solution)/shard_map/ppermute | solution.py:562
  83.4 4.0 %collective-permute-start.7 = (f32[16,1152]{1,0:T(8,128)S(1)}, f32[16,1152]{1,0:T(8,128)S(1)}, u32[]{:S(2)}, u32[]{:S(2)}) collective-permute-start(f32[16,1152]{1,0:T(8,128)S(1)} %slice_select_fusion), channel_id=1, source_target_pairs={{1,32},{0,225},{33,64},{32,1},{65,96},{64,33},{97,128},{96,65},{12... | collective-permute-start | bytes 221192 | tf_op jit(solution)/shard_map/ppermute | solution.py:628

commit v7 on v6

--- a/solution.py
+++ b/solution.py
@@ -19,6 +19,7 @@
 GROUPS = 4
 WINDOW = 24
 STEP = 16
+RUN = 32
 
 
 def vmem():
@@ -112,7 +113,8 @@
     index_rows = max(m_one, width)
     middle = index_rows // 2
     last_cell = float(tile_rows * tile_cols - 1)
-    parts = regs // 8
+    parts = regs // RUN
+    pairs = RUN // 2
     entries = total * (tile_rows // STEP + 1) + 8
 
     def kernel(src, out, held, left_a, left_b, right_a, right_b, acc, index, span_v, span_s, at, row_of, room, sem):
@@ -215,8 +217,8 @@
         lane = lax.broadcasted_iota(jnp.int32, (8, 128), 1)
         spans = jnp.zeros((8, 128), jnp.int32)
         for i in range(parts):
-            low = jnp.min(jnp.minimum(held[3, 8 * i], last_cell), axis=1, keepdims=True)
-            high = jnp.max(jnp.minimum(held[3, 8 * i + 7], last_cell), axis=1, keepdims=True)
+            low = jnp.min(jnp.minimum(held[3, RUN * i], last_cell), axis=1, keepdims=True)
+            high = jnp.max(jnp.minimum(held[3, RUN * i + RUN - 1], last_cell), axis=1, keepdims=True)
             low = quotient(low.astype(jnp.int32), tile_cols)
             high = quotient(high.astype(jnp.int32), tile_cols)
             spans = jnp.where(lane == i, low, jnp.where(lane == 64 + i, high, spans))
@@ -258,14 +260,15 @@
             c = at[t]
             s = c // parts
             i = c % parts
-            amount, north, east, cell = [held[w, pl.ds(i * 8, 8), s, :] for w in range(WORDS)]
+            amount, north, east, cell = [
+                held[w, pl.ds(i * RUN, RUN), s, :] for w in range(WORDS)
+            ]
             cell = cell.astype(jnp.int32)
             row = quotient(cell, tile_cols) - row_of[t]
             col = remainder(cell, tile_cols)
             inside = (row >= 0) & (row < room[t])
             place = quotient(col, width) * WINDOW + row - middle
             m_here = jnp.where(inside, place, 8 * index_rows).astype(F32)
-            m_next = m_here + 1.0
             n_here = (remainder(col, width) - middle).astype(F32)
             pieces = []
             for value in (amount, amount * east):
@@ -276,18 +279,18 @@
                 pieces += [(low_top, high_top), (low - low_top, high - high_top)]
             zero = jnp.zeros((16, 256), BF16)
             one = jnp.ones((16, 256), BF16)
-            for j in range(4):
+            for j in range(pairs):
                 here = spread(m_here, j)
-                after = spread(m_next, j)
+                after = here + one
                 column = spread(n_here, j)
                 values = [(spread(x, j), spread(y, j)) for x, y in pieces]
                 for q in range(m_one // 16):
                     own = index[q * 16 : (q + 1) * 16]
-                    at_row = own == here
-                    at_next = own == after
+                    at_row = jnp.where(own == here, one, zero)
+                    at_next = jnp.where(own == after, one, zero)
                     for f, (low, high) in enumerate(values):
-                        left[j, f * m_one + q * 16 : f * m_one + (q + 1) * 16] = jnp.where(
-                            at_row, low, jnp.where(at_next, high, zero)
+                        left[j, f * m_one + q * 16 : f * m_one + (q + 1) * 16] = (
+                            at_row * low + at_next * high
                         )
                 for q in range(width // 16):
                     right[j, q * 16 : (q + 1) * 16] = jnp.where(
@@ -295,7 +298,7 @@
                     )
 
         def joined(ref):
-            return jnp.concatenate([ref[j] for j in range(4)], axis=1)
+            return jnp.concatenate([ref[j] for j in range(pairs)], axis=1)
 
         def add(t, left, right):
             row = pl.multiple_of(row_of[t], 8)
@@ -332,15 +335,15 @@
     return pl.pallas_call(
         kernel,
         out_shape=pltpu.VMEM((row_pad, tile_cols + 128), F32),
-        compiler_params=limit(24),
+        compiler_params=limit(32),
         in_specs=[vmem()],
         out_specs=vmem(),
         scratch_shapes=[
             pltpu.VMEM((WORDS, regs, 8, 128), F32),
-            pltpu.VMEM((4, m_all, 256), BF16),
-            pltpu.VMEM((4, m_all, 256), BF16),
-            pltpu.VMEM((4, width, 256), BF16),
-            pltpu.VMEM((4, width, 256), BF16),
+            pltpu.VMEM((pairs, m_all, 256), BF16),
+            pltpu.VMEM((pairs, m_all, 256), BF16),
+            pltpu.VMEM((pairs, width, 256), BF16),
+            pltpu.VMEM((pairs, width, 256), BF16),
             pltpu.VMEM((4 * GROUPS, depth, width), F32),
             pltpu.VMEM((index_rows, 256), BF16),
             pltpu.VMEM((8, 128), jnp.int32),

time: 115 us -> 113 us (0.983)
  Pallas kernels: 35.6 us -> 33 us
    pallas_call x1, Pallas kernels: 24.7 us -> 22.1 us  [deposit(): pl.pallas_call(kernel, out_shape=pltpu.VMEM((row_pad, tile_cols + 128), F...]
  transfers between devices with their start and end apart: 9 -> 9, of which waited for: 7 -> 7; matrix products, arithmetic and copies ran while one was open for 0% -> 0% of each run, Pallas kernels for 22% -> 20%
where the time goes in v7:
time: 113 us; the launch traced here: 112 us
  starting transfers between devices  33.4 us (30%)
  Pallas kernels  33 us (29%)
  waiting for transfers between devices  23.4 us (21%)
  blocking collectives  19.4 us (17%)
  between operations  1.46 us (1%)
  local copies, waits for them, and re-layouts  1.18 us (1%)
    pallas_call x1, Pallas kernels, deposit(): pl.pallas_call(kernel, out_shape=pltpu.VMEM((row_pad, tile_cols + 128), F...  22.1 us
    all_to_all x1, blocking collectives, body(): lax.all_to_all(sums.reshape(tiles * n_obs, 1, 128), LAT_LON_OBS, split_ax...  19.4 us
    all_to_all x1, starting transfers between devices, body(): lax.all_to_all(sent.reshape(tiles, CAP * WORDS, 1, 128), LAT_LON, split_a...  16.5 us
    ppermute x6, starting transfers between devices, around(): lax.ppermute(value, axis, [(i, (i + steps) % count) for i in range(count)])  16.4 us
    ppermute x6, waiting for transfers between devices, around(): lax.ppermute(value, axis, [(i, (i + steps) % count) for i in range(count)])  8.78 us
    all_to_all x1, waiting for transfers between devices, body(): lax.all_to_all(sent.reshape(tiles, CAP * WORDS, 1, 128), LAT_LON, split_a...  8.44 us
    pallas_call x1, Pallas kernels, basis(): pl.pallas_call(basis_kernel, out_shape=(pltpu.VMEM(inertia.shape, F32), p...  5.95 us
    ppermute x1, waiting for transfers between devices, body(): other = lax.ppermute(outer, LAT_OBS, swap)  3.53 us
  transfers between devices with their start and end apart: 9, of which 7 were waited for; matrix products, arithmetic and copies ran while one was open for 0% of the time, Pallas kernels for 20%

profile of v7, /device:TPU:1, one launch (start us, length us, event | category | flops | bytes accessed | tf_op | source)
XLA Modules:
  0.0 112.3 jit_solution(1788204327149921496)
XLA Ops:
  1.3 2.8 %pack.1 = f32[1536,128]{1,0:T(8,128)} custom-call(s32[1,128]{1,0:T(1,128)} %owner.1, s32[1]{0:T(128)S(6)} %copy.13.count, f32[128,128]{1,0:T(8,128)} %innovation.1, f32[128,128]{1,0:T(8,128)} %error.1, f32[2,128,128]{2,1,0:T(8,128)} %offset.1, s32[128,128]{1,0:T(8,128)} %cell.1), custom_call_target="tpu_custom_call" | custom-call | tf_op jit(solution)/shard_map/pack/pallas_call | solution.py:74
  4.0 0.0 copy-start.1
  4.0 0.0 copy-start.2
  4.0 16.5 %all-to-all-start = ((f32[128,12,1,128]{3,2,1,0:T(1,128)}), f32[128,12,1,128]{3,2,1,0:T(1,128)S(1)}, u32[]{:S(2)}, u32[]{:S(2)}) async-start(f32[128,12,1,128]{3,2,1,0:T(1,128)} %bitcast.27), calls=%async_computation | async-start | bytes 1572864 | tf_op jit(solution)/shard_map/all_to_all | solution.py:585
  20.5 0.0 copy-done.1
  20.5 0.0 copy-done.2
  20.5 0.0 copy-start
  20.6 0.9 copy-done
  21.4 3.9 %collective-permute-start = (f32[2,32,128]{2,1,0:T(8,128)S(1)}, f32[2,32,128]{2,1,0:T(8,128)S(1)}, u32[]{:S(2)}, u32[]{:S(2)}) collective-permute-start(f32[2,32,128]{2,1,0:T(8,128)S(1)} %get-tuple-element.27), channel_id=1, source_target_pairs={{0,30},{2,0},{4,2},{6,4},{8,6},{10,8},{12,10},{14,12},{16,14},{18,... | collective-permute-start | bytes 98312 | tf_op jit(solution)/shard_map/ppermute | solution.py:565
  25.3 0.0 collective-permute-start.1
  25.3 1.0 collective-permute-done
  26.4 5.8 %collective-permute-done.1 = f32[2,32,128]{2,1,0:T(8,128)S(1)} collective-permute-done((f32[2,32,128]{2,1,0:T(8,128)S(1)}, f32[2,32,128]{2,1,0:T(8,128)S(1)}, u32[]{:S(2)}, u32[]{:S(2)}) %collective-permute-start.1) | collective-permute-done | bytes 32800 | tf_op jit(solution)/shard_map/ppermute | solution.py:565
  32.2 3.4 %collective-permute-start.2 = (f32[2,8,1152]{2,1,0:T(8,128)S(1)}, f32[2,8,1152]{2,1,0:T(8,128)S(1)}, u32[]{:S(2)}, u32[]{:S(2)}) collective-permute-start(f32[2,8,1152]{2,1,0:T(8,128)S(1)} %get-tuple-element.25), channel_id=1, source_target_pairs={{0,1},{1,32},{32,33},{33,64},{64,65},{65,96},{96,97},{97,128},{128... | collective-permute-start | bytes 221192 | tf_op jit(solution)/shard_map/ppermute | solution.py:565
  35.6 0.0 collective-permute-start.3
  35.6 8.4 %all-to-all-done = f32[128,12,1,128]{3,2,1,0:T(1,128)S(1)} async-done(((f32[128,12,1,128]{3,2,1,0:T(1,128)}), f32[128,12,1,128]{3,2,1,0:T(1,128)S(1)}, u32[]{:S(2)}, u32[]{:S(2)}) %all-to-all-start) | async-done | bytes 786464 | tf_op jit(solution)/shard_map/all_to_all | solution.py:585
  44.0 22.1 %deposit.1 = f32[72,1152]{1,0:T(8,128)S(1)} custom-call(f32[1536,128]{1,0:T(8,128)S(1)} %bitcast.24), custom_call_target="tpu_custom_call" | custom-call | tf_op jit(solution)/shard_map/deposit/pallas_call | solution.py:335
  66.2 0.0 collective-permute-done.2
  66.2 0.0 collective-permute-done.3
  66.2 4.3 %collective-permute-start.4 = (f32[72,1152]{1,0:T(8,128)S(1)}, f32[72,1152]{1,0:T(8,128)S(1)}, u32[]{:S(2)}, u32[]{:S(2)}) collective-permute-start(f32[72,1152]{1,0:T(8,128)S(1)} %deposit.1), channel_id=1, source_target_pairs={{0,1},{1,0},{2,3},{3,2},{4,5},{5,4},{6,7},{7,6},{8,9},{9,8},{10,11... | collective-permute-start | bytes 995336 | tf_op jit(solution)/shard_map/ppermute | solution.py:565
  70.4 1.3 %collective-permute-done.4 = f32[72,1152]{1,0:T(8,128)S(1)} collective-permute-done((f32[72,1152]{1,0:T(8,128)S(1)}, f32[72,1152]{1,0:T(8,128)S(1)}, u32[]{:S(2)}, u32[]{:S(2)}) %collective-permute-start.4) | collective-permute-done | bytes 331808 | tf_op jit(solution)/shard_map/ppermute | solution.py:565
  71.8 0.1 slice_reduce_fusion
  72.0 0.1 select_select_fusion
  72.1 0.1 collective-permute-start.5
  72.2 0.1 slice.79
  72.3 2.6 %collective-permute-done.5 = f32[72,128]{1,0:T(8,128)S(1)} collective-permute-done((f32[72,128]{1,0:T(8,128)S(1)}, f32[72,128]{1,0:T(8,128)S(1)}, u32[]{:S(2)}, u32[]{:S(2)}) %collective-permute-start.5) | collective-permute-done | bytes 36896 | tf_op jit(solution)/shard_map/ppermute | solution.py:614
  74.9 4.8 %collective-permute-start.6 = (f32[72,128]{1,0:T(8,128)S(1)}, f32[72,128]{1,0:T(8,128)S(1)}, u32[]{:S(2)}, u32[]{:S(2)}) collective-permute-start(f32[72,128]{1,0:T(8,128)S(1)} %collective-permute-done.5), channel_id=1, source_target_pairs={{0,1},{1,0},{2,3},{3,2},{4,5},{5,4},{6,7},{7,6},{8,9},{9,8},{10,11... | collective-permute-start | bytes 110600 | tf_op jit(solution)/shard_map/ppermute | solution.py:565
  79.8 0.1 fusion.1
  80.0 0.7 collective-permute-done.6
  80.7 0.5 collective-permute-start.7
  81.2 3.5 %collective-permute-done.7.other = f32[16,1152]{1,0:T(8,128)S(1)} collective-permute-done((f32[16,1152]{1,0:T(8,128)S(1)}, f32[16,1152]{1,0:T(8,128)S(1)}, u32[]{:S(2)}, u32[]{:S(2)}) %collective-permute-start.7) | collective-permute-done | bytes 73760 | tf_op jit(solution)/shard_map/ppermute | solution.py:631
  84.8 5.9 %basis.1 = (f32[48,1152]{1,0:T(8,128)S(1)}, f32[256,128]{1,0:T(8,128)S(1)}) custom-call(s32[1]{0:T(128)} %bitcast.side, f32[72,1152]{1,0:T(8,128)S(1)} %pad_maximum_fusion.1.tile, f32[16,1152]{1,0:T(8,128)S(1)} %collective-permute-done.7.other, f32[48,1152]{1,0:T(8,128)S(1)} %compare_convert_fusion.ocean, f32[48,1152]{1,0:T(8,128)S(1)} %get-tuple-element.21.inertia, ...), custom_call_target="tpu_custom_call" | custom-call | tf_op jit(solution)/shard_map/basis/pallas_call | solution.py:494
  90.7 19.4 %all_to_all.10 = f32[256,1,128]{2,1,0:T(1,128)S(1)} all-to-all(f32[256,1,128]{2,1,0:T(1,128)S(1)} %bitcast.26), channel_id=1, replica_groups=mesh['lat'=8,'lon_0'=4,'lon_1'=4,'obs'=2] {'lat','lon_0','lon_1','obs'}, dimensions={0} | all-to-all | bytes 262144 | tf_op jit(solution)/shard_map/all_to_all | solution.py:635
  110.1 2.2 %solve.1 = (f32[32,1024]{1,0:T(8,128)}, f32[32,1024]{1,0:T(8,128)}) custom-call(f32[256,128]{1,0:T(8,128)S(1)} %bitcast.25, f32[48,1152]{1,0:T(8,128)S(1)} %get-tuple-element.17.forcing, f32[48,1152]{1,0:T(8,128)S(1)} %get-tuple-element.21.inertia, f32[48,1152]{1,0:T(8,128)S(1)} %get-tuple-element.19.east, f32[48,1152]{1,0:T(8,128)S(1)} %get-tuple-element.18.south), custom_call_target="tpu_custom_call" | custom-call | tf_op jit(solution)/shard_map/solve/pallas_call | solution.py:553
  (17 shorter events, 0.3 us)
Async XLA Ops:
  4.0 16.5 %copy-start.1 = (f32[32,1024]{1,0:T(8,128)S(1)}, f32[32,1024]{1,0:T(8,128)}, u32[]{:S(2)}) copy-start(f32[32,1024]{1,0:T(8,128)} %param.17) | copy-start | bytes 393220
  4.0 16.5 %copy-start.2 = (s32[32,1024]{1,0:T(8,128)S(1)}, s32[32,1024]{1,0:T(8,128)}, u32[]{:S(2)}) copy-start(s32[32,1024]{1,0:T(8,128)} %param.15) | copy-start | bytes 393220
  4.0 40.0 %all-to-all-start = ((f32[128,12,1,128]{3,2,1,0:T(1,128)}), f32[128,12,1,128]{3,2,1,0:T(1,128)S(1)}, u32[]{:S(2)}, u32[]{:S(2)}) async-start(f32[128,12,1,128]{3,2,1,0:T(1,128)} %bitcast.27), calls=%async_computation | async-start | bytes 1572864 | tf_op jit(solution)/shard_map/all_to_all | solution.py:585
  20.5 0.9 copy-start
  21.4 4.9 %collective-permute-start = (f32[2,32,128]{2,1,0:T(8,128)S(1)}, f32[2,32,128]{2,1,0:T(8,128)S(1)}, u32[]{:S(2)}, u32[]{:S(2)}) collective-permute-start(f32[2,32,128]{2,1,0:T(8,128)S(1)} %get-tuple-element.27), channel_id=1, source_target_pairs={{0,30},{2,0},{4,2},{6,4},{8,6},{10,8},{12,10},{14,12},{16,14},{18,... | collective-permute-start | bytes 98312 | tf_op jit(solution)/shard_map/ppermute | solution.py:565
  25.3 6.8 %collective-permute-start.1 = (f32[2,32,128]{2,1,0:T(8,128)S(1)}, f32[2,32,128]{2,1,0:T(8,128)S(1)}, u32[]{:S(2)}, u32[]{:S(2)}) collective-permute-start(f32[2,32,128]{2,1,0:T(8,128)S(1)} %get-tuple-element.26), channel_id=1, source_target_pairs={{0,2},{2,4},{4,6},{6,8},{8,10},{10,12},{12,14},{14,16},{16,18},{18... | collective-permute-start | bytes 98312 | tf_op jit(solution)/shard_map/ppermute | solution.py:565
  32.2 34.0 %collective-permute-start.2 = (f32[2,8,1152]{2,1,0:T(8,128)S(1)}, f32[2,8,1152]{2,1,0:T(8,128)S(1)}, u32[]{:S(2)}, u32[]{:S(2)}) collective-permute-start(f32[2,8,1152]{2,1,0:T(8,128)S(1)} %get-tuple-element.25), channel_id=1, source_target_pairs={{0,1},{1,32},{32,33},{33,64},{64,65},{65,96},{96,97},{97,128},{128... | collective-permute-start | bytes 221192 | tf_op jit(solution)/shard_map/ppermute | solution.py:565
  35.6 30.6 %collective-permute-start.3 = (f32[2,8,1152]{2,1,0:T(8,128)S(1)}, f32[2,8,1152]{2,1,0:T(8,128)S(1)}, u32[]{:S(2)}, u32[]{:S(2)}) collective-permute-start(f32[2,8,1152]{2,1,0:T(8,128)S(1)} %get-tuple-element.24), channel_id=1, source_target_pairs={{0,225},{1,0},{32,1},{33,32},{64,33},{65,64},{96,65},{97,96},{128,... | collective-permute-start | bytes 221192 | tf_op jit(solution)/shard_map/ppermute | solution.py:565
  66.2 5.5 %collective-permute-start.4 = (f32[72,1152]{1,0:T(8,128)S(1)}, f32[72,1152]{1,0:T(8,128)S(1)}, u32[]{:S(2)}, u32[]{:S(2)}) collective-permute-start(f32[72,1152]{1,0:T(8,128)S(1)} %deposit.1), channel_id=1, source_target_pairs={{0,1},{1,0},{2,3},{3,2},{4,5},{5,4},{6,7},{7,6},{8,9},{9,8},{10,11... | collective-permute-start | bytes 995336 | tf_op jit(solution)/shard_map/ppermute | solution.py:565
  72.1 2.9 %collective-permute-start.5 = (f32[72,128]{1,0:T(8,128)S(1)}, f32[72,128]{1,0:T(8,128)S(1)}, u32[]{:S(2)}, u32[]{:S(2)}) collective-permute-start(f32[72,128]{1,0:T(8,128)S(1)} %select_select_fusion), channel_id=1, source_target_pairs={{0,2},{1,31},{2,4},{3,1},{4,6},{5,3},{6,8},{7,5},{8,10},{9,7},{10,... | collective-permute-start | bytes 110600 | tf_op jit(solution)/shard_map/ppermute | solution.py:614
  74.9 5.7 %collective-permute-start.6 = (f32[72,128]{1,0:T(8,128)S(1)}, f32[72,128]{1,0:T(8,128)S(1)}, u32[]{:S(2)}, u32[]{:S(2)}) collective-permute-start(f32[72,128]{1,0:T(8,128)S(1)} %collective-permute-done.5), channel_id=1, source_target_pairs={{0,1},{1,0},{2,3},{3,2},{4,5},{5,4},{6,7},{7,6},{8,9},{9,8},{10,11... | collective-permute-start | bytes 110600 | tf_op jit(solution)/shard_map/ppermute | solution.py:565
  80.7 4.0 %collective-permute-start.7 = (f32[16,1152]{1,0:T(8,128)S(1)}, f32[16,1152]{1,0:T(8,128)S(1)}, u32[]{:S(2)}, u32[]{:S(2)}) collective-permute-start(f32[16,1152]{1,0:T(8,128)S(1)} %slice_select_fusion), channel_id=1, source_target_pairs={{1,32},{0,225},{33,64},{32,1},{65,96},{64,33},{97,128},{96,65},{12... | collective-permute-start | bytes 221192 | tf_op jit(solution)/shard_map/ppermute | solution.py:631

commit v8 on v7

--- a/solution.py
+++ b/solution.py
@@ -221,7 +221,12 @@
             high = jnp.max(jnp.minimum(held[3, RUN * i + RUN - 1], last_cell), axis=1, keepdims=True)
             low = quotient(low.astype(jnp.int32), tile_cols)
             high = quotient(high.astype(jnp.int32), tile_cols)
+            most = jnp.abs(held[0, RUN * i])
+            for p in range(1, RUN):
+                most = jnp.maximum(most, jnp.abs(held[0, RUN * i + p]))
+            some = (jnp.max(most, axis=1, keepdims=True) > 0.0).astype(jnp.int32)
             spans = jnp.where(lane == i, low, jnp.where(lane == 64 + i, high, spans))
+            spans = jnp.where(lane == 32 + i, some, spans)
         span_v[...] = spans
         copy = pltpu.make_async_copy(span_v, span_s, sem)
         copy.start()
@@ -231,7 +236,8 @@
             s = c // parts
             i = c % parts
             low = span_s[s, i]
-            high = span_s[s, 64 + i]
+            some = span_s[s, 32 + i]
+            high = jnp.where(some > 0, span_s[s, 64 + i], low)
 
             def note(t, row, rows):
                 at[t] = c
@@ -244,7 +250,7 @@
 
             row, t = lax.while_loop(lambda x: high - x[0] >= WINDOW - 1, further, (low // 8 * 8, t))
             note(t, row, WINDOW - 1)
-            return t + 1
+            return t + some
 
         count = lax.fori_loop(0, -(-slots // regs) * parts, plan, jnp.int32(0))
         for e in range(3):

time: 113 us -> 104 us (0.920)
  Pallas kernels: 33 us -> 24.5 us
    pallas_call x1, Pallas kernels: 22.1 us -> 13.7 us  [deposit(): pl.pallas_call(kernel, out_shape=pltpu.VMEM((row_pad, tile_cols + 128), F...]
  transfers between devices with their start and end apart: 9 -> 9, of which waited for: 7 -> 7; matrix products, arithmetic and copies ran while one was open for 0% -> 0% of each run, Pallas kernels for 20% -> 13%
where the time goes in v8:
time: 104 us
  starting transfers between devices  33.2 us (32%)
  Pallas kernels  24.5 us (24%)
  waiting for transfers between devices  23.6 us (23%)
  blocking collectives  19.4 us (19%)
  between operations  1.47 us (1%)
  local copies, waits for them, and re-layouts  1.18 us (1%)
    all_to_all x1, blocking collectives, body(): lax.all_to_all(sums.reshape(tiles * n_obs, 1, 128), LAT_LON_OBS, split_ax...  19.4 us
    all_to_all x1, starting transfers between devices, body(): lax.all_to_all(sent.reshape(tiles, CAP * WORDS, 1, 128), LAT_LON, split_a...  16.5 us
    ppermute x6, starting transfers between devices, around(): lax.ppermute(value, axis, [(i, (i + steps) % count) for i in range(count)])  16.4 us
    pallas_call x1, Pallas kernels, deposit(): pl.pallas_call(kernel, out_shape=pltpu.VMEM((row_pad, tile_cols + 128), F...  13.7 us
    ppermute x6, waiting for transfers between devices, around(): lax.ppermute(value, axis, [(i, (i + steps) % count) for i in range(count)])  8.78 us
    all_to_all x1, waiting for transfers between devices, body(): lax.all_to_all(sent.reshape(tiles, CAP * WORDS, 1, 128), LAT_LON, split_a...  8.44 us
    pallas_call x1, Pallas kernels, basis(): pl.pallas_call(basis_kernel, out_shape=(pltpu.VMEM(inertia.shape, F32), p...  5.95 us
    ppermute x1, waiting for transfers between devices, body(): other = lax.ppermute(outer, LAT_OBS, swap)  3.74 us
  transfers between devices with their start and end apart: 9, of which 7 were waited for; matrix products, arithmetic and copies ran while one was open for 0% of the time, Pallas kernels for 13%

profile of v8, /device:TPU:1, one launch (start us, length us, event | category | flops | bytes accessed | tf_op | source)
XLA Modules:
  0.0 103.9 jit_solution(10436063648189111869)
XLA Ops:
  1.3 2.8 %pack.1 = f32[1536,128]{1,0:T(8,128)} custom-call(s32[1,128]{1,0:T(1,128)} %owner.1, s32[1]{0:T(128)S(6)} %copy.13.count, f32[128,128]{1,0:T(8,128)} %innovation.1, f32[128,128]{1,0:T(8,128)} %error.1, f32[2,128,128]{2,1,0:T(8,128)} %offset.1, s32[128,128]{1,0:T(8,128)} %cell.1), custom_call_target="tpu_custom_call" | custom-call | tf_op jit(solution)/shard_map/pack/pallas_call | solution.py:74
  4.0 0.0 copy-start.1
  4.0 0.0 copy-start.2
  4.0 16.5 %all-to-all-start = ((f32[128,12,1,128]{3,2,1,0:T(1,128)}), f32[128,12,1,128]{3,2,1,0:T(1,128)S(1)}, u32[]{:S(2)}, u32[]{:S(2)}) async-start(f32[128,12,1,128]{3,2,1,0:T(1,128)} %bitcast.27), calls=%async_computation | async-start | bytes 1572864 | tf_op jit(solution)/shard_map/all_to_all | solution.py:591
  20.5 0.0 copy-done.1
  20.5 0.0 copy-done.2
  20.5 0.0 copy-start
  20.6 0.9 copy-done
  21.4 3.9 %collective-permute-start = (f32[2,32,128]{2,1,0:T(8,128)S(1)}, f32[2,32,128]{2,1,0:T(8,128)S(1)}, u32[]{:S(2)}, u32[]{:S(2)}) collective-permute-start(f32[2,32,128]{2,1,0:T(8,128)S(1)} %get-tuple-element.27), channel_id=1, source_target_pairs={{0,30},{2,0},{4,2},{6,4},{8,6},{10,8},{12,10},{14,12},{16,14},{18,... | collective-permute-start | bytes 98312 | tf_op jit(solution)/shard_map/ppermute | solution.py:571
  25.3 0.0 collective-permute-start.1
  25.3 1.0 collective-permute-done
  26.4 5.8 %collective-permute-done.1 = f32[2,32,128]{2,1,0:T(8,128)S(1)} collective-permute-done((f32[2,32,128]{2,1,0:T(8,128)S(1)}, f32[2,32,128]{2,1,0:T(8,128)S(1)}, u32[]{:S(2)}, u32[]{:S(2)}) %collective-permute-start.1) | collective-permute-done | bytes 32800 | tf_op jit(solution)/shard_map/ppermute | solution.py:571
  32.2 3.4 %collective-permute-start.2 = (f32[2,8,1152]{2,1,0:T(8,128)S(1)}, f32[2,8,1152]{2,1,0:T(8,128)S(1)}, u32[]{:S(2)}, u32[]{:S(2)}) collective-permute-start(f32[2,8,1152]{2,1,0:T(8,128)S(1)} %get-tuple-element.25), channel_id=1, source_target_pairs={{0,1},{1,32},{32,33},{33,64},{64,65},{65,96},{96,97},{97,128},{128... | collective-permute-start | bytes 221192 | tf_op jit(solution)/shard_map/ppermute | solution.py:571
  35.6 0.0 collective-permute-start.3
  35.6 8.4 %all-to-all-done = f32[128,12,1,128]{3,2,1,0:T(1,128)S(1)} async-done(((f32[128,12,1,128]{3,2,1,0:T(1,128)}), f32[128,12,1,128]{3,2,1,0:T(1,128)S(1)}, u32[]{:S(2)}, u32[]{:S(2)}) %all-to-all-start) | async-done | bytes 786464 | tf_op jit(solution)/shard_map/all_to_all | solution.py:591
  44.0 13.7 %deposit.1 = f32[72,1152]{1,0:T(8,128)S(1)} custom-call(f32[1536,128]{1,0:T(8,128)S(1)} %bitcast.24), custom_call_target="tpu_custom_call" | custom-call | tf_op jit(solution)/shard_map/deposit/pallas_call | solution.py:341
  57.7 0.0 collective-permute-done.2
  57.7 0.0 collective-permute-done.3
  57.7 4.3 %collective-permute-start.4 = (f32[72,1152]{1,0:T(8,128)S(1)}, f32[72,1152]{1,0:T(8,128)S(1)}, u32[]{:S(2)}, u32[]{:S(2)}) collective-permute-start(f32[72,1152]{1,0:T(8,128)S(1)} %deposit.1), channel_id=1, source_target_pairs={{0,1},{1,0},{2,3},{3,2},{4,5},{5,4},{6,7},{7,6},{8,9},{9,8},{10,11... | collective-permute-start | bytes 995336 | tf_op jit(solution)/shard_map/ppermute | solution.py:571
  62.0 1.3 %collective-permute-done.4 = f32[72,1152]{1,0:T(8,128)S(1)} collective-permute-done((f32[72,1152]{1,0:T(8,128)S(1)}, f32[72,1152]{1,0:T(8,128)S(1)}, u32[]{:S(2)}, u32[]{:S(2)}) %collective-permute-start.4) | collective-permute-done | bytes 331808 | tf_op jit(solution)/shard_map/ppermute | solution.py:571
  63.4 0.1 slice_reduce_fusion
  63.5 0.1 select_select_fusion
  63.6 0.1 collective-permute-start.5
  63.7 0.1 slice.79
  63.8 2.6 %collective-permute-done.5 = f32[72,128]{1,0:T(8,128)S(1)} collective-permute-done((f32[72,128]{1,0:T(8,128)S(1)}, f32[72,128]{1,0:T(8,128)S(1)}, u32[]{:S(2)}, u32[]{:S(2)}) %collective-permute-start.5) | collective-permute-done | bytes 36896 | tf_op jit(solution)/shard_map/ppermute | solution.py:620
  66.5 4.8 %collective-permute-start.6 = (f32[72,128]{1,0:T(8,128)S(1)}, f32[72,128]{1,0:T(8,128)S(1)}, u32[]{:S(2)}, u32[]{:S(2)}) collective-permute-start(f32[72,128]{1,0:T(8,128)S(1)} %collective-permute-done.5), channel_id=1, source_target_pairs={{0,1},{1,0},{2,3},{3,2},{4,5},{5,4},{6,7},{7,6},{8,9},{9,8},{10,11... | collective-permute-start | bytes 110600 | tf_op jit(solution)/shard_map/ppermute | solution.py:571
  71.3 0.1 fusion.1
  71.5 0.7 collective-permute-done.6
  72.3 0.3 collective-permute-start.7
  72.6 3.7 %collective-permute-done.7.other = f32[16,1152]{1,0:T(8,128)S(1)} collective-permute-done((f32[16,1152]{1,0:T(8,128)S(1)}, f32[16,1152]{1,0:T(8,128)S(1)}, u32[]{:S(2)}, u32[]{:S(2)}) %collective-permute-start.7) | collective-permute-done | bytes 73760 | tf_op jit(solution)/shard_map/ppermute | solution.py:637
  76.3 5.9 %basis.1 = (f32[48,1152]{1,0:T(8,128)S(1)}, f32[256,128]{1,0:T(8,128)S(1)}) custom-call(s32[1]{0:T(128)} %bitcast.side, f32[72,1152]{1,0:T(8,128)S(1)} %pad_maximum_fusion.1.tile, f32[16,1152]{1,0:T(8,128)S(1)} %collective-permute-done.7.other, f32[48,1152]{1,0:T(8,128)S(1)} %compare_convert_fusion.ocean, f32[48,1152]{1,0:T(8,128)S(1)} %get-tuple-element.21.inertia, ...), custom_call_target="tpu_custom_call" | custom-call | tf_op jit(solution)/shard_map/basis/pallas_call | solution.py:500
  82.3 19.4 %all_to_all.10 = f32[256,1,128]{2,1,0:T(1,128)S(1)} all-to-all(f32[256,1,128]{2,1,0:T(1,128)S(1)} %bitcast.26), channel_id=1, replica_groups=mesh['lat'=8,'lon_0'=4,'lon_1'=4,'obs'=2] {'lat','lon_0','lon_1','obs'}, dimensions={0} | all-to-all | bytes 262144 | tf_op jit(solution)/shard_map/all_to_all | solution.py:641
  101.7 2.2 %solve.1 = (f32[32,1024]{1,0:T(8,128)}, f32[32,1024]{1,0:T(8,128)}) custom-call(f32[256,128]{1,0:T(8,128)S(1)} %bitcast.25, f32[48,1152]{1,0:T(8,128)S(1)} %get-tuple-element.17.forcing, f32[48,1152]{1,0:T(8,128)S(1)} %get-tuple-element.21.inertia, f32[48,1152]{1,0:T(8,128)S(1)} %get-tuple-element.19.east, f32[48,1152]{1,0:T(8,128)S(1)} %get-tuple-element.18.south), custom_call_target="tpu_custom_call" | custom-call | tf_op jit(solution)/shard_map/solve/pallas_call | solution.py:559
  (17 shorter events, 0.3 us)
Async XLA Ops:
  4.0 16.5 %copy-start.1 = (f32[32,1024]{1,0:T(8,128)S(1)}, f32[32,1024]{1,0:T(8,128)}, u32[]{:S(2)}) copy-start(f32[32,1024]{1,0:T(8,128)} %param.17) | copy-start | bytes 393220
  4.0 16.5 %copy-start.2 = (s32[32,1024]{1,0:T(8,128)S(1)}, s32[32,1024]{1,0:T(8,128)}, u32[]{:S(2)}) copy-start(s32[32,1024]{1,0:T(8,128)} %param.15) | copy-start | bytes 393220
  4.0 40.0 %all-to-all-start = ((f32[128,12,1,128]{3,2,1,0:T(1,128)}), f32[128,12,1,128]{3,2,1,0:T(1,128)S(1)}, u32[]{:S(2)}, u32[]{:S(2)}) async-start(f32[128,12,1,128]{3,2,1,0:T(1,128)} %bitcast.27), calls=%async_computation | async-start | bytes 1572864 | tf_op jit(solution)/shard_map/all_to_all | solution.py:591
  20.5 0.9 copy-start
  21.4 4.9 %collective-permute-start = (f32[2,32,128]{2,1,0:T(8,128)S(1)}, f32[2,32,128]{2,1,0:T(8,128)S(1)}, u32[]{:S(2)}, u32[]{:S(2)}) collective-permute-start(f32[2,32,128]{2,1,0:T(8,128)S(1)} %get-tuple-element.27), channel_id=1, source_target_pairs={{0,30},{2,0},{4,2},{6,4},{8,6},{10,8},{12,10},{14,12},{16,14},{18,... | collective-permute-start | bytes 98312 | tf_op jit(solution)/shard_map/ppermute | solution.py:571
  25.3 6.8 %collective-permute-start.1 = (f32[2,32,128]{2,1,0:T(8,128)S(1)}, f32[2,32,128]{2,1,0:T(8,128)S(1)}, u32[]{:S(2)}, u32[]{:S(2)}) collective-permute-start(f32[2,32,128]{2,1,0:T(8,128)S(1)} %get-tuple-element.26), channel_id=1, source_target_pairs={{0,2},{2,4},{4,6},{6,8},{8,10},{10,12},{12,14},{14,16},{16,18},{18... | collective-permute-start | bytes 98312 | tf_op jit(solution)/shard_map/ppermute | solution.py:571
  32.2 25.5 %collective-permute-start.2 = (f32[2,8,1152]{2,1,0:T(8,128)S(1)}, f32[2,8,1152]{2,1,0:T(8,128)S(1)}, u32[]{:S(2)}, u32[]{:S(2)}) collective-permute-start(f32[2,8,1152]{2,1,0:T(8,128)S(1)} %get-tuple-element.25), channel_id=1, source_target_pairs={{0,1},{1,32},{32,33},{33,64},{64,65},{65,96},{96,97},{97,128},{128... | collective-permute-start | bytes 221192 | tf_op jit(solution)/shard_map/ppermute | solution.py:571
  35.6 22.1 %collective-permute-start.3 = (f32[2,8,1152]{2,1,0:T(8,128)S(1)}, f32[2,8,1152]{2,1,0:T(8,128)S(1)}, u32[]{:S(2)}, u32[]{:S(2)}) collective-permute-start(f32[2,8,1152]{2,1,0:T(8,128)S(1)} %get-tuple-element.24), channel_id=1, source_target_pairs={{0,225},{1,0},{32,1},{33,32},{64,33},{65,64},{96,65},{97,96},{128,... | collective-permute-start | bytes 221192 | tf_op jit(solution)/shard_map/ppermute | solution.py:571
  57.7 5.5 %collective-permute-start.4 = (f32[72,1152]{1,0:T(8,128)S(1)}, f32[72,1152]{1,0:T(8,128)S(1)}, u32[]{:S(2)}, u32[]{:S(2)}) collective-permute-start(f32[72,1152]{1,0:T(8,128)S(1)} %deposit.1), channel_id=1, source_target_pairs={{0,1},{1,0},{2,3},{3,2},{4,5},{5,4},{6,7},{7,6},{8,9},{9,8},{10,11... | collective-permute-start | bytes 995336 | tf_op jit(solution)/shard_map/ppermute | solution.py:571
  63.6 2.9 %collective-permute-start.5 = (f32[72,128]{1,0:T(8,128)S(1)}, f32[72,128]{1,0:T(8,128)S(1)}, u32[]{:S(2)}, u32[]{:S(2)}) collective-permute-start(f32[72,128]{1,0:T(8,128)S(1)} %select_select_fusion), channel_id=1, source_target_pairs={{0,2},{1,31},{2,4},{3,1},{4,6},{5,3},{6,8},{7,5},{8,10},{9,7},{10,... | collective-permute-start | bytes 110600 | tf_op jit(solution)/shard_map/ppermute | solution.py:620
  66.5 5.7 %collective-permute-start.6 = (f32[72,128]{1,0:T(8,128)S(1)}, f32[72,128]{1,0:T(8,128)S(1)}, u32[]{:S(2)}, u32[]{:S(2)}) collective-permute-start(f32[72,128]{1,0:T(8,128)S(1)} %collective-permute-done.5), channel_id=1, source_target_pairs={{0,1},{1,0},{2,3},{3,2},{4,5},{5,4},{6,7},{7,6},{8,9},{9,8},{10,11... | collective-permute-start | bytes 110600 | tf_op jit(solution)/shard_map/ppermute | solution.py:571
  72.3 4.0 %collective-permute-start.7 = (f32[16,1152]{1,0:T(8,128)S(1)}, f32[16,1152]{1,0:T(8,128)S(1)}, u32[]{:S(2)}, u32[]{:S(2)}) collective-permute-start(f32[16,1152]{1,0:T(8,128)S(1)} %slice_select_fusion), channel_id=1, source_target_pairs={{1,32},{0,225},{33,64},{32,1},{65,96},{64,33},{97,128},{96,65},{12... | collective-permute-start | bytes 221192 | tf_op jit(solution)/shard_map/ppermute | solution.py:637

commit v9 on v8

--- a/solution.py
+++ b/solution.py
@@ -610,17 +610,8 @@
     south = jnp.sqrt(conduct * jnp.roll(conduct, -1, 0))
     spill = tile[:, cols:]
     side = lax.axis_index("obs").astype(jnp.int32)
-    leaving = jnp.where(
-        side == 0, jnp.where(lane == 0, spill[:, :1], tile[:, cols - 128 : cols]), tile[:, :128]
-    )
-    split = []
-    for i in range(n_lon):
-        split.append((2 * i, 2 * ((i + 1) % n_lon)))
-        split.append((2 * i + 1, 2 * ((i - 1) % n_lon) + 1))
-    came = lax.ppermute(leaving, LON + ("obs",), split)
-    swapped = around(came, "obs", 1)
-    from_west = jnp.where(side == 0, came, swapped)
-    from_east = jnp.where(side == 0, swapped, came)
+    from_west = around(jnp.where(lane == 0, spill[:, :1], tile[:, cols - 128 : cols]), LON, 1)
+    from_east = around(tile[:, :128], LON, -1)
     tile = jnp.concatenate(
         [
             tile[:, :128] + jnp.where(lane == 0, from_west, 0.0),

time: 104 us -> 105 us (level)
  waiting for transfers between devices: 23.6 us -> 20.1 us
  blocking collectives: 19.4 us -> 22.8 us
  starting transfers between devices: 33.2 us -> 34.5 us
    all_to_all x1, blocking collectives: 19.4 us -> 22.8 us  [body(): lax.all_to_all(sums.reshape(tiles * n_obs, 1, 128), LAT_LON_OBS, split_ax...]
    ppermute x1 -> x0, waiting for transfers between devices: 2.65 us -> none  [body(): came = lax.ppermute(leaving, LON + ('obs',), split)]
    ppermute x1, starting transfers between devices: 0.27 us -> 1.65 us  [body(): other = lax.ppermute(outer, LAT_OBS, swap)]
    ppermute x1, waiting for transfers between devices: 3.74 us -> 2.37 us  [body(): other = lax.ppermute(outer, LAT_OBS, swap)]
    ppermute x6 -> x7, waiting for transfers between devices: 8.78 us -> 9.26 us  [around(): lax.ppermute(value, axis, [(i, (i + steps) % count) for i in range(count)])]
    ppermute x6 -> x7, starting transfers between devices: 16.4 us -> 16.4 us  [around(): lax.ppermute(value, axis, [(i, (i + steps) % count) for i in range(count)])]
  transfers between devices with their start and end apart: 9 -> 9, of which waited for: 7 -> 6; matrix products, arithmetic and copies ran while one was open for 0% -> 0% of each run, Pallas kernels for 13% -> 13%
where the time goes in v9:
time: 105 us
  starting transfers between devices  34.5 us (33%)
  Pallas kernels  24.5 us (23%)
  blocking collectives  22.8 us (22%)
  waiting for transfers between devices  20.1 us (19%)
  between operations  1.44 us (1%)
  local copies, waits for them, and re-layouts  1.18 us (1%)
    all_to_all x1, blocking collectives, body(): lax.all_to_all(sums.reshape(tiles * n_obs, 1, 128), LAT_LON_OBS, split_ax...  22.8 us
    all_to_all x1, starting transfers between devices, body(): lax.all_to_all(sent.reshape(tiles, CAP * WORDS, 1, 128), LAT_LON, split_a...  16.5 us
    ppermute x7, starting transfers between devices, around(): lax.ppermute(value, axis, [(i, (i + steps) % count) for i in range(count)])  16.4 us
    pallas_call x1, Pallas kernels, deposit(): pl.pallas_call(kernel, out_shape=pltpu.VMEM((row_pad, tile_cols + 128), F...  13.7 us
    ppermute x7, waiting for transfers between devices, around(): lax.ppermute(value, axis, [(i, (i + steps) % count) for i in range(count)])  9.26 us
    all_to_all x1, waiting for transfers between devices, body(): lax.all_to_all(sent.reshape(tiles, CAP * WORDS, 1, 128), LAT_LON, split_a...  8.44 us
    pallas_call x1, Pallas kernels, basis(): pl.pallas_call(basis_kernel, out_shape=(pltpu.VMEM(inertia.shape, F32), p...  5.95 us
    pallas_call x1, Pallas kernels, pack(): pl.pallas_call(pack_kernel, out_shape=jax.ShapeDtypeStruct((tiles * CAP *...  2.75 us
  transfers between devices with their start and end apart: 9, of which 6 were waited for; matrix products, arithmetic and copies ran while one was open for 0% of the time, Pallas kernels for 13%

profile of v9, /device:TPU:1, one launch (start us, length us, event | category | flops | bytes accessed | tf_op | source)
XLA Modules:
  0.0 104.9 jit_solution(14623528318641646890)
XLA Ops:
  1.3 2.8 %pack.1 = f32[1536,128]{1,0:T(8,128)} custom-call(s32[1,128]{1,0:T(1,128)} %owner.1, s32[1]{0:T(128)S(6)} %copy.13.count, f32[128,128]{1,0:T(8,128)} %innovation.1, f32[128,128]{1,0:T(8,128)} %error.1, f32[2,128,128]{2,1,0:T(8,128)} %offset.1, s32[128,128]{1,0:T(8,128)} %cell.1), custom_call_target="tpu_custom_call" | custom-call | tf_op jit(solution)/shard_map/pack/pallas_call | solution.py:74
  4.0 0.0 copy-start.1
  4.0 0.0 copy-start.2
  4.0 16.5 %all-to-all-start = ((f32[128,12,1,128]{3,2,1,0:T(1,128)}), f32[128,12,1,128]{3,2,1,0:T(1,128)S(1)}, u32[]{:S(2)}, u32[]{:S(2)}) async-start(f32[128,12,1,128]{3,2,1,0:T(1,128)} %bitcast.27), calls=%async_computation | async-start | bytes 1572864 | tf_op jit(solution)/shard_map/all_to_all | solution.py:591
  20.5 0.0 copy-done.1
  20.5 0.0 copy-done.2
  20.5 0.0 copy-start
  20.6 0.9 copy-done
  21.4 3.9 %collective-permute-start = (f32[2,32,128]{2,1,0:T(8,128)S(1)}, f32[2,32,128]{2,1,0:T(8,128)S(1)}, u32[]{:S(2)}, u32[]{:S(2)}) collective-permute-start(f32[2,32,128]{2,1,0:T(8,128)S(1)} %get-tuple-element.29), channel_id=1, source_target_pairs={{0,30},{2,0},{4,2},{6,4},{8,6},{10,8},{12,10},{14,12},{16,14},{18,... | collective-permute-start | bytes 98312 | tf_op jit(solution)/shard_map/ppermute | solution.py:571
  25.3 0.0 collective-permute-start.1
  25.3 1.0 collective-permute-done
  26.4 5.8 %collective-permute-done.1 = f32[2,32,128]{2,1,0:T(8,128)S(1)} collective-permute-done((f32[2,32,128]{2,1,0:T(8,128)S(1)}, f32[2,32,128]{2,1,0:T(8,128)S(1)}, u32[]{:S(2)}, u32[]{:S(2)}) %collective-permute-start.1) | collective-permute-done | bytes 32800 | tf_op jit(solution)/shard_map/ppermute | solution.py:571
  32.2 3.4 %collective-permute-start.2 = (f32[2,8,1152]{2,1,0:T(8,128)S(1)}, f32[2,8,1152]{2,1,0:T(8,128)S(1)}, u32[]{:S(2)}, u32[]{:S(2)}) collective-permute-start(f32[2,8,1152]{2,1,0:T(8,128)S(1)} %get-tuple-element.27), channel_id=1, source_target_pairs={{0,1},{1,32},{32,33},{33,64},{64,65},{65,96},{96,97},{97,128},{128... | collective-permute-start | bytes 221192 | tf_op jit(solution)/shard_map/ppermute | solution.py:571
  35.6 0.0 collective-permute-start.3
  35.6 8.4 %all-to-all-done = f32[128,12,1,128]{3,2,1,0:T(1,128)S(1)} async-done(((f32[128,12,1,128]{3,2,1,0:T(1,128)}), f32[128,12,1,128]{3,2,1,0:T(1,128)S(1)}, u32[]{:S(2)}, u32[]{:S(2)}) %all-to-all-start) | async-done | bytes 786464 | tf_op jit(solution)/shard_map/all_to_all | solution.py:591
  44.0 13.7 %deposit.1 = f32[72,1152]{1,0:T(8,128)S(1)} custom-call(f32[1536,128]{1,0:T(8,128)S(1)} %bitcast.24), custom_call_target="tpu_custom_call" | custom-call | tf_op jit(solution)/shard_map/deposit/pallas_call | solution.py:341
  57.7 0.0 collective-permute-done.2
  57.7 0.0 collective-permute-done.3
  57.7 4.3 %collective-permute-start.4 = (f32[72,1152]{1,0:T(8,128)S(1)}, f32[72,1152]{1,0:T(8,128)S(1)}, u32[]{:S(2)}, u32[]{:S(2)}) collective-permute-start(f32[72,1152]{1,0:T(8,128)S(1)} %deposit.1), channel_id=1, source_target_pairs={{0,1},{1,0},{2,3},{3,2},{4,5},{5,4},{6,7},{7,6},{8,9},{9,8},{10,11... | collective-permute-start | bytes 995336 | tf_op jit(solution)/shard_map/ppermute | solution.py:571
  62.0 1.3 %collective-permute-done.4 = f32[72,1152]{1,0:T(8,128)S(1)} collective-permute-done((f32[72,1152]{1,0:T(8,128)S(1)}, f32[72,1152]{1,0:T(8,128)S(1)}, u32[]{:S(2)}, u32[]{:S(2)}) %collective-permute-start.4) | collective-permute-done | bytes 331808 | tf_op jit(solution)/shard_map/ppermute | solution.py:571
  63.4 0.1 slice.79
  63.6 0.1 slice_reduce_fusion
  63.7 0.1 slice_select_fusion.1
  63.7 0.4 collective-permute-start.5
  64.1 4.4 %collective-permute-start.6 = (f32[72,128]{1,0:T(8,128)S(1)}, f32[72,128]{1,0:T(8,128)S(1)}, u32[]{:S(2)}, u32[]{:S(2)}) collective-permute-start(f32[72,128]{1,0:T(8,128)S(1)} %get-tuple-element.25), channel_id=1, source_target_pairs={{0,30},{2,0},{4,2},{6,4},{8,6},{10,8},{12,10},{14,12},{16,14},{18,... | collective-permute-start | bytes 110600 | tf_op jit(solution)/shard_map/ppermute | solution.py:571
  68.6 0.1 fusion.1
  68.7 1.2 %collective-permute-done.5 = f32[72,128]{1,0:T(8,128)S(1)} collective-permute-done((f32[72,128]{1,0:T(8,128)S(1)}, f32[72,128]{1,0:T(8,128)S(1)}, u32[]{:S(2)}, u32[]{:S(2)}) %collective-permute-start.5) | collective-permute-done | bytes 36896 | tf_op jit(solution)/shard_map/ppermute | solution.py:571
  69.9 0.0 collective-permute-done.6
  70.0 1.7 %collective-permute-start.7 = (f32[16,1152]{1,0:T(8,128)S(1)}, f32[16,1152]{1,0:T(8,128)S(1)}, u32[]{:S(2)}, u32[]{:S(2)}) collective-permute-start(f32[16,1152]{1,0:T(8,128)S(1)} %slice_select_fusion), channel_id=1, source_target_pairs={{1,32},{0,225},{33,64},{32,1},{65,96},{64,33},{97,128},{96,65},{12... | collective-permute-start | bytes 221192 | tf_op jit(solution)/shard_map/ppermute | solution.py:628
  71.7 2.4 %collective-permute-done.7.other = f32[16,1152]{1,0:T(8,128)S(1)} collective-permute-done((f32[16,1152]{1,0:T(8,128)S(1)}, f32[16,1152]{1,0:T(8,128)S(1)}, u32[]{:S(2)}, u32[]{:S(2)}) %collective-permute-start.7) | collective-permute-done | bytes 73760 | tf_op jit(solution)/shard_map/ppermute | solution.py:628
  74.0 5.9 %basis.1 = (f32[48,1152]{1,0:T(8,128)S(1)}, f32[256,128]{1,0:T(8,128)S(1)}) custom-call(s32[1]{0:T(128)} %bitcast.side, f32[72,1152]{1,0:T(8,128)S(1)} %pad_maximum_fusion.1.tile, f32[16,1152]{1,0:T(8,128)S(1)} %collective-permute-done.7.other, f32[48,1152]{1,0:T(8,128)S(1)} %compare_convert_fusion.ocean, f32[48,1152]{1,0:T(8,128)S(1)} %get-tuple-element.21.inertia, ...), custom_call_target="tpu_custom_call" | custom-call | tf_op jit(solution)/shard_map/basis/pallas_call | solution.py:500
  80.0 22.8 %all_to_all.10 = f32[256,1,128]{2,1,0:T(1,128)S(1)} all-to-all(f32[256,1,128]{2,1,0:T(1,128)S(1)} %bitcast.26), channel_id=1, replica_groups=mesh['lat'=8,'lon_0'=4,'lon_1'=4,'obs'=2] {'lat','lon_0','lon_1','obs'}, dimensions={0} | all-to-all | bytes 262144 | tf_op jit(solution)/shard_map/all_to_all | solution.py:632
  102.7 2.2 %solve.1 = (f32[32,1024]{1,0:T(8,128)}, f32[32,1024]{1,0:T(8,128)}) custom-call(f32[256,128]{1,0:T(8,128)S(1)} %bitcast.25, f32[48,1152]{1,0:T(8,128)S(1)} %get-tuple-element.17.forcing, f32[48,1152]{1,0:T(8,128)S(1)} %get-tuple-element.21.inertia, f32[48,1152]{1,0:T(8,128)S(1)} %get-tuple-element.19.east, f32[48,1152]{1,0:T(8,128)S(1)} %get-tuple-element.18.south), custom_call_target="tpu_custom_call" | custom-call | tf_op jit(solution)/shard_map/solve/pallas_call | solution.py:559
  (17 shorter events, 0.3 us)
Async XLA Ops:
  4.0 16.5 %copy-start.1 = (f32[32,1024]{1,0:T(8,128)S(1)}, f32[32,1024]{1,0:T(8,128)}, u32[]{:S(2)}) copy-start(f32[32,1024]{1,0:T(8,128)} %param.17) | copy-start | bytes 393220
  4.0 16.5 %copy-start.2 = (s32[32,1024]{1,0:T(8,128)S(1)}, s32[32,1024]{1,0:T(8,128)}, u32[]{:S(2)}) copy-start(s32[32,1024]{1,0:T(8,128)} %param.15) | copy-start | bytes 393220
  4.0 40.0 %all-to-all-start = ((f32[128,12,1,128]{3,2,1,0:T(1,128)}), f32[128,12,1,128]{3,2,1,0:T(1,128)S(1)}, u32[]{:S(2)}, u32[]{:S(2)}) async-start(f32[128,12,1,128]{3,2,1,0:T(1,128)} %bitcast.27), calls=%async_computation | async-start | bytes 1572864 | tf_op jit(solution)/shard_map/all_to_all | solution.py:591
  20.5 0.9 copy-start
  21.4 4.9 %collective-permute-start = (f32[2,32,128]{2,1,0:T(8,128)S(1)}, f32[2,32,128]{2,1,0:T(8,128)S(1)}, u32[]{:S(2)}, u32[]{:S(2)}) collective-permute-start(f32[2,32,128]{2,1,0:T(8,128)S(1)} %get-tuple-element.29), channel_id=1, source_target_pairs={{0,30},{2,0},{4,2},{6,4},{8,6},{10,8},{12,10},{14,12},{16,14},{18,... | collective-permute-start | bytes 98312 | tf_op jit(solution)/shard_map/ppermute | solution.py:571
  25.3 6.8 %collective-permute-start.1 = (f32[2,32,128]{2,1,0:T(8,128)S(1)}, f32[2,32,128]{2,1,0:T(8,128)S(1)}, u32[]{:S(2)}, u32[]{:S(2)}) collective-permute-start(f32[2,32,128]{2,1,0:T(8,128)S(1)} %get-tuple-element.28), channel_id=1, source_target_pairs={{0,2},{2,4},{4,6},{6,8},{8,10},{10,12},{12,14},{14,16},{16,18},{18... | collective-permute-start | bytes 98312 | tf_op jit(solution)/shard_map/ppermute | solution.py:571
  32.2 25.5 %collective-permute-start.2 = (f32[2,8,1152]{2,1,0:T(8,128)S(1)}, f32[2,8,1152]{2,1,0:T(8,128)S(1)}, u32[]{:S(2)}, u32[]{:S(2)}) collective-permute-start(f32[2,8,1152]{2,1,0:T(8,128)S(1)} %get-tuple-element.27), channel_id=1, source_target_pairs={{0,1},{1,32},{32,33},{33,64},{64,65},{65,96},{96,97},{97,128},{128... | collective-permute-start | bytes 221192 | tf_op jit(solution)/shard_map/ppermute | solution.py:571
  35.6 22.1 %collective-permute-start.3 = (f32[2,8,1152]{2,1,0:T(8,128)S(1)}, f32[2,8,1152]{2,1,0:T(8,128)S(1)}, u32[]{:S(2)}, u32[]{:S(2)}) collective-permute-start(f32[2,8,1152]{2,1,0:T(8,128)S(1)} %get-tuple-element.26), channel_id=1, source_target_pairs={{0,225},{1,0},{32,1},{33,32},{64,33},{65,64},{96,65},{97,96},{128,... | collective-permute-start | bytes 221192 | tf_op jit(solution)/shard_map/ppermute | solution.py:571
  57.7 5.6 %collective-permute-start.4 = (f32[72,1152]{1,0:T(8,128)S(1)}, f32[72,1152]{1,0:T(8,128)S(1)}, u32[]{:S(2)}, u32[]{:S(2)}) collective-permute-start(f32[72,1152]{1,0:T(8,128)S(1)} %deposit.1), channel_id=1, source_target_pairs={{0,1},{1,0},{2,3},{3,2},{4,5},{5,4},{6,7},{7,6},{8,9},{9,8},{10,11... | collective-permute-start | bytes 995336 | tf_op jit(solution)/shard_map/ppermute | solution.py:571
  63.7 6.2 %collective-permute-start.5 = (f32[72,128]{1,0:T(8,128)S(1)}, f32[72,128]{1,0:T(8,128)S(1)}, u32[]{:S(2)}, u32[]{:S(2)}) collective-permute-start(f32[72,128]{1,0:T(8,128)S(1)} %get-tuple-element.24), channel_id=1, source_target_pairs={{0,2},{2,4},{4,6},{6,8},{8,10},{10,12},{12,14},{14,16},{16,18},{18... | collective-permute-start | bytes 110600 | tf_op jit(solution)/shard_map/ppermute | solution.py:571
  64.1 5.8 %collective-permute-start.6 = (f32[72,128]{1,0:T(8,128)S(1)}, f32[72,128]{1,0:T(8,128)S(1)}, u32[]{:S(2)}, u32[]{:S(2)}) collective-permute-start(f32[72,128]{1,0:T(8,128)S(1)} %get-tuple-element.25), channel_id=1, source_target_pairs={{0,30},{2,0},{4,2},{6,4},{8,6},{10,8},{12,10},{14,12},{16,14},{18,... | collective-permute-start | bytes 110600 | tf_op jit(solution)/shard_map/ppermute | solution.py:571
  70.0 4.0 %collective-permute-start.7 = (f32[16,1152]{1,0:T(8,128)S(1)}, f32[16,1152]{1,0:T(8,128)S(1)}, u32[]{:S(2)}, u32[]{:S(2)}) collective-permute-start(f32[16,1152]{1,0:T(8,128)S(1)} %slice_select_fusion), channel_id=1, source_target_pairs={{1,32},{0,225},{33,64},{32,1},{65,96},{64,33},{97,128},{96,65},{12... | collective-permute-start | bytes 221192 | tf_op jit(solution)/shard_map/ppermute | solution.py:628
